TPU v7x, 32 devices: a whole 2x2x4 slice. The times are simulated.
32 devices in a mesh: wave: 8 (over z, y), lev: 4 (over x, core).
Axes of the slice: x: 2, y: 2, z: 4, core: 2. Of those that a mesh axis runs over, the one named last changes fastest.
Arguments:
- spectra: bfloat16 [104, 4, 16, 1280], P('wave', None, 'lev'), may hold values from -0.625 to 0.625
- legendre: bfloat16 [104, 16, 1280], P('wave'), may hold values from -0.15625 to 0.15625
- derivative: bfloat16 [104, 16, 1280], P('wave'), may hold values from -0.15625 to 0.15625
- tracer: float32 [16, 16, 2560], P('lev', 'wave'), may hold values from -6 to 6
- limiter_flags: int32 [16, 16, 2560], P('lev', 'wave'), may hold values 0 or 1
- lat_weight: float32 [16], P('wave'), may hold values from 1 to 10
- slot_wave: int32 [104], replicated, may hold values from 0 to 103, each once
Outputs:
- tendency_spectra: float32 [104, 2, 16, 1280], P('wave', None, 'lev')
Inputs may be any that keep to these rules, and one draw needn't show every extreme that they name: `slot_wave`: every wavenumber 0 to 103 stands in exactly one slot.
All inputs are finite; a program needn't handle non-finite values. No bound on the sum of `limiter_flags` on one device may be relied on, other than what follows from the above.
Results may differ from a plain program's by a relative error of at most 0.0003.
The roundings to bfloat16 on the way count: a program that leaves them out, or rounds other values in their place, can miss the bound.
Values may be sent and summed in bfloat16 or wider, within the bound.
No kernel may reach another device: no remote copies, remote signals or barrier semaphores. Data moves between devices by JAX's collectives and lax.ppermute only.
A program may use at most 128 MiB of HBM per device.

v0:
```python
import math

import jax
import jax.numpy as jnp
from jax import lax
from jax.sharding import PartitionSpec as P

diffusivity = 0.15
courant_limit = 0.45


def extended(block, sides, width):
    for axis, dim in sides:
        count = lax.axis_size(axis)
        forward = [(i, i + 1) for i in range(count - 1)]
        backward = [(target, source) for source, target in forward]
        low = lax.ppermute(
            lax.slice_in_dim(block, block.shape[dim] - width, None, axis=dim), axis, forward
        )
        high = lax.ppermute(lax.slice_in_dim(block, 0, width, axis=dim), axis, backward)
        block = jnp.concatenate([low, block, high], axis=dim)
    return block


def wave_tables(slot_wave, lon_count):
    longitude = jnp.arange(lon_count, dtype=jnp.int32)
    phase_index = slot_wave[:, None] * longitude[None, :] % lon_count
    angles = 2.0 * math.pi / lon_count * phase_index.astype(jnp.float32)
    cosine = jnp.cos(angles)
    sine_part = jnp.sin(angles)
    doubled = jnp.where(slot_wave == 0, 1.0, 2.0).astype(jnp.float32)[:, None]
    synthesis_table = jnp.stack([doubled * cosine, -doubled * sine_part]).astype(jnp.bfloat16)
    analysis_table = jnp.stack([cosine, -sine_part]).astype(jnp.bfloat16)
    return (synthesis_table, analysis_table)


def combine_winds(legendre_sum, slope_sum, scaled_wave):
    zonal_real = -scaled_wave * legendre_sum[:, 3] - slope_sum[:, 0]
    zonal_imag = scaled_wave * legendre_sum[:, 2] - slope_sum[:, 1]
    merid_real = -scaled_wave * legendre_sum[:, 1] + slope_sum[:, 2]
    merid_imag = scaled_wave * legendre_sum[:, 0] + slope_sum[:, 3]
    return jnp.stack([zonal_real, zonal_imag, merid_real, merid_imag], axis=1).astype(jnp.bfloat16)


def face_terms(zonal_courant, limiter_flags):
    face_speed = 0.5 * (jnp.roll(zonal_courant, 1, axis=2) + zonal_courant)
    magnitude = jnp.abs(face_speed)
    switched = limiter_flags.astype(jnp.float32)
    diffuse = 0.5 * (magnitude - switched * (magnitude - face_speed * face_speed))
    return (face_speed, diffuse)


def tendency_of(
    padded, face_speed, diffuse, meridional, row_start, level_start, rows_total, levels_total
):
    centre = padded[1:-1, 1:-1]
    western = jnp.roll(centre, 1, axis=2)
    flux_east = face_speed * 0.5 * (western + centre) - diffuse * (centre - western)
    southern = padded[1:-1, :-1]
    northern = padded[1:-1, 1:]
    lat_speed = 0.5 * (meridional[1:-1, :-1] + meridional[1:-1, 1:])
    flux_north = lat_speed * 0.5 * (southern + northern) - 0.5 * jnp.abs(lat_speed) * (
        northern - southern
    )
    face_index = row_start + jnp.arange(flux_north.shape[1], dtype=jnp.int32)
    open_rows = ((face_index > 0) & (face_index < rows_total)).astype(jnp.float32)
    flux_north = flux_north * open_rows[None, :, None]
    level_index = level_start + jnp.arange(padded.shape[0] - 1, dtype=jnp.int32)
    open_levels = ((level_index > 0) & (level_index < levels_total)).astype(jnp.float32)
    flux_up = diffusivity * (padded[1:, 1:-1] - padded[:-1, 1:-1]) * open_levels[:, None, None]
    return (
        -(jnp.roll(flux_east, -1, axis=2) - flux_east)
        - (flux_north[:, 1:] - flux_north[:, :-1])
        + (flux_up[1:] - flux_up[:-1])
    )


def on_device(spectra, legendre, derivative, tracer, limiter_flags, lat_weight, slot_wave):
    slot_count = spectra.shape[0]
    level_count = spectra.shape[2]
    degree_count = spectra.shape[3]
    lat_total = legendre.shape[1]
    band_rows = tracer.shape[1]
    lon_count = tracer.shape[2]
    lev_total = level_count * lax.axis_size("lev")
    band_index = lax.axis_index("wave")
    row_start = band_index * band_rows
    level_start = lax.axis_index("lev") * level_count
    local_wave = lax.dynamic_slice_in_dim(slot_wave, band_index * slot_count, slot_count)
    degree = jnp.arange(degree_count, dtype=jnp.int32)
    live_mask = degree[None, :] >= local_wave[:, None]
    coefficients = (spectra * live_mask[:, None, None, :].astype(spectra.dtype)).reshape(
        slot_count, 4 * level_count, degree_count
    )
    legendre_sum = jnp.einsum(
        "mcn,mln->mcl", coefficients, legendre, preferred_element_type=jnp.float32
    ).reshape(slot_count, 4, level_count, lat_total)
    slope_sum = jnp.einsum(
        "mcn,mln->mcl", coefficients, derivative, preferred_element_type=jnp.float32
    ).reshape(slot_count, 4, level_count, lat_total)
    scaled_wave = (local_wave.astype(jnp.float32) / degree_count)[:, None, None]
    fourier = combine_winds(legendre_sum, slope_sum, scaled_wave)
    synthesis_table, analysis_table = wave_tables(slot_wave, lon_count)
    flipped = lax.all_to_all(fourier, "wave", split_axis=3, concat_axis=0, tiled=True).transpose(
        1, 0, 2, 3
    )
    eastward = jnp.einsum(
        "rmkj,rmi->kji", flipped[0:2], synthesis_table, preferred_element_type=jnp.float32
    )
    northward = jnp.einsum(
        "rmkj,rmi->kji", flipped[2:4], synthesis_table, preferred_element_type=jnp.float32
    )
    winds = jnp.stack([eastward, northward], axis=1)
    zonal_courant = courant_limit * jnp.tanh(winds[:, 0])
    merid_courant = courant_limit * jnp.tanh(winds[:, 1])
    face_speed, diffuse = face_terms(zonal_courant, limiter_flags)
    rimmed, rimmed_merid = (
        extended(tracer, (("wave", 1), ("lev", 0)), 1),
        extended(merid_courant, (("wave", 1), ("lev", 0)), 1),
    )
    section_one = tracer + tendency_of(
        rimmed, face_speed, diffuse, rimmed_merid, row_start, level_start, lat_total, lev_total
    )
    rimmed_section = extended(section_one, (("wave", 1), ("lev", 0)), 1)
    section_two = tendency_of(
        rimmed_section,
        face_speed,
        diffuse,
        rimmed_merid,
        row_start,
        level_start,
        lat_total,
        lev_total,
    )
    updated = 0.5 * tracer + 0.5 * (section_one + section_two)
    change = updated - tracer
    lat_scale = lat_weight * (1.0 / math.sqrt(lon_count))
    projected = jnp.einsum(
        "kji,rmi->mrkj", change, analysis_table.astype(jnp.float32), precision=lax.Precision.HIGHEST
    )
    outgoing = projected * lat_scale[None, None, None, :]
    live_float = live_mask.astype(jnp.float32)
    legendre_wide = legendre.astype(jnp.float32)
    summed = jnp.einsum(
        "mrkj,mjn->mrkn",
        lax.all_to_all(outgoing, "wave", split_axis=0, concat_axis=3, tiled=True),
        legendre_wide,
        precision=lax.Precision.HIGHEST,
    )
    return summed * live_float[:, None, None, :]


def solution(mesh):
    return jax.shard_map(
        on_device,
        mesh=mesh,
        in_specs=(
            P("wave", None, "lev", None),
            P("wave", None, None),
            P("wave", None, None),
            P("lev", "wave", None),
            P("lev", "wave", None),
            P("wave"),
            P(),
        ),
        out_specs=P("wave", None, "lev", None),
        check_vma=False,
    )
```

profile of v0, /device:TPU:2, one launch (start us, length us, event | category | flops | bytes accessed | tf_op | source)
XLA Modules:
  0.0 72.1 jit_solution(9594675138765185971)
XLA Ops:
  0.0 0.8 %fusion.52 = (f32[13]{0:T(128)S(1)}, s32[13]{0:T(128)S(1)}) fusion(s32[104]{0:T(128)} %param.13, s32[]{:T(128)S(6)} %select_n.34), kind=kLoop, calls=%fused_computation.108 | loop fusion | flops 39 | bytes 160 | tf_op jit(solution)/shard_map/neg | solution.py:38
  0.9 1.3 %broadcast_multiply_fusion = bf16[13,4,4,1280]{3,2,1,0:T(4,128)(2,1)S(1)} fusion(bf16[13,4,4,1280]{3,2,1,0:T(4,128)(2,1)} %param.7, bf16[13,1280]{1,0:T(8,128)(2,1)S(1)} %get-tuple-element.34), kind=kLoop, calls=%fused_computation.27 | loop fusion | flops 266240 | bytes 1098240 | tf_op jit(solution)/shard_map/mul | solution.py:92
  2.3 0.3 fusion.62
  2.8 0.6 copy-done.2
  3.4 0.3 fusion.63
  4.6 0.7 %reshape.235 = bf16[8,2,208]{2,1,0:T(2,128)(2,1)} reshape(bf16[16,4,4,13]{3,2,1,0:T(4,128)(2,1)S(1)} %fusion.61) | data formatting | bytes 13312
  5.3 5.8 %all-to-all-start = ((bf16[8,2,208]{2,1,0:T(2,128)(2,1)}), bf16[8,2,208]{2,1,0:T(2,128)(2,1)S(1)}, u32[]{:S(2)}, u32[]{:S(2)}) async-start(bf16[8,2,208]{2,1,0:T(2,128)(2,1)} %reshape.235), calls=%async_computation | async-start | bytes 16384 | tf_op jit(solution)/shard_map/all_to_all | solution.py:104
  11.3 3.9 %collective-permute-start.2 = (f32[4,1,2560]{2,0,1:T(4,128)S(1)}, f32[4,1,2560]{2,0,1:T(4,128)S(1)}, u32[]{:S(2)}, u32[]{:S(2)}) collective-permute-start(f32[4,1,2560]{2,0,1:T(4,128)S(1)} %copy.105), channel_id=1, source_target_pairs={{0,4},{4,8},{8,12},{12,16},{16,20},{20,24},{24,28},{1,5},{5,9},{9,... | collective-permute-start | bytes 122888 | tf_op jit(solution)/shard_map/ppermute | solution.py:17
  15.2 1.3 %collective-permute-start.3 = (f32[4,1,2560]{2,0,1:T(4,128)S(1)}, f32[4,1,2560]{2,0,1:T(4,128)S(1)}, u32[]{:S(2)}, u32[]{:S(2)}) collective-permute-start(f32[4,1,2560]{2,0,1:T(4,128)S(1)} %copy.106), channel_id=1, source_target_pairs={{4,0},{8,4},{12,8},{16,12},{20,16},{24,20},{28,24},{5,1},{9,5},{13... | collective-permute-start | bytes 122888 | tf_op jit(solution)/shard_map/ppermute | solution.py:20
  16.6 4.6 %multiply_convert_fusion.1 = (bf16[1,104,2560]{2,1,0:T(8,128)(2,1)S(1)}, bf16[1,104,2560]{2,1,0:T(8,128)(2,1)S(1)}, bf16[1,104,2560]{2,1,0:T(8,128)(2,1)S(1)}, bf16[1,104,2560]{2,1,0:T(8,128)(2,1)S(1)}) fusion(f32[104]{0:T(128)S(1)} %get-tuple-element.43, s32[104]{0:T(128)S(1)} %copy-done.4, f32[104]{0:T(128)S(1)} %get-tuple-element.44), kind=kLoop, calls=%fused_computation.17 | loop fusion | flops 4259840 | bytes 2131168 | tf_op jit(solution)/shard_map/convert
  21.6 0.3 fusion.1
  21.9 0.3 fusion.3
  22.2 4.5 %collective-permute-start = (f32[4,1,2560]{2,0,1:T(4,128)S(1)}, f32[4,1,2560]{2,0,1:T(4,128)S(1)}, u32[]{:S(2)}, u32[]{:S(2)}) collective-permute-start(f32[4,1,2560]{2,0,1:T(4,128)S(1)} %get-tuple-element.25), channel_id=1, source_target_pairs={{0,4},{4,8},{8,12},{12,16},{16,20},{20,24},{24,28},{1,5},{5,9},{9,... | collective-permute-start | bytes 122888 | tf_op jit(solution)/shard_map/ppermute | solution.py:17
  26.8 1.3 %collective-permute-start.1 = (f32[4,1,2560]{2,0,1:T(4,128)S(1)}, f32[4,1,2560]{2,0,1:T(4,128)S(1)}, u32[]{:S(2)}, u32[]{:S(2)}) collective-permute-start(f32[4,1,2560]{2,0,1:T(4,128)S(1)} %get-tuple-element.26), channel_id=1, source_target_pairs={{4,0},{8,4},{12,8},{16,12},{20,16},{24,20},{28,24},{5,1},{9,5},{13... | collective-permute-start | bytes 122888 | tf_op jit(solution)/shard_map/ppermute | solution.py:20
  28.6 1.9 %collective-permute-start.4 = (f32[1,4,2560]{2,0,1:T(1,128)S(1)}, f32[1,4,2560]{2,0,1:T(1,128)S(1)}, u32[]{:S(2)}, u32[]{:S(2)}) collective-permute-start(f32[1,4,2560]{2,0,1:T(1,128)S(1)} %get-tuple-element.9), channel_id=1, source_target_pairs={{1,0},{2,1},{3,2},{5,4},{6,5},{7,6},{9,8},{10,9},{11,10},{13,12},{... | collective-permute-start | bytes 122888 | tf_op jit(solution)/shard_map/ppermute | solution.py:20
  30.5 2.4 %collective-permute-start.5 = (f32[1,4,2560]{2,0,1:T(1,128)S(1)}, f32[1,4,2560]{2,0,1:T(1,128)S(1)}, u32[]{:S(2)}, u32[]{:S(2)}) collective-permute-start(f32[1,4,2560]{2,0,1:T(1,128)S(1)} %get-tuple-element.10), channel_id=1, source_target_pairs={{0,1},{1,2},{2,3},{4,5},{5,6},{6,7},{8,9},{9,10},{10,11},{12,13},{... | collective-permute-start | bytes 122888 | tf_op jit(solution)/shard_map/ppermute | solution.py:17
  33.1 2.7 %collective-permute-done.5 = f32[1,4,2560]{2,0,1:T(1,128)S(1)} collective-permute-done((f32[1,4,2560]{2,0,1:T(1,128)S(1)}, f32[1,4,2560]{2,0,1:T(1,128)S(1)}, u32[]{:S(2)}, u32[]{:S(2)}) %collective-permute-start.5) | collective-permute-done | bytes 40992 | tf_op jit(solution)/shard_map/ppermute | solution.py:17
  36.1 4.9 %collective-permute-start.6 = (f32[4,1,2560]{2,0,1:T(4,128)S(1)}, f32[4,1,2560]{2,0,1:T(4,128)S(1)}, u32[]{:S(2)}, u32[]{:S(2)}) collective-permute-start(f32[4,1,2560]{2,0,1:T(4,128)S(1)} %get-tuple-element.19), channel_id=1, source_target_pairs={{0,4},{4,8},{8,12},{12,16},{16,20},{20,24},{24,28},{1,5},{5,9},{9,... | collective-permute-start | bytes 122888 | tf_op jit(solution)/shard_map/ppermute | solution.py:17
  41.0 1.3 %collective-permute-start.7 = (f32[4,1,2560]{2,0,1:T(4,128)S(1)}, f32[4,1,2560]{2,0,1:T(4,128)S(1)}, u32[]{:S(2)}, u32[]{:S(2)}) collective-permute-start(f32[4,1,2560]{2,0,1:T(4,128)S(1)} %get-tuple-element.20), channel_id=1, source_target_pairs={{4,0},{8,4},{12,8},{16,12},{20,16},{24,20},{28,24},{5,1},{9,5},{13... | collective-permute-start | bytes 122888 | tf_op jit(solution)/shard_map/ppermute | solution.py:20
  42.6 5.1 %collective-permute-done.7 = f32[4,1,2560]{2,0,1:T(4,128)S(1)} collective-permute-done((f32[4,1,2560]{2,0,1:T(4,128)S(1)}, f32[4,1,2560]{2,0,1:T(4,128)S(1)}, u32[]{:S(2)}, u32[]{:S(2)}) %collective-permute-start.7) | collective-permute-done | bytes 40992 | tf_op jit(solution)/shard_map/ppermute | solution.py:20
  47.9 1.9 %collective-permute-start.8 = (f32[1,4,2560]{2,0,1:T(1,128)S(1)}, f32[1,4,2560]{2,0,1:T(1,128)S(1)}, u32[]{:S(2)}, u32[]{:S(2)}) collective-permute-start(f32[1,4,2560]{2,0,1:T(1,128)S(1)} %get-tuple-element.7), channel_id=1, source_target_pairs={{1,0},{2,1},{3,2},{5,4},{6,5},{7,6},{9,8},{10,9},{11,10},{13,12},{... | collective-permute-start | bytes 122888 | tf_op jit(solution)/shard_map/ppermute | solution.py:20
  49.8 2.4 %collective-permute-start.9 = (f32[1,4,2560]{2,0,1:T(1,128)S(1)}, f32[1,4,2560]{2,0,1:T(1,128)S(1)}, u32[]{:S(2)}, u32[]{:S(2)}) collective-permute-start(f32[1,4,2560]{2,0,1:T(1,128)S(1)} %get-tuple-element.8), channel_id=1, source_target_pairs={{0,1},{1,2},{2,3},{4,5},{5,6},{6,7},{8,9},{9,10},{10,11},{12,13},{... | collective-permute-start | bytes 122888 | tf_op jit(solution)/shard_map/ppermute | solution.py:17
  52.3 2.8 %collective-permute-done.9 = f32[1,4,2560]{2,0,1:T(1,128)S(1)} collective-permute-done((f32[1,4,2560]{2,0,1:T(1,128)S(1)}, f32[1,4,2560]{2,0,1:T(1,128)S(1)}, u32[]{:S(2)}, u32[]{:S(2)}) %collective-permute-start.9) | collective-permute-done | bytes 40992 | tf_op jit(solution)/shard_map/ppermute | solution.py:17
  55.2 1.0 %fusion.4 = f32[104,2,4,2]{0,2,3,1:T(4,128)S(1)} fusion(bf16[1,104,2560]{2,1,0:T(8,128)(2,1)S(1)} %get-tuple-element.41, bf16[1,104,2560]{2,1,0:T(8,128)(2,1)S(1)} %get-tuple-element.42, f32[4,2,2560]{2,0,1:T(4,128)S(1)} %fusion.32, f32[5,2,2560]{2,0,1:T(8,128)S(1)} %fusion.17, f32[4,3,2560]{2,0,1:T(4,128)S(1)} %subtract_multiply_fusion, ...), kind=kOutput, calls=%fused_computation.9 | convolution fusion | flops 53474944 | bytes 1731584 | tf_op jit(solution)/shard_map/kji,rmi->mrkj/dot_general | solution.py:138
  56.2 0.2 copy.70
  56.4 0.2 reshape.237
  56.7 12.3 %all_to_all.36 = f32[8,1,208]{2,1,0:T(1,128)S(1)} all-to-all(f32[8,1,208]{2,1,0:T(1,128)S(1)} %reshape.237), channel_id=1, replica_groups=mesh['wave'=8,'lev'=4] {'wave'}, dimensions={0} | all-to-all | bytes 13312 | tf_op jit(solution)/shard_map/all_to_all | solution.py:146
  69.0 0.5 broadcast.309
  69.5 0.7 reduce
  70.2 0.2 reshape.238
  70.4 0.3 copy.71
  70.9 1.3 %convolution_multiply_fusion = f32[13,2,4,1280]{3,2,1,0:T(4,128)} fusion(f32[13,2,4,16]{3,2,1,0:T(4,128)S(1)} %copy.72, bf16[13,16,1280]{2,1,0:T(8,128)(2,1)S(1)} %copy-done, f32[13,1280]{1,0:T(8,128)S(1)} %get-tuple-element.33), kind=kOutput, calls=%fused_computation.6 | convolution fusion | flops 25692160 | bytes 1138176 | tf_op jit(solution)/shard_map/mrkj,mjn->mrkn/dot_general | solution.py:144
  (68 shorter events, 3.4 us)
Async XLA Ops:
  0.0 2.3 %copy-start = (bf16[13,16,1280]{2,1,0:T(8,128)(2,1)S(1)}, bf16[13,16,1280]{2,1,0:T(8,128)(2,1)}, u32[]{:S(2)}) copy-start(bf16[13,16,1280]{2,1,0:T(8,128)(2,1)} %param.8) | copy-start | bytes 1597444
  2.3 1.0 %copy-start.2 = (bf16[13,16,1280]{2,1,0:T(8,128)(2,1)S(1)}, bf16[13,16,1280]{2,1,0:T(8,128)(2,1)}, u32[]{:S(2)}) copy-start(bf16[13,16,1280]{2,1,0:T(8,128)(2,1)} %param.9) | copy-start | bytes 1597444
  3.7 7.5 %copy-start.1 = (f32[4,2,2560]{2,1,0:T(2,128)S(1)}, f32[4,2,2560]{2,1,0:T(2,128)}, u32[]{:S(2)}) copy-start(f32[4,2,2560]{2,1,0:T(2,128)} %param.10) | copy-start | bytes 245764
  4.2 12.4 %copy-start.4 = (s32[104]{0:T(128)S(1)}, s32[104]{0:T(128)}, u32[]{:S(2)}) copy-start(s32[104]{0:T(128)} %param.13) | copy-start | bytes 1252
  4.2 12.4 %copy-start.5 = (f32[2]{0:T(128)S(1)}, f32[2]{0:T(128)}, u32[]{:S(2)}) copy-start(f32[2]{0:T(128)} %param.12) | copy-start | bytes 28
  5.3 16.0 %all-to-all-start = ((bf16[8,2,208]{2,1,0:T(2,128)(2,1)}), bf16[8,2,208]{2,1,0:T(2,128)(2,1)S(1)}, u32[]{:S(2)}, u32[]{:S(2)}) async-start(bf16[8,2,208]{2,1,0:T(2,128)(2,1)} %reshape.235), calls=%async_computation | async-start | bytes 16384 | tf_op jit(solution)/shard_map/all_to_all | solution.py:104
  11.3 16.9 %collective-permute-start.2 = (f32[4,1,2560]{2,0,1:T(4,128)S(1)}, f32[4,1,2560]{2,0,1:T(4,128)S(1)}, u32[]{:S(2)}, u32[]{:S(2)}) collective-permute-start(f32[4,1,2560]{2,0,1:T(4,128)S(1)} %copy.105), channel_id=1, source_target_pairs={{0,4},{4,8},{8,12},{12,16},{16,20},{20,24},{24,28},{1,5},{5,9},{9,... | collective-permute-start | bytes 122888 | tf_op jit(solution)/shard_map/ppermute | solution.py:17
  15.2 13.1 %collective-permute-start.3 = (f32[4,1,2560]{2,0,1:T(4,128)S(1)}, f32[4,1,2560]{2,0,1:T(4,128)S(1)}, u32[]{:S(2)}, u32[]{:S(2)}) collective-permute-start(f32[4,1,2560]{2,0,1:T(4,128)S(1)} %copy.106), channel_id=1, source_target_pairs={{4,0},{8,4},{12,8},{16,12},{20,16},{24,20},{28,24},{5,1},{9,5},{13... | collective-permute-start | bytes 122888 | tf_op jit(solution)/shard_map/ppermute | solution.py:20
  21.9 6.3 %copy-start.3 = (s32[4,2,2560]{2,1,0:T(2,128)S(1)}, s32[4,2,2560]{2,1,0:T(2,128)}, u32[]{:S(2)}) copy-start(s32[4,2,2560]{2,1,0:T(2,128)} %param.11) | copy-start | bytes 245764
  22.2 10.7 %collective-permute-start = (f32[4,1,2560]{2,0,1:T(4,128)S(1)}, f32[4,1,2560]{2,0,1:T(4,128)S(1)}, u32[]{:S(2)}, u32[]{:S(2)}) collective-permute-start(f32[4,1,2560]{2,0,1:T(4,128)S(1)} %get-tuple-element.25), channel_id=1, source_target_pairs={{0,4},{4,8},{8,12},{12,16},{16,20},{20,24},{24,28},{1,5},{5,9},{9,... | collective-permute-start | bytes 122888 | tf_op jit(solution)/shard_map/ppermute | solution.py:17
  26.8 6.2 %collective-permute-start.1 = (f32[4,1,2560]{2,0,1:T(4,128)S(1)}, f32[4,1,2560]{2,0,1:T(4,128)S(1)}, u32[]{:S(2)}, u32[]{:S(2)}) collective-permute-start(f32[4,1,2560]{2,0,1:T(4,128)S(1)} %get-tuple-element.26), channel_id=1, source_target_pairs={{4,0},{8,4},{12,8},{16,12},{20,16},{24,20},{28,24},{5,1},{9,5},{13... | collective-permute-start | bytes 122888 | tf_op jit(solution)/shard_map/ppermute | solution.py:20
  28.6 4.5 %collective-permute-start.4 = (f32[1,4,2560]{2,0,1:T(1,128)S(1)}, f32[1,4,2560]{2,0,1:T(1,128)S(1)}, u32[]{:S(2)}, u32[]{:S(2)}) collective-permute-start(f32[1,4,2560]{2,0,1:T(1,128)S(1)} %get-tuple-element.9), channel_id=1, source_target_pairs={{1,0},{2,1},{3,2},{5,4},{6,5},{7,6},{9,8},{10,9},{11,10},{13,12},{... | collective-permute-start | bytes 122888 | tf_op jit(solution)/shard_map/ppermute | solution.py:20
  30.5 5.3 %collective-permute-start.5 = (f32[1,4,2560]{2,0,1:T(1,128)S(1)}, f32[1,4,2560]{2,0,1:T(1,128)S(1)}, u32[]{:S(2)}, u32[]{:S(2)}) collective-permute-start(f32[1,4,2560]{2,0,1:T(1,128)S(1)} %get-tuple-element.10), channel_id=1, source_target_pairs={{0,1},{1,2},{2,3},{4,5},{5,6},{6,7},{8,9},{9,10},{10,11},{12,13},{... | collective-permute-start | bytes 122888 | tf_op jit(solution)/shard_map/ppermute | solution.py:17
  36.1 6.6 %collective-permute-start.6 = (f32[4,1,2560]{2,0,1:T(4,128)S(1)}, f32[4,1,2560]{2,0,1:T(4,128)S(1)}, u32[]{:S(2)}, u32[]{:S(2)}) collective-permute-start(f32[4,1,2560]{2,0,1:T(4,128)S(1)} %get-tuple-element.19), channel_id=1, source_target_pairs={{0,4},{4,8},{8,12},{12,16},{16,20},{20,24},{24,28},{1,5},{5,9},{9,... | collective-permute-start | bytes 122888 | tf_op jit(solution)/shard_map/ppermute | solution.py:17
  41.0 6.8 %collective-permute-start.7 = (f32[4,1,2560]{2,0,1:T(4,128)S(1)}, f32[4,1,2560]{2,0,1:T(4,128)S(1)}, u32[]{:S(2)}, u32[]{:S(2)}) collective-permute-start(f32[4,1,2560]{2,0,1:T(4,128)S(1)} %get-tuple-element.20), channel_id=1, source_target_pairs={{4,0},{8,4},{12,8},{16,12},{20,16},{24,20},{28,24},{5,1},{9,5},{13... | collective-permute-start | bytes 122888 | tf_op jit(solution)/shard_map/ppermute | solution.py:20
  47.9 4.5 %collective-permute-start.8 = (f32[1,4,2560]{2,0,1:T(1,128)S(1)}, f32[1,4,2560]{2,0,1:T(1,128)S(1)}, u32[]{:S(2)}, u32[]{:S(2)}) collective-permute-start(f32[1,4,2560]{2,0,1:T(1,128)S(1)} %get-tuple-element.7), channel_id=1, source_target_pairs={{1,0},{2,1},{3,2},{5,4},{6,5},{7,6},{9,8},{10,9},{11,10},{13,12},{... | collective-permute-start | bytes 122888 | tf_op jit(solution)/shard_map/ppermute | solution.py:20
  49.8 5.3 %collective-permute-start.9 = (f32[1,4,2560]{2,0,1:T(1,128)S(1)}, f32[1,4,2560]{2,0,1:T(1,128)S(1)}, u32[]{:S(2)}, u32[]{:S(2)}) collective-permute-start(f32[1,4,2560]{2,0,1:T(1,128)S(1)} %get-tuple-element.8), channel_id=1, source_target_pairs={{0,1},{1,2},{2,3},{4,5},{5,6},{6,7},{8,9},{9,10},{10,11},{12,13},{... | collective-permute-start | bytes 122888 | tf_op jit(solution)/shard_map/ppermute | solution.py:17
where the time goes:
time: 72.7 us; the launch traced here: 72.1 us
  starting transfers between devices  31.7 us (44%)
  blocking collectives  12.3 us (17%)
  waiting for transfers between devices  10.8 us (15%)
  other arithmetic  8.43 us (12%)
  local copies, waits for them, and re-layouts  4.93 us (7%)
  matrix products  3.49 us (5%)
    ppermute x5, starting transfers between devices, extended(): lax.ppermute(lax.slice_in_dim(block, block.shape[dim] - width, None, axis...  18.2 us
    all_to_all x1, blocking collectives, on_device(): lax.all_to_all(outgoing, 'wave', split_axis=0, concat_axis=3, tiled=True)  12.3 us
    ppermute x5, starting transfers between devices, extended(): lax.ppermute(lax.slice_in_dim(block, 0, width, axis=dim), axis, backward)  7.72 us
    all_to_all x1, starting transfers between devices, on_device(): lax.all_to_all(fourier, 'wave', split_axis=3, concat_axis=0, tiled=True)  5.83 us
    ppermute x5, waiting for transfers between devices, extended(): lax.ppermute(lax.slice_in_dim(block, block.shape[dim] - width, None, axis...  5.54 us
    ppermute x5, waiting for transfers between devices, extended(): lax.ppermute(lax.slice_in_dim(block, 0, width, axis=dim), axis, backward)  5.22 us
    another operation x2, other arithmetic  4.61 us
    unnamed x29, local copies, waits for them, and re-layouts  2.8 us
  transfers between devices with their start and end apart: 11, of which 5 were waited for; matrix products, arithmetic and copies ran while one was open for 9% of the time, Pallas kernels for 0%

commit v1 on v0

v1 whole, which is shorter than its diff:
```python
import math

import jax
import jax.numpy as jnp
from jax import lax
from jax.sharding import PartitionSpec as P

diffusivity = 0.15
courant_limit = 0.45
halo = 2


def neighbours(axis):
    count = lax.axis_size(axis)
    forward = [(i, i + 1) for i in range(count - 1)]
    return forward, [(target, source) for source, target in forward]


def wave_table(slot_wave, lon_count):
    longitude = jnp.arange(lon_count, dtype=jnp.int32)
    phase_index = slot_wave[:, None] * longitude[None, :] % lon_count
    angles = 2.0 * math.pi / lon_count * phase_index.astype(jnp.float32)
    return jnp.stack([jnp.cos(angles), -jnp.sin(angles)]).astype(jnp.bfloat16)


def combine_winds(legendre_sum, slope_sum, scaled_wave, doubled):
    zonal_real = -scaled_wave * legendre_sum[:, 3] - slope_sum[:, 0]
    zonal_imag = scaled_wave * legendre_sum[:, 2] - slope_sum[:, 1]
    merid_real = -scaled_wave * legendre_sum[:, 1] + slope_sum[:, 2]
    merid_imag = scaled_wave * legendre_sum[:, 0] + slope_sum[:, 3]
    stacked = jnp.stack([zonal_real, zonal_imag, merid_real, merid_imag], axis=1)
    return (stacked * doubled).astype(jnp.bfloat16)


def face_terms(zonal_courant, switched):
    face_speed = 0.5 * (jnp.roll(zonal_courant, 1, axis=2) + zonal_courant)
    magnitude = jnp.abs(face_speed)
    diffuse = 0.5 * (magnitude - switched * (magnitude - face_speed * face_speed))
    return (face_speed, diffuse)


def tendency_of(
    padded, face_speed, diffuse, meridional, row_start, level_start, rows_total, levels_total
):
    centre = padded[1:-1, 1:-1]
    western = jnp.roll(centre, 1, axis=2)
    flux_east = face_speed * 0.5 * (western + centre) - diffuse * (centre - western)
    southern = padded[1:-1, :-1]
    northern = padded[1:-1, 1:]
    lat_speed = 0.5 * (meridional[1:-1, :-1] + meridional[1:-1, 1:])
    flux_north = lat_speed * 0.5 * (southern + northern) - 0.5 * jnp.abs(lat_speed) * (
        northern - southern
    )
    face_index = row_start + jnp.arange(flux_north.shape[1], dtype=jnp.int32)
    open_rows = ((face_index > 0) & (face_index < rows_total)).astype(jnp.float32)
    flux_north = flux_north * open_rows[None, :, None]
    level_index = level_start + jnp.arange(padded.shape[0] - 1, dtype=jnp.int32)
    open_levels = ((level_index > 0) & (level_index < levels_total)).astype(jnp.float32)
    flux_up = diffusivity * (padded[1:, 1:-1] - padded[:-1, 1:-1]) * open_levels[:, None, None]
    return (
        -(jnp.roll(flux_east, -1, axis=2) - flux_east)
        - (flux_north[:, 1:] - flux_north[:, :-1])
        + (flux_up[1:] - flux_up[:-1])
    )


def exchange_edges(tracer, switched):
    levels, rows, lon_count = tracer.shape
    forward, backward = neighbours("wave")
    north = jnp.concatenate([tracer[:, -2:], switched[:, -1:]], axis=1)
    south = jnp.concatenate([tracer[:, :2], switched[:, :1]], axis=1)
    from_south = lax.ppermute(north, "wave", forward)
    from_north = lax.ppermute(south, "wave", backward)
    rows_ext = jnp.concatenate([from_south[:, :2], tracer, from_north[:, :2]], axis=1)
    flags_ext = jnp.concatenate([from_south[:, 2:], switched, from_north[:, 2:]], axis=1)
    forward, backward = neighbours("lev")

    def packed(edge, inner):
        return jnp.concatenate(
            [rows_ext[edge, 1:-1], rows_ext[inner, 2:-2], switched[edge]], axis=0
        )

    from_below = lax.ppermute(packed(levels - 1, levels - 2), "lev", forward)
    from_above = lax.ppermute(packed(0, 1), "lev", backward)

    def unpacked(got):
        near = jnp.pad(got[: rows + 2], ((1, 1), (0, 0)))
        far = jnp.pad(got[rows + 2 : 2 * rows + 2], ((2, 2), (0, 0)))
        flags = jnp.pad(got[2 * rows + 2 :], ((1, 1), (0, 0)))
        return near[None], far[None], flags[None]

    near_b, far_b, flags_b = unpacked(from_below)
    near_a, far_a, flags_a = unpacked(from_above)
    tracer_ext = jnp.concatenate([far_b, near_b, rows_ext, near_a, far_a], axis=0)
    return tracer_ext, jnp.concatenate([flags_b, flags_ext, flags_a], axis=0)


def on_device(spectra, legendre, derivative, tracer, limiter_flags, lat_weight, slot_wave):
    slot_count = spectra.shape[0]
    level_count = spectra.shape[2]
    degree_count = spectra.shape[3]
    lat_total = legendre.shape[1]
    band_rows = tracer.shape[1]
    lon_count = tracer.shape[2]
    bands = lax.axis_size("wave")
    sets = lax.axis_size("lev")
    assert band_rows >= halo and level_count >= halo
    lev_total = level_count * sets
    band_index = lax.axis_index("wave")
    row_start = band_index * band_rows
    level_start = lax.axis_index("lev") * level_count
    local_wave = lax.dynamic_slice_in_dim(slot_wave, band_index * slot_count, slot_count)
    degree = jnp.arange(degree_count, dtype=jnp.int32)
    live_mask = degree[None, :] >= local_wave[:, None]
    coefficients = (spectra * live_mask[:, None, None, :].astype(spectra.dtype)).reshape(
        slot_count, 4 * level_count, degree_count
    )
    legendre_sum = jnp.einsum(
        "mcn,mln->mcl", coefficients, legendre, preferred_element_type=jnp.float32
    ).reshape(slot_count, 4, level_count, lat_total)
    slope_sum = jnp.einsum(
        "mcn,mln->mcl", coefficients, derivative, preferred_element_type=jnp.float32
    ).reshape(slot_count, 4, level_count, lat_total)
    scaled_wave = (local_wave.astype(jnp.float32) / degree_count)[:, None, None]
    doubled = jnp.where(local_wave == 0, 1.0, 2.0).astype(jnp.float32)[:, None, None, None]
    fourier = combine_winds(legendre_sum, slope_sum, scaled_wave, doubled)
    rimmed = jnp.pad(fourier, ((0, 0), (0, 0), (0, 0), (halo, halo)))
    window = band_rows + 2 * halo
    pieces = jnp.stack([rimmed[..., b * band_rows : b * band_rows + window] for b in range(bands)])
    piece_shape = pieces.shape[1:]
    pieces = jnp.broadcast_to(
        pieces.reshape(bands, 1, -1), (bands, sets, math.prod(piece_shape))
    ).reshape(bands * sets, -1)
    arrived = lax.all_to_all(pieces, ("wave", "lev"), split_axis=0, concat_axis=0, tiled=True)
    table = wave_table(slot_wave, lon_count)
    tracer_ext, flags_ext = exchange_edges(tracer, limiter_flags.astype(jnp.float32))

    arrived = arrived.reshape((bands, sets) + piece_shape)
    arrived = arrived.transpose(3, 0, 2, 1, 4, 5).reshape(
        2, 2, bands * slot_count, lev_total, window
    )
    arrived = jnp.pad(arrived, ((0, 0), (0, 0), (0, 0), (halo, halo), (0, 0)))
    arrived = lax.dynamic_slice_in_dim(arrived, level_start, level_count + 2 * halo, axis=3)
    winds = jnp.einsum("ermkj,rmi->ekji", arrived, table, preferred_element_type=jnp.float32)
    zonal_courant = courant_limit * jnp.tanh(winds[0, 1:-1, 1:-1])
    merid_courant = courant_limit * jnp.tanh(winds[1])
    face_speed, diffuse = face_terms(zonal_courant, flags_ext)
    section_one = tracer_ext[1:-1, 1:-1] + tendency_of(
        tracer_ext,
        face_speed,
        diffuse,
        merid_courant,
        row_start - 1,
        level_start - 1,
        lat_total,
        lev_total,
    )
    section_two = tendency_of(
        section_one,
        face_speed[1:-1, 1:-1],
        diffuse[1:-1, 1:-1],
        merid_courant[1:-1, 1:-1],
        row_start,
        level_start,
        lat_total,
        lev_total,
    )
    updated = 0.5 * tracer + 0.5 * (section_one[1:-1, 1:-1] + section_two)
    change = updated - tracer
    lat_scale = lat_weight * (1.0 / math.sqrt(lon_count))
    projected = jnp.einsum(
        "kji,rmi->mrkj", change, table.astype(jnp.float32), precision=lax.Precision.HIGHEST
    )
    outgoing = projected * lat_scale[None, None, None, :]
    live_float = live_mask.astype(jnp.float32)
    legendre_wide = legendre.astype(jnp.float32)
    summed = jnp.einsum(
        "mrkj,mjn->mrkn",
        lax.all_to_all(outgoing, "wave", split_axis=0, concat_axis=3, tiled=True),
        legendre_wide,
        precision=lax.Precision.HIGHEST,
    )
    return summed * live_float[:, None, None, :]


def solution(mesh):
    return jax.shard_map(
        on_device,
        mesh=mesh,
        in_specs=(
            P("wave", None, "lev", None),
            P("wave", None, None),
            P("wave", None, None),
            P("lev", "wave", None),
            P("lev", "wave", None),
            P("wave"),
            P(),
        ),
        out_specs=P("wave", None, "lev", None),
        check_vma=False,
    )
```

time: 72.7 us -> 71.8 us (0.988)
  the two profiles are of different devices: /device:TPU:2 before, /device:TPU:0 now
where the time goes in v1:
time: 71.8 us; the launch traced here: 71.1 us
  local copies, waits for them, and re-layouts  21 us (29%)
  starting transfers between devices  18.1 us (25%)
  other arithmetic  14.9 us (21%)
  blocking collectives  12.1 us (17%)
  matrix products  4.33 us (6%)
    all_to_all x1, blocking collectives, on_device(): lax.all_to_all(outgoing, 'wave', split_axis=0, concat_axis=3, tiled=True)  12.1 us
    all_to_all x1, starting transfers between devices, on_device(): lax.all_to_all(pieces, ('wave', 'lev'), split_axis=0, concat_axis=0, tile...  6.96 us
    another operation x1, other arithmetic  5.37 us
    transpose x1, local copies, waits for them, and re-layouts, on_device(): arrived.transpose(3, 0, 2, 1, 4, 5)  5.32 us
    ppermute x1, starting transfers between devices, exchange_edges(): from_south = lax.ppermute(north, 'wave', forward)  4.91 us
    unnamed x31, local copies, waits for them, and re-layouts  4.07 us
    ppermute x1, starting transfers between devices, exchange_edges(): from_below = lax.ppermute(packed(levels - 1, levels - 2), 'lev', forward)  3.66 us
    slice x2, local copies, waits for them, and re-layouts, unpacked(): flags = jnp.pad(got[2 * rows + 2:], ((1, 1), (0, 0)))  1.97 us
  transfers between devices with their start and end apart: 5, of which 0 were waited for; matrix products, arithmetic and copies ran while one was open for 35% of the time, Pallas kernels for 0%

profile of v1, /device:TPU:0, one launch (start us, length us, event | category | flops | bytes accessed | tf_op | source)
XLA Modules:
  0.0 71.1 jit_solution(16736982161866792287)
XLA Ops:
  0.0 1.0 %convert_element_type.79 = f32[4,2,2560]{2,1,0:T(2,128)S(1)} convert(s32[4,2,2560]{2,1,0:T(2,128)} %param.11) | non-fusion elementwise | flops 20480 | bytes 163840 | tf_op jit(solution)/shard_map/convert_element_type | solution.py:136
  1.1 1.0 %pad_maximum_fusion.18 = (f32[4,3,2560]{2,1,0:T(4,128)S(1)}, f32[4,3,2560]{2,1,0:T(4,128)S(1)}) fusion(f32[4,2,2560]{2,1,0:T(2,128)} %param.10, f32[4,1,2560]{2,1,0:T(1,128)S(1)} %get-tuple-element.31, f32[4,1,2560]{2,1,0:T(1,128)S(1)} %get-tuple-element.32), kind=kLoop, calls=%fused_computation.55 | loop fusion | flops 61440 | bytes 409600 | tf_op jit(solution)/shard_map/concatenate | solution.py:70
  2.1 4.9 %collective-permute-start = (f32[4,3,2560]{2,1,0:T(4,128)S(1)}, f32[4,3,2560]{2,1,0:T(4,128)S(1)}, u32[]{:S(2)}, u32[]{:S(2)}) collective-permute-start(f32[4,3,2560]{2,1,0:T(4,128)S(1)} %get-tuple-element.29), channel_id=1, source_target_pairs={{0,4},{4,8},{8,12},{12,16},{16,20},{20,24},{24,28},{1,5},{5,9},{9,... | collective-permute-start | bytes 368648 | tf_op jit(solution)/shard_map/ppermute | solution.py:72
  7.0 1.3 %collective-permute-start.1 = (f32[4,3,2560]{2,1,0:T(4,128)S(1)}, f32[4,3,2560]{2,1,0:T(4,128)S(1)}, u32[]{:S(2)}, u32[]{:S(2)}) collective-permute-start(f32[4,3,2560]{2,1,0:T(4,128)S(1)} %get-tuple-element.30), channel_id=1, source_target_pairs={{4,0},{8,4},{12,8},{16,12},{20,16},{24,20},{28,24},{5,1},{9,5},{13... | collective-permute-start | bytes 368648 | tf_op jit(solution)/shard_map/ppermute | solution.py:73
  8.3 0.7 %compare_select_fusion = (f32[13]{0:T(128)S(1)}, s32[13]{0:T(128)S(1)}) fusion(s32[104]{0:T(128)} %param.13, s32[]{:T(128)S(6)} %select_n.29), kind=kLoop, calls=%fused_computation.127 | loop fusion | flops 26 | bytes 160 | tf_op jit(solution)/shard_map/jit(_where)/select_n | solution.py:125
  9.5 0.7 copy-done.6
  12.8 0.5 broadcast.281
  13.4 1.1 %reduce.1 = bf16[32,1248]{1,0:T(8,128)(2,1)S(1)} reduce(bf16[32,1,1248]{2,1,0:T(2,128)(2,1)S(1)} %all_to_all.25, bf16[]{:T(256)} %broadcast.281), dimensions={1}, to_apply=%all_to_all.25.reduce_sub_computation | reduce | bytes 159746 | tf_op jit(solution)/shard_map/all_to_all | solution.py:134
  14.5 0.8 %reshape.205 = bf16[32,2,624]{2,1,0:T(2,128)(2,1)} reshape(bf16[32,1248]{1,0:T(8,128)(2,1)S(1)} %reduce.1) | data formatting | bytes 159744
  15.3 7.0 %all-to-all-start = ((bf16[32,2,624]{2,1,0:T(2,128)(2,1)}), bf16[32,2,624]{2,1,0:T(2,128)(2,1)S(1)}, u32[]{:S(2)}, u32[]{:S(2)}) async-start(bf16[32,2,624]{2,1,0:T(2,128)(2,1)} %reshape.205), calls=%async_computation | async-start | bytes 163840 | tf_op jit(solution)/shard_map/all_to_all | solution.py:134
  22.3 5.4 %cosine_convert_fusion = (bf16[1,104,2560]{2,1,0:T(8,128)(2,1)}, bf16[1,104,2560]{2,1,0:T(8,128)(2,1)}) fusion(s32[104]{0:T(128)S(1)} %copy-done.7), kind=kLoop, calls=%fused_computation.11 | loop fusion | flops 3194880 | bytes 1065376 | tf_op jit(solution)/shard_map/convert
  28.0 0.9 %copy.73 = f32[4,6,2560]{2,0,1:T(4,128)} copy(f32[4,6,2560]{2,1,0:T(8,128)S(1)} %pad_maximum_fusion.7) | data formatting | bytes 491520 | tf_op jit(solution)/shard_map/concatenate | solution.py:74
  28.8 0.7 pad_maximum_fusion.20
  29.5 1.3 %collective-permute-start.3 = (f32[8,2560]{1,0:T(8,128)}, f32[8,2560]{1,0:T(8,128)}, u32[]{:S(2)}, u32[]{:S(2)}) collective-permute-start(f32[8,2560]{1,0:T(8,128)} %pad_maximum_fusion.20), channel_id=1, source_target_pairs={{1,0},{2,1},{3,2},{5,4},{6,5},{7,6},{9,8},{10,9},{11,10},{13,12},{... | collective-permute-start | bytes 245768 | tf_op jit(solution)/shard_map/ppermute | solution.py:84
  30.8 0.7 pad_maximum_fusion.19
  31.5 3.7 %collective-permute-start.2 = (f32[8,2560]{1,0:T(8,128)}, f32[8,2560]{1,0:T(8,128)}, u32[]{:S(2)}, u32[]{:S(2)}) collective-permute-start(f32[8,2560]{1,0:T(8,128)} %pad_maximum_fusion.19), channel_id=1, source_target_pairs={{0,1},{1,2},{2,3},{4,5},{5,6},{6,7},{8,9},{9,10},{10,11},{12,13},{... | collective-permute-start | bytes 245768 | tf_op jit(solution)/shard_map/ppermute | solution.py:83
  35.9 2.0 %reshape.197 = bf16[8,4,13,4,4,6]{5,4,3,2,1,0:T(4,128)(2,1)S(1)} reshape(bf16[32,1248]{1,0:T(8,128)(2,1)S(1)} %reduce) | data formatting | bytes 159744 | tf_op jit(solution)/shard_map/reshape | solution.py:138
  37.9 5.3 %copy.65 = bf16[4,8,13,4,4,6]{2,1,4,3,5,0:T(8,128)(2,1)S(1)} copy(bf16[4,8,13,4,4,6]{5,4,0,2,3,1:T(4,128)(2,1)S(1)} %bitcast.77) | data formatting | bytes 159744 | tf_op jit(solution)/shard_map/transpose | solution.py:139
  43.7 0.5 copy-done.2
  44.2 1.4 %convolution_bitcast_fusion = f32[2,8,6,2560]{3,1,2,0:T(8,128)S(1)} fusion(bf16[1,104,2560]{2,1,0:T(8,128)(2,1)} %get-tuple-element.48, bf16[1,104,2560]{2,1,0:T(8,128)(2,1)S(1)} %copy-done.2, s32[]{:T(128)S(6)} %select_n.31, bf16[2,2,104,16,6]{2,3,4,1,0:T(8,128)(2,1)S(1)} %reshape.198), kind=kOutput, calls=%fused_computation | convolution fusion | flops 102768640 | bytes 2127876 | tf_op jit(solution)/shard_map/ermkj,rmi->ekji/dot_general | solution.py:144
  46.1 1.0 %fusion.54 = (f32[2,2560]{1,0:T(2,128)S(1)}, f32[2,2560]{1,0:T(2,128)S(1)}) fusion(f32[8,2560]{1,0:T(8,128)} %collective-permute-done.3), kind=kLoop, calls=%fused_computation.139 | loop fusion | bytes 81920 | tf_op jit(solution)/shard_map/slice | solution.py:89
  47.1 1.0 %fusion.53 = (f32[2,2560]{1,0:T(2,128)S(1)}, f32[2,2560]{1,0:T(2,128)S(1)}) fusion(f32[8,2560]{1,0:T(8,128)} %collective-permute-done.2), kind=kLoop, calls=%fused_computation.138 | loop fusion | bytes 81920 | tf_op jit(solution)/shard_map/slice | solution.py:89
  48.1 0.9 %slice.314 = f32[4,2560]{1,0:T(4,128)S(1)} slice(f32[8,2560]{1,0:T(8,128)} %collective-permute-done.2), slice={[0:4], [0:2560]} | slice | bytes 81920 | tf_op jit(solution)/shard_map/slice | solution.py:87
  49.1 0.9 %slice.317 = f32[4,2560]{1,0:T(4,128)S(1)} slice(f32[8,2560]{1,0:T(8,128)} %collective-permute-done.3), slice={[0:4], [0:2560]} | slice | bytes 81920 | tf_op jit(solution)/shard_map/slice | solution.py:87
  50.2 0.6 multiply_subtract_fusion
  51.4 0.5 subtract_multiply_fusion
  52.0 0.8 %copy-done.4 = f32[4,6,2560]{2,0,1:T(4,128)S(1)} copy-done((f32[4,6,2560]{2,0,1:T(4,128)S(1)}, f32[4,6,2560]{2,0,1:T(4,128)}, u32[]{:S(2)}) %copy-start.4) | copy-done | bytes 245784
  54.4 1.0 %fusion = f32[104,2,4,2]{0,2,3,1:T(4,128)S(1)} fusion(bf16[1,104,2560]{2,1,0:T(8,128)(2,1)S(1)} %copy-done.3, bf16[1,104,2560]{2,1,0:T(8,128)(2,1)S(1)} %copy-done.2, f32[5,2,2560]{2,0,1:T(8,128)S(1)} %fusion.20, f32[4,3,2560]{2,0,1:T(4,128)S(1)} %subtract_multiply_fusion.1, f32[4,2,2560]{2,0,1:T(4,128)S(1)} %fusion.38, f32[4,2,1]{2,0,1:T(4,128)S(1)} %slice.360, ...), kind=kOutput, calls=%fused_computation.4 | convolution fusion | flops 53474944 | bytes 1731584 | tf_op jit(solution)/shard_map/kji,rmi->mrkj/dot_general | solution.py:171
  55.8 12.1 %all_to_all.28 = f32[8,1,208]{2,1,0:T(1,128)S(1)} all-to-all(f32[8,1,208]{2,1,0:T(1,128)S(1)} %reshape.207), channel_id=1, replica_groups=mesh['wave'=8,'lev'=4] {'wave'}, dimensions={0} | all-to-all | bytes 13312 | tf_op jit(solution)/shard_map/all_to_all | solution.py:179
  68.0 0.5 broadcast.282
  68.5 0.7 reduce.2
  69.8 1.3 %convolution_multiply_fusion = f32[13,2,4,1280]{3,2,1,0:T(4,128)} fusion(f32[13,2,4,16]{3,2,1,0:T(4,128)S(1)} %copy.83, bf16[13,16,1280]{2,1,0:T(8,128)(2,1)S(1)} %copy-done, f32[13,1280]{1,0:T(8,128)S(1)} %get-tuple-element.43), kind=kOutput, calls=%fused_computation.1 | convolution fusion | flops 25692160 | bytes 1138176 | tf_op jit(solution)/shard_map/mrkj,mjn->mrkn/dot_general | solution.py:177
  (101 shorter events, 8.5 us)
Async XLA Ops:
  0.0 10.5 %copy-start = (bf16[13,16,1280]{2,1,0:T(8,128)(2,1)S(1)}, bf16[13,16,1280]{2,1,0:T(8,128)(2,1)}, u32[]{:S(2)}) copy-start(bf16[13,16,1280]{2,1,0:T(8,128)(2,1)} %param.8) | copy-start | bytes 1597444
  0.0 9.2 %copy-start.5 = (bf16[13,4,4,1280]{3,2,1,0:T(4,128)(2,1)S(1)}, bf16[13,4,4,1280]{3,2,1,0:T(4,128)(2,1)}, u32[]{:S(2)}) copy-start(bf16[13,4,4,1280]{3,2,1,0:T(4,128)(2,1)} %param.7) | copy-start | bytes 1597444
  2.1 25.6 %collective-permute-start = (f32[4,3,2560]{2,1,0:T(4,128)S(1)}, f32[4,3,2560]{2,1,0:T(4,128)S(1)}, u32[]{:S(2)}, u32[]{:S(2)}) collective-permute-start(f32[4,3,2560]{2,1,0:T(4,128)S(1)} %get-tuple-element.29), channel_id=1, source_target_pairs={{0,4},{4,8},{8,12},{12,16},{16,20},{20,24},{24,28},{1,5},{5,9},{9,... | collective-permute-start | bytes 368648 | tf_op jit(solution)/shard_map/ppermute | solution.py:72
  7.0 20.8 %collective-permute-start.1 = (f32[4,3,2560]{2,1,0:T(4,128)S(1)}, f32[4,3,2560]{2,1,0:T(4,128)S(1)}, u32[]{:S(2)}, u32[]{:S(2)}) collective-permute-start(f32[4,3,2560]{2,1,0:T(4,128)S(1)} %get-tuple-element.30), channel_id=1, source_target_pairs={{4,0},{8,4},{12,8},{16,12},{20,16},{24,20},{28,24},{5,1},{9,5},{13... | collective-permute-start | bytes 368648 | tf_op jit(solution)/shard_map/ppermute | solution.py:73
  9.2 1.0 %copy-start.6 = (bf16[13,16,1280]{2,1,0:T(8,128)(2,1)S(1)}, bf16[13,16,1280]{2,1,0:T(8,128)(2,1)}, u32[]{:S(2)}) copy-start(bf16[13,16,1280]{2,1,0:T(8,128)(2,1)} %param.9) | copy-start | bytes 1597444
  11.1 11.2 %copy-start.1 = (f32[4,2,2560]{2,1,0:T(2,128)S(1)}, f32[4,2,2560]{2,1,0:T(2,128)}, u32[]{:S(2)}) copy-start(f32[4,2,2560]{2,1,0:T(2,128)} %param.10) | copy-start | bytes 245764
  11.1 11.2 %copy-start.7 = (s32[104]{0:T(128)S(1)}, s32[104]{0:T(128)}, u32[]{:S(2)}) copy-start(s32[104]{0:T(128)} %param.13) | copy-start | bytes 1252
  12.7 14.9 %copy-start.8 = (f32[2]{0:T(128)S(1)}, f32[2]{0:T(128)}, u32[]{:S(2)}) copy-start(f32[2]{0:T(128)} %param.12) | copy-start | bytes 28
  15.3 19.9 %all-to-all-start = ((bf16[32,2,624]{2,1,0:T(2,128)(2,1)}), bf16[32,2,624]{2,1,0:T(2,128)(2,1)S(1)}, u32[]{:S(2)}, u32[]{:S(2)}) async-start(bf16[32,2,624]{2,1,0:T(2,128)(2,1)} %reshape.205), calls=%async_computation | async-start | bytes 163840 | tf_op jit(solution)/shard_map/all_to_all | solution.py:134
  29.5 16.6 %collective-permute-start.3 = (f32[8,2560]{1,0:T(8,128)}, f32[8,2560]{1,0:T(8,128)}, u32[]{:S(2)}, u32[]{:S(2)}) collective-permute-start(f32[8,2560]{1,0:T(8,128)} %pad_maximum_fusion.20), channel_id=1, source_target_pairs={{1,0},{2,1},{3,2},{5,4},{6,5},{7,6},{9,8},{10,9},{11,10},{13,12},{... | collective-permute-start | bytes 245768 | tf_op jit(solution)/shard_map/ppermute | solution.py:84
  31.5 15.6 %collective-permute-start.2 = (f32[8,2560]{1,0:T(8,128)}, f32[8,2560]{1,0:T(8,128)}, u32[]{:S(2)}, u32[]{:S(2)}) collective-permute-start(f32[8,2560]{1,0:T(8,128)} %pad_maximum_fusion.19), channel_id=1, source_target_pairs={{0,1},{1,2},{2,3},{4,5},{5,6},{6,7},{8,9},{9,10},{10,11},{12,13},{... | collective-permute-start | bytes 245768 | tf_op jit(solution)/shard_map/ppermute | solution.py:83
  43.2 1.0 %copy-start.2 = (bf16[1,104,2560]{2,1,0:T(8,128)(2,1)S(1)}, bf16[1,104,2560]{2,1,0:T(8,128)(2,1)}, u32[]{:S(2)}) copy-start(bf16[1,104,2560]{2,1,0:T(8,128)(2,1)} %get-tuple-element.47) | copy-start | bytes 1597444
  51.9 0.9 %copy-start.4 = (f32[4,6,2560]{2,0,1:T(4,128)S(1)}, f32[4,6,2560]{2,0,1:T(4,128)}, u32[]{:S(2)}) copy-start(f32[4,6,2560]{2,0,1:T(4,128)} %copy.73) | copy-start | bytes 737284
  53.3 1.0 %copy-start.3 = (bf16[1,104,2560]{2,1,0:T(8,128)(2,1)S(1)}, bf16[1,104,2560]{2,1,0:T(8,128)(2,1)}, u32[]{:S(2)}) copy-start(bf16[1,104,2560]{2,1,0:T(8,128)(2,1)} %get-tuple-element.48) | copy-start | bytes 1597444

commit v2 on v0

v2 whole, which is shorter than its diff:
```python
import functools
import math

import jax
import jax.numpy as jnp
import numpy as np
from jax import lax
from jax.experimental import pallas as pl
from jax.experimental.pallas import tpu as pltpu
from jax.sharding import PartitionSpec as P

diffusivity = 0.15
courant_limit = 0.45
halo = 2
lanes = 128
packed_rows = 16


def round_up(value, step):
    return -(-value // step) * step


def contract(left, right, dims):
    return lax.dot_general(left, right, (dims, ((), ())), preferred_element_type=jnp.float32)


def vmem(count):
    return [pl.BlockSpec(memory_space=pltpu.VMEM)] * count


def smem(count):
    return [pl.BlockSpec(memory_space=pltpu.SMEM)] * count


def params(*byte_counts):
    return pltpu.CompilerParams(vmem_limit_bytes=min(60 * 2**20, 6 * 2**20 + sum(byte_counts)))


class Sizes:
    def __init__(self, spectra, legendre, tracer, bands, sets):
        self.slots, _, self.levels, self.degrees = spectra.shape
        self.lats = legendre.shape[1]
        self.rows, self.lon = tracer.shape[1:]
        self.bands, self.sets = bands, sets
        self.slot_pad = round_up(self.slots, packed_rows)
        self.window = self.rows + 2 * halo
        self.deep = self.levels + 2 * halo
        self.half = round_up(2 * self.levels * self.window, lanes // 2)
        self.piece = round_up(2 * self.half, lanes)
        self.stack = round_up(self.window * self.deep, 8)
        self.reply = round_up(2 * self.levels * self.slot_pad, lanes)
        assert self.rows == halo and self.deep == 8 and self.lon % lanes == 0


def piece_lanes(z):
    at = np.arange(z.piece)
    part, rest = at // z.half, at % z.half
    wind, rest = rest // (z.levels * z.window), rest % (z.levels * z.window)
    valid = (part < 2) & (wind < 2)
    return part, wind, rest // z.levels, rest % z.levels, valid


def pack_constants(z):
    part, wind, row, level, valid = piece_lanes(z)
    source = np.arange(z.slots * 4 * z.levels)
    channel = source // z.levels % 4
    pick = (channel[:, None] == wind * 2 + part) & (source[:, None] % z.levels == level) & valid
    gather = np.arange(z.slot_pad)[:, None] == source // (4 * z.levels)
    offset = np.where(valid, row - halo, -(10**6)) - np.arange(z.lats)[:, None]
    return (
        pick.astype(np.float32),
        jnp.asarray(gather, jnp.bfloat16),
        offset.astype(np.int32),
    )


def unpack_constant(z):
    part, wind, row, level, valid = piece_lanes(z)
    height = round_up(2 * z.stack, lanes)
    target = np.arange(2 * height)
    t_part, rest = target // height, target % height
    t_wind, rest = rest // z.stack, rest % z.stack
    t_row, t_deep = rest // z.deep, rest % z.deep
    t_valid = (t_wind < 2) & (t_row < z.window)
    same = (t_part[:, None] == part) & (t_wind[:, None] == wind) & (t_row[:, None] == row)
    same = same & valid & t_valid[:, None]
    own = same & (t_deep[:, None] == level + halo)
    below = same & (t_deep[:, None] == halo - 1) & (level == z.levels - 1)
    above = same & (t_deep[:, None] == halo + z.levels) & (level == 0)
    return jnp.asarray(np.concatenate([own, below, above], axis=1), jnp.bfloat16)


def reply_constants(z):
    at = np.arange(z.reply)
    part, rest = at // (z.levels * z.slot_pad), at % (z.levels * z.slot_pad)
    level, slot = rest // z.slot_pad, rest % z.slot_pad
    source = np.arange(2 * z.slot_pad)
    spread = (source[:, None] // z.slot_pad == part) & (source[:, None] % z.slot_pad == slot)
    pick = np.arange(z.deep)[:, None] == level + halo
    return jnp.asarray(spread, jnp.bfloat16), pick.astype(np.float32)


def legendre_kernel(
    z,
    wave_ref,
    spectra_ref,
    legendre_ref,
    derivative_ref,
    pick_ref,
    gather_ref,
    offset_ref,
    tracer_ref,
    flags_ref,
    pieces_ref,
    north_ref,
    south_ref,
):
    height = 4 * z.levels
    degree = lax.broadcasted_iota(jnp.int32, (height, z.degrees), 1)
    channel = lax.broadcasted_iota(jnp.int32, (height, z.lats), 0) // z.levels
    sign_sum = jnp.where(channel % 2 == 0, -1.0, 1.0)
    sign_slope = jnp.where(channel < 2, -1.0, 1.0)
    winds = []
    for s in range(z.slots):
        wave = wave_ref[s]
        coefficients = spectra_ref[s].reshape(height, z.degrees)
        coefficients = coefficients * jnp.where(degree >= wave, 1.0, 0.0).astype(jnp.bfloat16)
        sums = contract(coefficients, legendre_ref[s], ((1,), (1,)))
        slopes = contract(coefficients, derivative_ref[s], ((1,), (1,)))
        turned = jnp.concatenate(
            [sums[c * z.levels : (c + 1) * z.levels] for c in (3, 2, 1, 0)], axis=0
        )
        scaled = wave.astype(jnp.float32) / z.degrees
        doubled = jnp.where(wave == 0, 1.0, 2.0)
        winds.append((scaled * sign_sum * turned + sign_slope * slopes) * doubled)
    winds = jnp.concatenate(winds, axis=0).astype(jnp.bfloat16)

    def one_band(b, carry):
        choose = jnp.where(offset_ref[...] + b * z.rows == 0, 1.0, 0.0).astype(jnp.bfloat16)
        spread = contract(winds, choose, ((1,), (0,))) * pick_ref[...]
        piece = contract(gather_ref[...], spread.astype(jnp.bfloat16), ((1,), (0,)))
        piece = piece.astype(jnp.bfloat16)
        for l in range(z.sets):
            pieces_ref[b * z.sets + l] = piece
        return carry

    if z.bands <= 16:
        for b in range(z.bands):
            one_band(b, 0)
    else:
        lax.fori_loop(0, z.bands, one_band, 0)

    for j in range(z.rows):
        row = tracer_ref[:, j, :]
        north_ref[j] = row
        south_ref[j] = row
    north_ref[z.rows] = flags_ref[:, z.rows - 1, :].astype(jnp.float32)
    south_ref[z.rows] = flags_ref[:, 0, :].astype(jnp.float32)


def table_kernel(z, wave_ref, table_ref):
    wave = wave_ref[...].astype(jnp.float32)
    height = wave.shape[0]
    chunks = z.lon // lanes
    at = lax.broadcasted_iota(jnp.int32, (height, lanes), 1).astype(jnp.float32)

    def parts(phase):
        phase = phase - jnp.floor(phase * (1.0 / z.lon) + 0.5) * z.lon
        angle = phase * (2.0 * math.pi / z.lon)
        return jnp.cos(angle), jnp.sin(angle)

    fine_cos, fine_sin = parts(wave * at)
    coarse = [parts(wave * ((at + b) * lanes)) for b in range(0, chunks, lanes)]
    for a in range(chunks):
        cos_a = coarse[a // lanes][0][:, a % lanes : a % lanes + 1]
        sin_a = coarse[a // lanes][1][:, a % lanes : a % lanes + 1]
        columns = slice(a * lanes, (a + 1) * lanes)
        table_ref[:height, columns] = (cos_a * fine_cos - sin_a * fine_sin).astype(jnp.bfloat16)
        table_ref[height:, columns] = (-(sin_a * fine_cos + cos_a * fine_sin)).astype(jnp.bfloat16)


def edge_kernel(z, tracer_ref, flags_ref, south_ref, north_ref, up_ref, down_ref):
    for out_ref, near, far in (
        (up_ref, z.levels - 1, z.levels - 2),
        (down_ref, 0, 1),
    ):
        out_ref[0:1] = south_ref[z.rows - 1, near : near + 1]
        out_ref[1 : 1 + z.rows] = tracer_ref[near]
        out_ref[1 + z.rows : 2 + z.rows] = north_ref[0, near : near + 1]
        out_ref[2 + z.rows : 2 + 2 * z.rows] = tracer_ref[far]
        out_ref[2 + 2 * z.rows : 2 + 3 * z.rows] = flags_ref[near].astype(jnp.float32)


def grid_kernel(
    z,
    place_ref,
    weight_ref,
    arrived_ref,
    unpack_ref,
    table_ref,
    tracer_ref,
    flags_ref,
    south_ref,
    north_ref,
    below_ref,
    above_ref,
    spread_ref,
    pick_ref,
    reply_ref,
    q_ref,
    f_ref,
):
    band, level_set = place_ref[0], place_ref[1]
    lat_total = z.bands * z.rows
    lev_total = z.sets * z.levels
    own = slice(halo, halo + z.levels)
    q_ref[...] = jnp.zeros_like(q_ref)
    f_ref[...] = jnp.zeros_like(f_ref)
    for j in range(halo):
        q_ref[j, own] = south_ref[z.rows - halo + j]
        q_ref[halo + z.rows + j, own] = north_ref[j]
    f_ref[0, own] = south_ref[z.rows]
    f_ref[z.rows + 1, own] = north_ref[z.rows]
    for j in range(z.rows):
        q_ref[halo + j, own] = tracer_ref[:, j, :]
        f_ref[1 + j, own] = flags_ref[:, j, :].astype(jnp.float32)
    for got_ref, near, far in ((below_ref, halo - 1, 0), (above_ref, halo + z.levels, z.deep - 1)):
        for j in range(z.rows + 2):
            q_ref[halo - 1 + j, near : near + 1] = got_ref[j : j + 1]
        for j in range(z.rows):
            at = z.rows + 2 + j
            q_ref[halo + j, far : far + 1] = got_ref[at : at + 1]
            at = 2 * z.rows + 2 + j
            f_ref[1 + j, near : near + 1] = got_ref[at : at + 1]

    height = z.bands * z.slot_pad

    def from_set(index):
        return arrived_ref[:, index].reshape(height, z.piece)

    blocks = jnp.concatenate(
        [
            from_set(level_set),
            from_set(jnp.maximum(level_set - 1, 0)),
            from_set(jnp.minimum(level_set + 1, z.sets - 1)),
        ],
        axis=1,
    )
    turned = contract(unpack_ref[...], blocks, ((1,), (1,))).astype(jnp.bfloat16)
    span = turned.shape[0] // 2
    turned = jnp.concatenate([turned[:span], turned[span:]], axis=1)
    winds = contract(turned, table_ref[...], ((1,), (0,)))

    def wind(which, j):
        first = which * z.stack + j * z.deep
        return courant_limit * jnp.tanh(winds[first : first + z.deep])

    zonal = [wind(0, j) for j in range(1, z.rows + 3)]
    merid = [wind(1, j) for j in range(z.window)]

    def west(x):
        return pltpu.roll(x, 1, 1)

    def east(x):
        return pltpu.roll(x, z.lon - 1, 1)

    face = []
    for j in range(z.rows + 2):
        speed = 0.5 * (west(zonal[j]) + zonal[j])
        magnitude = jnp.abs(speed)
        diffuse = 0.5 * (magnitude - f_ref[j] * (magnitude - speed * speed))
        face.append((speed, diffuse))
    lat_face = []
    for j in range(1, z.window):
        index = band * z.rows - halo + j
        is_open = jnp.where((index > 0) & (index < lat_total), 0.5, 0.0).astype(jnp.float32)
        speed = 0.5 * (merid[j - 1] + merid[j])
        lat_face.append((speed * is_open, jnp.abs(speed) * is_open))
    deep = lax.broadcasted_iota(jnp.int32, (z.deep, z.lon), 0) + (level_set * z.levels - halo)
    rise = jnp.where((deep > 0) & (deep < lev_total), diffusivity, 0.0).astype(jnp.float32)

    def tendency(q, first):
        north_flux = []
        for j in range(len(q) - 1):
            mean, spread = lat_face[first - 1 + j]
            north_flux.append(mean * (q[j] + q[j + 1]) - spread * (q[j + 1] - q[j]))
        result = []
        for j in range(1, len(q) - 1):
            speed, diffuse = face[first - 2 + j]
            centre = q[j]
            western = west(centre)
            flux = speed * 0.5 * (western + centre) - diffuse * (centre - western)
            lift = rise * (centre - pltpu.roll(centre, 1, 0))
            result.append(
                -(east(flux) - flux)
                - (north_flux[j] - north_flux[j - 1])
                + (pltpu.roll(lift, z.deep - 1, 0) - lift)
            )
        return result

    tracer = [q_ref[j] for j in range(z.window)]
    first_tendency = tendency(tracer, 1)
    section_one = [q + t for q, t in zip(tracer[1:-1], first_tendency)]
    section_two = tendency(section_one, 2)
    tops, lows = [], []
    for j in range(z.rows):
        q = tracer[halo + j]
        change = 0.5 * q + 0.5 * (section_one[1 + j] + section_two[j]) - q
        top = change.astype(jnp.bfloat16)
        tops.append(top.astype(jnp.float32))
        lows.append(change - tops[-1])
    both = jnp.concatenate(tops + lows, axis=0).astype(jnp.bfloat16)
    projected = contract(both, table_ref[...], ((1,), (1,)))
    count = z.rows * z.deep
    projected = projected[:count] + projected[count:]
    scaled = []
    for j in range(z.rows):
        scale = weight_ref[j] * (1.0 / math.sqrt(z.lon))
        scaled.append(projected[j * z.deep : (j + 1) * z.deep] * scale)
    scaled = jnp.concatenate(scaled, axis=0)
    top = scaled.astype(jnp.bfloat16)
    low = (scaled - top.astype(jnp.float32)).astype(jnp.bfloat16)
    both = jnp.concatenate([top, low], axis=0)
    for b in range(z.bands):
        first = b * z.slot_pad
        block = jnp.concatenate(
            [both[:, p * height + first : p * height + first + z.slot_pad] for p in range(2)], axis=1
        )
        block = contract(block, spread_ref[...], ((1,), (0,)))
        block = block[:count] + block[count:]
        for j in range(z.rows):
            mine = block[j * z.deep : (j + 1) * z.deep] * pick_ref[...]
            reply_ref[b, j : j + 1] = jnp.sum(mine, axis=0, keepdims=True)


def analysis_kernel(z, wave_ref, arrived_ref, legendre_ref, out_ref, turned_ref):
    arrived = arrived_ref[...].reshape(z.lats, z.reply)
    top = arrived.astype(jnp.bfloat16).astype(jnp.float32)
    turned = jnp.concatenate([top, arrived - top], axis=0)
    width = turned_ref.shape[2]
    for c in range(turned_ref.shape[0]):
        turned_ref[c] = turned[c * width : (c + 1) * width].T
    height = 2 * z.levels
    degree = lax.broadcasted_iota(jnp.int32, (height, z.degrees), 1)
    for s in range(z.slots):
        left = [
            turned_ref[c, pl.ds(s, height, stride=z.slot_pad), :].astype(jnp.bfloat16)
            for c in range(turned_ref.shape[0])
        ]
        left = jnp.concatenate(left, axis=1)
        right = jnp.concatenate([legendre_ref[s], legendre_ref[s]], axis=0)
        summed = contract(left, right, ((1,), (0,)))
        summed = jnp.where(degree >= wave_ref[s], summed, 0.0)
        out_ref[s] = summed.reshape(2, z.levels, z.degrees)


def nbytes(array, dtype=None):
    return array.size * jnp.dtype(dtype or array.dtype).itemsize


def neighbours(axis):
    count = lax.axis_size(axis)
    forward = [(i, i + 1) for i in range(count - 1)]
    return forward, [(target, source) for source, target in forward]


def on_device(spectra, legendre, derivative, tracer, limiter_flags, lat_weight, slot_wave):
    z = Sizes(spectra, legendre, tracer, lax.axis_size("wave"), lax.axis_size("lev"))
    band_index = lax.axis_index("wave")
    place = jnp.stack([band_index, lax.axis_index("lev")]).astype(jnp.int32)
    local_wave = lax.dynamic_slice_in_dim(slot_wave, band_index * z.slots, z.slots)
    f32 = jnp.float32
    fan = 4 * z.bands * z.sets * z.slot_pad * z.piece
    table_bytes = 4 * z.bands * z.slot_pad * z.lon
    edge_shape = jax.ShapeDtypeStruct((z.rows + 1, z.levels, z.lon), f32)
    pieces, to_north, to_south = pl.pallas_call(
        functools.partial(legendre_kernel, z),
        name="legendre",
        in_specs=smem(1) + vmem(8),
        out_specs=tuple(vmem(3)),
        out_shape=(
            jax.ShapeDtypeStruct((z.bands * z.sets, z.slot_pad, z.piece), jnp.bfloat16),
            edge_shape,
            edge_shape,
        ),
        compiler_params=params(2 * nbytes(spectra), 2 * nbytes(legendre), 4 * nbytes(tracer), fan),
    )(
        local_wave,
        spectra,
        legendre,
        derivative,
        *pack_constants(z),
        tracer,
        limiter_flags,
    )
    arrived = lax.all_to_all(pieces, ("wave", "lev"), split_axis=0, concat_axis=0, tiled=True)
    padded_wave = jnp.pad(
        slot_wave.reshape(z.bands, z.slots), ((0, 0), (0, z.slot_pad - z.slots))
    ).reshape(-1, 1)
    table = pl.pallas_call(
        functools.partial(table_kernel, z),
        name="table",
        in_specs=vmem(1),
        out_specs=vmem(1)[0],
        out_shape=jax.ShapeDtypeStruct((2 * z.bands * z.slot_pad, z.lon), jnp.bfloat16),
        compiler_params=params(table_bytes),
    )(padded_wave)
    forward, backward = neighbours("wave")
    from_south = lax.ppermute(to_north, "wave", forward)
    from_north = lax.ppermute(to_south, "wave", backward)
    up_shape = jax.ShapeDtypeStruct((3 * z.rows + 2, z.lon), f32)
    up, down = pl.pallas_call(
        functools.partial(edge_kernel, z),
        name="edges",
        in_specs=vmem(4),
        out_specs=tuple(vmem(2)),
        out_shape=(up_shape, up_shape),
        compiler_params=params(8 * nbytes(tracer)),
    )(tracer, limiter_flags, from_south, from_north)
    forward, backward = neighbours("lev")
    from_below = lax.ppermute(up, "lev", forward)
    from_above = lax.ppermute(down, "lev", backward)
    reply = pl.pallas_call(
        functools.partial(grid_kernel, z),
        name="grid",
        in_specs=smem(2) + vmem(11),
        out_specs=vmem(1)[0],
        out_shape=jax.ShapeDtypeStruct((z.bands, z.rows, z.reply), f32),
        scratch_shapes=[
            pltpu.VMEM((z.window, z.deep, z.lon), f32),
            pltpu.VMEM((z.rows + 2, z.deep, z.lon), f32),
        ],
        compiler_params=params(3 * table_bytes, 24 * nbytes(tracer), fan),
    )(
        place,
        lat_weight,
        arrived.reshape(z.bands, z.sets, z.slot_pad, z.piece),
        unpack_constant(z),
        table,
        tracer,
        limiter_flags,
        from_south,
        from_north,
        from_below,
        from_above,
        *reply_constants(z),
    )
    returned = lax.all_to_all(reply, "wave", split_axis=0, concat_axis=0, tiled=True)
    width = math.gcd(2 * z.lats, lanes)
    return pl.pallas_call(
        functools.partial(analysis_kernel, z),
        name="analysis",
        in_specs=smem(1) + vmem(2),
        out_specs=vmem(1)[0],
        out_shape=jax.ShapeDtypeStruct((z.slots, 2, z.levels, z.degrees), f32),
        scratch_shapes=[pltpu.VMEM((2 * z.lats // width, z.reply, width), f32)],
        compiler_params=params(nbytes(spectra, f32), nbytes(legendre)),
    )(local_wave, returned, legendre)


def solution(mesh):
    return jax.shard_map(
        on_device,
        mesh=mesh,
        in_specs=(
            P("wave", None, "lev", None),
            P("wave", None, None),
            P("wave", None, None),
            P("lev", "wave", None),
            P("lev", "wave", None),
            P("wave"),
            P(),
        ),
        out_specs=P("wave", None, "lev", None),
        check_vma=False,
    )
```

time: 72.7 us -> 53.2 us (0.73)
  the two profiles are of different devices: /device:TPU:2 before, /device:TPU:1 now
where the time goes in v2:
time: 53.2 us; the launch traced here: 52.6 us
  starting transfers between devices  17.9 us (34%)
  blocking collectives  10.4 us (20%)
  Pallas kernels  8.65 us (16%)
  local copies, waits for them, and re-layouts  8.2 us (15%)
  waiting for transfers between devices  7.25 us (14%)
    all_to_all x1, blocking collectives, on_device(): lax.all_to_all(reply, 'wave', split_axis=0, concat_axis=0, tiled=True)  10.4 us
    unnamed x32, local copies, waits for them, and re-layouts  7.23 us
    all_to_all x1, starting transfers between devices, on_device(): lax.all_to_all(pieces, ('wave', 'lev'), split_axis=0, concat_axis=0, tile...  7.09 us
    ppermute x1, starting transfers between devices, on_device(): from_below = lax.ppermute(up, 'lev', forward)  4.33 us
    ppermute x1, waiting for transfers between devices, on_device(): from_above = lax.ppermute(down, 'lev', backward)  3.75 us
    ppermute x1, waiting for transfers between devices, on_device(): from_north = lax.ppermute(to_south, 'wave', backward)  3.5 us
    ppermute x1, starting transfers between devices, on_device(): from_south = lax.ppermute(to_north, 'wave', forward)  3.26 us
    pallas_call x1, Pallas kernels, on_device(): pl.pallas_call(functools.partial(legendre_kernel, z), name='legendre', in...  3.23 us
  transfers between devices with their start and end apart: 5, of which 2 were waited for; matrix products, arithmetic and copies ran while one was open for 0% of the time, Pallas kernels for 2%

profile of v2, /device:TPU:1, one launch (start us, length us, event | category | flops | bytes accessed | tf_op | source)
XLA Modules:
  0.0 52.6 jit_solution(10470104435666394343)
XLA Ops:
  0.0 0.8 %dynamic_slice.3.wave_ref = s32[13]{0:T(128)S(1)} dynamic-slice(s32[104]{0:T(128)} %param.19, s32[]{:T(128)S(6)} %select_n.3), dynamic_slice_sizes={13} | dynamic-slice | bytes 108 | tf_op jit(solution)/shard_map/dynamic_slice | solution.py:371
  0.8 1.0 %copy-done = bf16[13,16,1280]{2,1,0:T(8,128)(2,1)S(1)} copy-done((bf16[13,16,1280]{2,1,0:T(8,128)(2,1)S(1)}, bf16[13,16,1280]{2,1,0:T(8,128)(2,1)}, u32[]{:S(2)}) %copy-start) | copy-done | bytes 532504
  1.8 0.9 %copy-done.2 = f32[4,2,2560]{2,1,0:T(2,128)S(1)} copy-done((f32[4,2,2560]{2,1,0:T(2,128)S(1)}, f32[4,2,2560]{2,1,0:T(2,128)}, u32[]{:S(2)}) %copy-start.2) | copy-done | bytes 81944
  2.7 0.9 %copy-done.4 = s32[4,2,2560]{2,1,0:T(2,128)S(1)} copy-done((s32[4,2,2560]{2,1,0:T(2,128)S(1)}, s32[4,2,2560]{2,1,0:T(2,128)}, u32[]{:S(2)}) %copy-start.4) | copy-done | bytes 81944
  3.6 1.0 %copy-done.6 = bf16[13,4,4,1280]{3,2,1,0:T(4,128)(2,1)S(1)} copy-done((bf16[13,4,4,1280]{3,2,1,0:T(4,128)(2,1)S(1)}, bf16[13,4,4,1280]{3,2,1,0:T(4,128)(2,1)}, u32[]{:S(2)}) %copy-start.6) | copy-done | bytes 532504
  4.7 1.0 %copy-done.7 = bf16[13,16,1280]{2,1,0:T(8,128)(2,1)S(1)} copy-done((bf16[13,16,1280]{2,1,0:T(8,128)(2,1)S(1)}, bf16[13,16,1280]{2,1,0:T(8,128)(2,1)}, u32[]{:S(2)}) %copy-start.7) | copy-done | bytes 532504
  5.7 0.9 %copy-done.9 = f32[208,128]{1,0:T(8,128)S(1)} copy-done((f32[208,128]{1,0:T(8,128)S(1)}, f32[208,128]{1,0:T(8,128)}, u32[]{:S(2)}) %copy-start.9) | copy-done | bytes 106520
  6.6 0.7 %copy-done.11 = s32[16,128]{1,0:T(8,128)S(1)} copy-done((s32[16,128]{1,0:T(8,128)S(1)}, s32[16,128]{1,0:T(8,128)}, u32[]{:S(2)}) %copy-start.11) | copy-done | bytes 8216
  7.3 0.7 %copy-done.12 = bf16[16,208]{1,0:T(8,128)(2,1)S(1)} copy-done((bf16[16,208]{1,0:T(8,128)(2,1)S(1)}, bf16[16,208]{1,0:T(8,128)(2,1)}, u32[]{:S(2)}) %copy-start.12) | copy-done | bytes 6680
  8.0 3.2 %legendre.1 = (bf16[32,16,128]{2,1,0:T(8,128)(2,1)}, f32[3,4,2560]{2,1,0:T(4,128)S(1)}, f32[3,4,2560]{2,1,0:T(4,128)S(1)}) custom-call(s32[13]{0:T(128)S(1)} %dynamic_slice.3.wave_ref, bf16[13,4,4,1280]{3,2,1,0:T(4,128)(2,1)S(1)} %copy-done.6, bf16[13,16,1280]{2,1,0:T(8,128)(2,1)S(1)} %copy-done, bf16[13,16,1280]{2,1,0:T(8,128)(2,1)S(1)} %copy-done.7, ...), custom_call_target="tpu_custom_call" | custom-call | tf_op jit(solution)/shard_map/legendre/pallas_call | solution.py:376
  11.2 0.0 copy-start.13
  11.3 0.0 copy-start.14
  11.3 7.1 %all-to-all-start = ((bf16[32,16,128]{2,1,0:T(8,128)(2,1)}), bf16[32,16,128]{2,1,0:T(8,128)(2,1)S(1)}, u32[]{:S(2)}, u32[]{:S(2)}) async-start(bf16[32,16,128]{2,1,0:T(8,128)(2,1)} %get-tuple-element.10), calls=%async_computation | async-start | bytes 262144 | tf_op jit(solution)/shard_map/all_to_all | solution.py:396
  18.4 3.3 %collective-permute-start = (f32[3,4,2560]{2,1,0:T(4,128)S(1)}, f32[3,4,2560]{2,1,0:T(4,128)S(1)}, u32[]{:S(2)}, u32[]{:S(2)}) collective-permute-start(f32[3,4,2560]{2,1,0:T(4,128)S(1)} %get-tuple-element.11), channel_id=1, source_target_pairs={{0,4},{4,8},{8,12},{12,16},{16,20},{20,24},{24,28},{1,5},{5,9},{9,... | collective-permute-start | bytes 368648 | tf_op jit(solution)/shard_map/ppermute | solution.py:409
  21.6 1.3 %collective-permute-start.1 = (f32[3,4,2560]{2,1,0:T(4,128)S(1)}, f32[3,4,2560]{2,1,0:T(4,128)S(1)}, u32[]{:S(2)}, u32[]{:S(2)}) collective-permute-start(f32[3,4,2560]{2,1,0:T(4,128)S(1)} %get-tuple-element.12), channel_id=1, source_target_pairs={{4,0},{8,4},{12,8},{16,12},{20,16},{24,20},{28,24},{5,1},{9,5},{13... | collective-permute-start | bytes 368648 | tf_op jit(solution)/shard_map/ppermute | solution.py:410
  22.9 0.1 reshape.10
  23.0 0.1 reshape.12.wave_ref
  23.1 1.3 %table.1.table_ref = bf16[256,2560]{1,0:T(8,128)(2,1)S(1)} custom-call(s32[128,1]{1,0:T(8,128)S(1)} %reshape.12.wave_ref), custom_call_target="tpu_custom_call" | custom-call | tf_op jit(solution)/shard_map/table/pallas_call | solution.py:400
  24.4 0.0 copy-start.1
  24.4 0.0 collective-permute-done.south_ref
  24.4 3.5 %collective-permute-done.1.north_ref = f32[3,4,2560]{2,1,0:T(4,128)S(1)} collective-permute-done((f32[3,4,2560]{2,1,0:T(4,128)S(1)}, f32[3,4,2560]{2,1,0:T(4,128)S(1)}, u32[]{:S(2)}, u32[]{:S(2)}) %collective-permute-start.1) | collective-permute-done | bytes 122912 | tf_op jit(solution)/shard_map/ppermute | solution.py:410
  27.9 0.0 copy-done.5
  28.0 4.3 %collective-permute-start.2 = (f32[8,2560]{1,0:T(8,128)S(1)}, f32[8,2560]{1,0:T(8,128)S(1)}, u32[]{:S(2)}, u32[]{:S(2)}) collective-permute-start(f32[8,2560]{1,0:T(8,128)S(1)} %get-tuple-element.13), channel_id=1, source_target_pairs={{0,1},{1,2},{2,3},{4,5},{5,6},{6,7},{8,9},{9,10},{10,11},{12,13},{... | collective-permute-start | bytes 245768 | tf_op jit(solution)/shard_map/ppermute | solution.py:421
  32.3 1.9 %collective-permute-start.3 = (f32[8,2560]{1,0:T(8,128)S(1)}, f32[8,2560]{1,0:T(8,128)S(1)}, u32[]{:S(2)}, u32[]{:S(2)}) collective-permute-start(f32[8,2560]{1,0:T(8,128)S(1)} %get-tuple-element.14), channel_id=1, source_target_pairs={{1,0},{2,1},{3,2},{5,4},{6,5},{7,6},{9,8},{10,9},{11,10},{13,12},{... | collective-permute-start | bytes 245768 | tf_op jit(solution)/shard_map/ppermute | solution.py:422
  34.2 0.1 pad_add_fusion.place_ref
  34.3 0.0 collective-permute-done.2.below_ref
  34.3 3.7 %collective-permute-done.3.above_ref = f32[8,2560]{1,0:T(8,128)S(1)} collective-permute-done((f32[8,2560]{1,0:T(8,128)S(1)}, f32[8,2560]{1,0:T(8,128)S(1)}, u32[]{:S(2)}, u32[]{:S(2)}) %collective-permute-start.3) | collective-permute-done | bytes 81952 | tf_op jit(solution)/shard_map/ppermute | solution.py:422
  38.1 0.0 all-to-all-done
  38.1 0.0 copy-done.8
  38.1 2.4 %grid.1 = f32[8,2,128]{2,1,0:T(2,128)S(1)} custom-call(s32[2]{0:T(128)S(1)} %pad_add_fusion.place_ref, f32[2]{0:T(128)S(1)} %copy-done.14, bf16[8,4,16,128]{3,2,1,0:T(8,128)(2,1)S(1)} %bitcast.3, bf16[256,384]{1,0:T(8,128)(2,1)S(1)} %copy-done.8, bf16[256,2560]{1,0:T(8,128)(2,1)S(1)} %table.1.table_ref, f32[4,2,2560]{2,1,0:T(2,128)S(1)} %copy-done.3, ...), custom_call_target="tpu_custom_call" | custom-call | tf_op jit(solution)/shard_map/grid/pallas_call | solution.py:423
  40.5 10.4 %all_to_all.10.arrived_ref = f32[8,2,128]{2,1,0:T(2,128)S(1)} all-to-all(f32[8,2,128]{2,1,0:T(2,128)S(1)} %grid.1), channel_id=1, replica_groups=mesh['wave'=8,'lev'=4] {'wave'}, dimensions={0} | all-to-all | bytes 16384 | tf_op jit(solution)/shard_map/all_to_all | solution.py:448
  50.9 1.7 %analysis.1 = f32[13,2,4,1280]{3,2,1,0:T(4,128)} custom-call(s32[13]{0:T(128)S(1)} %dynamic_slice.3.wave_ref, f32[8,2,128]{2,1,0:T(2,128)S(1)} %all_to_all.10.arrived_ref, bf16[13,16,1280]{2,1,0:T(8,128)(2,1)S(1)} %copy-done.1), custom_call_target="tpu_custom_call" | custom-call | tf_op jit(solution)/shard_map/analysis/pallas_call | solution.py:450
  (21 shorter events, 0.1 us)
Async XLA Ops:
  0.0 22.9 %copy-start.15 = (s32[104]{0:T(128)S(1)}, s32[104]{0:T(128)}, u32[]{:S(2)}) copy-start(s32[104]{0:T(128)} %param.19) | copy-start | bytes 1252
  0.8 1.0 %copy-start = (bf16[13,16,1280]{2,1,0:T(8,128)(2,1)S(1)}, bf16[13,16,1280]{2,1,0:T(8,128)(2,1)}, u32[]{:S(2)}) copy-start(bf16[13,16,1280]{2,1,0:T(8,128)(2,1)} %legendre_ref.3) | copy-start | bytes 1597444
  1.8 0.9 %copy-start.2 = (f32[4,2,2560]{2,1,0:T(2,128)S(1)}, f32[4,2,2560]{2,1,0:T(2,128)}, u32[]{:S(2)}) copy-start(f32[4,2,2560]{2,1,0:T(2,128)} %tracer_ref.5) | copy-start | bytes 245764
  2.7 0.9 %copy-start.4 = (s32[4,2,2560]{2,1,0:T(2,128)S(1)}, s32[4,2,2560]{2,1,0:T(2,128)}, u32[]{:S(2)}) copy-start(s32[4,2,2560]{2,1,0:T(2,128)} %flags_ref.5) | copy-start | bytes 245764
  3.6 1.0 %copy-start.6 = (bf16[13,4,4,1280]{3,2,1,0:T(4,128)(2,1)S(1)}, bf16[13,4,4,1280]{3,2,1,0:T(4,128)(2,1)}, u32[]{:S(2)}) copy-start(bf16[13,4,4,1280]{3,2,1,0:T(4,128)(2,1)} %spectra_ref.1) | copy-start | bytes 1597444
  4.7 1.0 %copy-start.7 = (bf16[13,16,1280]{2,1,0:T(8,128)(2,1)S(1)}, bf16[13,16,1280]{2,1,0:T(8,128)(2,1)}, u32[]{:S(2)}) copy-start(bf16[13,16,1280]{2,1,0:T(8,128)(2,1)} %derivative_ref.1) | copy-start | bytes 1597444
  5.7 0.9 %copy-start.9 = (f32[208,128]{1,0:T(8,128)S(1)}, f32[208,128]{1,0:T(8,128)}, u32[]{:S(2)}) copy-start(f32[208,128]{1,0:T(8,128)} %constant.28.clone.pick_ref) | copy-start | bytes 319492
  6.6 0.7 %copy-start.11 = (s32[16,128]{1,0:T(8,128)S(1)}, s32[16,128]{1,0:T(8,128)}, u32[]{:S(2)}) copy-start(s32[16,128]{1,0:T(8,128)} %constant.29.clone.offset_ref) | copy-start | bytes 24580
  7.3 0.7 %copy-start.12 = (bf16[16,208]{1,0:T(8,128)(2,1)S(1)}, bf16[16,208]{1,0:T(8,128)(2,1)}, u32[]{:S(2)}) copy-start(bf16[16,208]{1,0:T(8,128)(2,1)} %constant.27.clone.gather_ref) | copy-start | bytes 19972
  11.2 16.7 %copy-start.3 = (f32[4,2,2560]{2,1,0:T(2,128)S(1)}, f32[4,2,2560]{2,1,0:T(2,128)}, u32[]{:S(2)}) copy-start(f32[4,2,2560]{2,1,0:T(2,128)} %tracer_ref.5) | copy-start | bytes 245764
  11.2 16.7 %copy-start.5 = (s32[4,2,2560]{2,1,0:T(2,128)S(1)}, s32[4,2,2560]{2,1,0:T(2,128)}, u32[]{:S(2)}) copy-start(s32[4,2,2560]{2,1,0:T(2,128)} %flags_ref.5) | copy-start | bytes 245764
  11.2 26.8 %copy-start.8 = (bf16[256,384]{1,0:T(8,128)(2,1)S(1)}, bf16[256,384]{1,0:T(8,128)(2,1)}, u32[]{:S(2)}) copy-start(bf16[256,384]{1,0:T(8,128)(2,1)} %constant.30.clone.unpack_ref) | copy-start | bytes 589828
  11.2 26.8 %copy-start.10 = (bf16[32,128]{1,0:T(8,128)(2,1)S(1)}, bf16[32,128]{1,0:T(8,128)(2,1)}, u32[]{:S(2)}) copy-start(bf16[32,128]{1,0:T(8,128)(2,1)} %constant.31.clone.spread_ref) | copy-start | bytes 24580
  11.2 26.8 %copy-start.13 = (f32[8,128]{1,0:T(8,128)S(1)}, f32[8,128]{1,0:T(8,128)}, u32[]{:S(2)}) copy-start(f32[8,128]{1,0:T(8,128)} %constant.32.clone.pick_ref) | copy-start | bytes 12292
  11.3 26.8 %copy-start.14 = (f32[2]{0:T(128)S(1)}, f32[2]{0:T(128)}, u32[]{:S(2)}) copy-start(f32[2]{0:T(128)} %weight_ref.1) | copy-start | bytes 28
  11.3 26.8 %all-to-all-start = ((bf16[32,16,128]{2,1,0:T(8,128)(2,1)}), bf16[32,16,128]{2,1,0:T(8,128)(2,1)S(1)}, u32[]{:S(2)}, u32[]{:S(2)}) async-start(bf16[32,16,128]{2,1,0:T(8,128)(2,1)} %get-tuple-element.10), calls=%async_computation | async-start | bytes 262144 | tf_op jit(solution)/shard_map/all_to_all | solution.py:396
  18.4 6.0 %collective-permute-start = (f32[3,4,2560]{2,1,0:T(4,128)S(1)}, f32[3,4,2560]{2,1,0:T(4,128)S(1)}, u32[]{:S(2)}, u32[]{:S(2)}) collective-permute-start(f32[3,4,2560]{2,1,0:T(4,128)S(1)} %get-tuple-element.11), channel_id=1, source_target_pairs={{0,4},{4,8},{8,12},{12,16},{16,20},{20,24},{24,28},{1,5},{5,9},{9,... | collective-permute-start | bytes 368648 | tf_op jit(solution)/shard_map/ppermute | solution.py:409
  21.6 6.3 %collective-permute-start.1 = (f32[3,4,2560]{2,1,0:T(4,128)S(1)}, f32[3,4,2560]{2,1,0:T(4,128)S(1)}, u32[]{:S(2)}, u32[]{:S(2)}) collective-permute-start(f32[3,4,2560]{2,1,0:T(4,128)S(1)} %get-tuple-element.12), channel_id=1, source_target_pairs={{4,0},{8,4},{12,8},{16,12},{20,16},{24,20},{28,24},{5,1},{9,5},{13... | collective-permute-start | bytes 368648 | tf_op jit(solution)/shard_map/ppermute | solution.py:410
  24.4 26.5 %copy-start.1 = (bf16[13,16,1280]{2,1,0:T(8,128)(2,1)S(1)}, bf16[13,16,1280]{2,1,0:T(8,128)(2,1)}, u32[]{:S(2)}) copy-start(bf16[13,16,1280]{2,1,0:T(8,128)(2,1)} %legendre_ref.3) | copy-start | bytes 1597444
  28.0 6.4 %collective-permute-start.2 = (f32[8,2560]{1,0:T(8,128)S(1)}, f32[8,2560]{1,0:T(8,128)S(1)}, u32[]{:S(2)}, u32[]{:S(2)}) collective-permute-start(f32[8,2560]{1,0:T(8,128)S(1)} %get-tuple-element.13), channel_id=1, source_target_pairs={{0,1},{1,2},{2,3},{4,5},{5,6},{6,7},{8,9},{9,10},{10,11},{12,13},{... | collective-permute-start | bytes 245768 | tf_op jit(solution)/shard_map/ppermute | solution.py:421
  32.3 5.8 %collective-permute-start.3 = (f32[8,2560]{1,0:T(8,128)S(1)}, f32[8,2560]{1,0:T(8,128)S(1)}, u32[]{:S(2)}, u32[]{:S(2)}) collective-permute-start(f32[8,2560]{1,0:T(8,128)S(1)} %get-tuple-element.14), channel_id=1, source_target_pairs={{1,0},{2,1},{3,2},{5,4},{6,5},{7,6},{9,8},{10,9},{11,10},{13,12},{... | collective-permute-start | bytes 245768 | tf_op jit(solution)/shard_map/ppermute | solution.py:422

commit v3 on v2

--- a/solution.py
+++ b/solution.py
@@ -14,6 +14,7 @@
 halo = 2
 lanes = 128
 packed_rows = 16
+group_slots = 8
 
 
 def round_up(value, step):
@@ -26,10 +27,6 @@
 
 def vmem(count):
     return [pl.BlockSpec(memory_space=pltpu.VMEM)] * count
-
-
-def smem(count):
-    return [pl.BlockSpec(memory_space=pltpu.SMEM)] * count
 
 
 def params(*byte_counts):
@@ -100,40 +97,121 @@
     return jnp.asarray(spread, jnp.bfloat16), pick.astype(np.float32)
 
 
+def pack_kernel(z, tracer_hbm, flags_hbm, own_ref, first_ref, second_ref, tracer_ref, flags_ref, sems):
+    copies = [
+        pltpu.make_async_copy(tracer_hbm, tracer_ref, sems.at[0]),
+        pltpu.make_async_copy(flags_hbm, flags_ref, sems.at[1]),
+    ]
+    for copy in copies:
+        copy.start()
+    even = lax.axis_index("wave") % 2 == 0
+    copies[0].wait()
+    for j in range(z.rows):
+        row = tracer_ref[:, j, :]
+        own_ref[j] = row
+        first_ref[j] = row
+        second_ref[j] = row
+    copies[1].wait()
+    switched = [flags_ref[:, j, :].astype(jnp.float32) for j in range(z.rows)]
+    for j in range(z.rows):
+        own_ref[z.rows + j] = switched[j]
+    first_ref[z.rows] = jnp.where(even, switched[-1], switched[0])
+    second_ref[z.rows] = jnp.where(even, switched[0], switched[-1])
+
+
 def legendre_kernel(
     z,
+    wave_hbm,
+    weight_hbm,
+    spectra_hbm,
+    legendre_hbm,
+    derivative_hbm,
+    pick_hbm,
+    gather_hbm,
+    offset_hbm,
+    pieces_ref,
+    live_ref,
+    scale_ref,
     wave_ref,
+    weight_ref,
     spectra_ref,
     legendre_ref,
     derivative_ref,
     pick_ref,
     gather_ref,
     offset_ref,
-    tracer_ref,
-    flags_ref,
-    pieces_ref,
-    north_ref,
-    south_ref,
+    sems,
 ):
+    groups = [
+        (first, min(first + group_slots, z.slots)) for first in range(0, z.slots, group_slots)
+    ]
+    fetches = []
+    for g, (first, last) in enumerate(groups):
+        part = pl.ds(first, last - first)
+        fetches.append(
+            [
+                pltpu.make_async_copy(hbm.at[part], ref.at[part], sems.at[a, g])
+                for a, (hbm, ref) in enumerate(
+                    (
+                        (spectra_hbm, spectra_ref),
+                        (legendre_hbm, legendre_ref),
+                        (derivative_hbm, derivative_ref),
+                    )
+                )
+            ]
+        )
+    constants = [
+        pltpu.make_async_copy(hbm, ref, sems.at[3 + a, 0])
+        for a, (hbm, ref) in enumerate(
+            ((pick_hbm, pick_ref), (gather_hbm, gather_ref), (offset_hbm, offset_ref))
+        )
+    ]
+    scalars = [
+        pltpu.make_async_copy(hbm, ref, sems.at[6 + a, 0])
+        for a, (hbm, ref) in enumerate(((wave_hbm, wave_ref), (weight_hbm, weight_ref)))
+    ]
+    for copies in [scalars] + fetches:
+        for copy in copies:
+            copy.start()
+    for copy in constants:
+        copy.start()
+    base = lax.axis_index("wave") * z.slots
+    for copy in scalars:
+        copy.wait()
+    for j in range(z.rows):
+        scale = weight_ref[j] * (1.0 / math.sqrt(z.lon))
+        scale_ref[j * z.deep : (j + 1) * z.deep] = jnp.full((z.deep, lanes), scale, jnp.float32)
     height = 4 * z.levels
-    degree = lax.broadcasted_iota(jnp.int32, (height, z.degrees), 1)
+    degree = lax.broadcasted_iota(jnp.int32, (z.lats, z.degrees), 1)
     channel = lax.broadcasted_iota(jnp.int32, (height, z.lats), 0) // z.levels
     sign_sum = jnp.where(channel % 2 == 0, -1.0, 1.0)
     sign_slope = jnp.where(channel < 2, -1.0, 1.0)
     winds = []
-    for s in range(z.slots):
-        wave = wave_ref[s]
-        coefficients = spectra_ref[s].reshape(height, z.degrees)
-        coefficients = coefficients * jnp.where(degree >= wave, 1.0, 0.0).astype(jnp.bfloat16)
-        sums = contract(coefficients, legendre_ref[s], ((1,), (1,)))
-        slopes = contract(coefficients, derivative_ref[s], ((1,), (1,)))
-        turned = jnp.concatenate(
-            [sums[c * z.levels : (c + 1) * z.levels] for c in (3, 2, 1, 0)], axis=0
-        )
-        scaled = wave.astype(jnp.float32) / z.degrees
-        doubled = jnp.where(wave == 0, 1.0, 2.0)
-        winds.append((scaled * sign_sum * turned + sign_slope * slopes) * doubled)
+    for (first, last), copies in zip(groups, fetches):
+        waves = [wave_ref[base + s] for s in range(first, last)]
+        for copy in copies:
+            copy.wait()
+        right = []
+        for s, wave in zip(range(first, last), waves):
+            live = jnp.where(degree >= wave, 1.0, 0.0).astype(jnp.bfloat16)
+            masked = legendre_ref[s] * live
+            live_ref[s] = masked
+            right += [masked, derivative_ref[s] * live]
+        left = [spectra_ref[s].reshape(height, z.degrees) for s in range(first, last)]
+        sums = contract(jnp.concatenate(left, axis=0), jnp.concatenate(right, axis=0), ((1,), (1,)))
+        for at, wave in enumerate(waves):
+            mine = sums[at * height : (at + 1) * height]
+            sums_at = mine[:, 2 * at * z.lats : (2 * at + 1) * z.lats]
+            slopes = mine[:, (2 * at + 1) * z.lats : (2 * at + 2) * z.lats]
+            turned = jnp.concatenate(
+                [sums_at[c * z.levels : (c + 1) * z.levels] for c in (3, 2, 1, 0)], axis=0
+            )
+            scaled = wave.astype(jnp.float32) / z.degrees
+            doubled = jnp.where(wave == 0, 1.0, 2.0)
+            winds.append((scaled * sign_sum * turned + sign_slope * slopes) * doubled)
     winds = jnp.concatenate(winds, axis=0).astype(jnp.bfloat16)
+    for copy in constants:
+        copy.wait()
 
     def one_band(b, carry):
         choose = jnp.where(offset_ref[...] + b * z.rows == 0, 1.0, 0.0).astype(jnp.bfloat16)
@@ -150,13 +228,6 @@
     else:
         lax.fori_loop(0, z.bands, one_band, 0)
 
-    for j in range(z.rows):
-        row = tracer_ref[:, j, :]
-        north_ref[j] = row
-        south_ref[j] = row
-    north_ref[z.rows] = flags_ref[:, z.rows - 1, :].astype(jnp.float32)
-    south_ref[z.rows] = flags_ref[:, 0, :].astype(jnp.float32)
-
 
 def table_kernel(z, wave_ref, table_ref):
     wave = wave_ref[...].astype(jnp.float32)
@@ -179,59 +250,67 @@
         table_ref[height:, columns] = (-(sin_a * fine_cos + cos_a * fine_sin)).astype(jnp.bfloat16)
 
 
-def edge_kernel(z, tracer_ref, flags_ref, south_ref, north_ref, up_ref, down_ref):
-    for out_ref, near, far in (
-        (up_ref, z.levels - 1, z.levels - 2),
-        (down_ref, 0, 1),
-    ):
-        out_ref[0:1] = south_ref[z.rows - 1, near : near + 1]
-        out_ref[1 : 1 + z.rows] = tracer_ref[near]
-        out_ref[1 + z.rows : 2 + z.rows] = north_ref[0, near : near + 1]
-        out_ref[2 + z.rows : 2 + 2 * z.rows] = tracer_ref[far]
-        out_ref[2 + 2 * z.rows : 2 + 3 * z.rows] = flags_ref[near].astype(jnp.float32)
+def by_parity(axis, first, second):
+    even = lax.axis_index(axis) % 2 == 0
+    return jnp.where(even, second, first), jnp.where(even, first, second)
+
+
+def edge_kernel(z, own_ref, first_ref, second_ref, up_ref, down_ref):
+    south, _ = by_parity("wave", first_ref[z.rows - 1], second_ref[z.rows - 1])
+    _, north = by_parity("wave", first_ref[0], second_ref[0])
+    even = lax.axis_index("lev") % 2 == 0
+    rows = [south] + [own_ref[j] for j in range(z.rows)] + [north]
+    plan = [(row, z.levels - 1, 0) for row in rows]
+    plan += [(row, z.levels - 2, 1) for row in rows[1:-1]]
+    plan += [(own_ref[z.rows + j], z.levels - 1, 0) for j in range(z.rows)]
+    for at, (row, top, bottom) in enumerate(plan):
+        top, bottom = row[top : top + 1], row[bottom : bottom + 1]
+        up_ref[at : at + 1] = jnp.where(even, top, bottom)
+        down_ref[at : at + 1] = jnp.where(even, bottom, top)
 
 
 def grid_kernel(
     z,
-    place_ref,
-    weight_ref,
     arrived_ref,
     unpack_ref,
     table_ref,
-    tracer_ref,
-    flags_ref,
-    south_ref,
-    north_ref,
-    below_ref,
-    above_ref,
+    own_ref,
+    first_ref,
+    second_ref,
+    lev_first_ref,
+    lev_second_ref,
     spread_ref,
     pick_ref,
+    scale_ref,
     reply_ref,
     q_ref,
     f_ref,
 ):
-    band, level_set = place_ref[0], place_ref[1]
+    band, level_set = lax.axis_index("wave"), lax.axis_index("lev")
     lat_total = z.bands * z.rows
     lev_total = z.sets * z.levels
     own = slice(halo, halo + z.levels)
     q_ref[...] = jnp.zeros_like(q_ref)
     f_ref[...] = jnp.zeros_like(f_ref)
     for j in range(halo):
-        q_ref[j, own] = south_ref[z.rows - halo + j]
-        q_ref[halo + z.rows + j, own] = north_ref[j]
-    f_ref[0, own] = south_ref[z.rows]
-    f_ref[z.rows + 1, own] = north_ref[z.rows]
+        south, north = by_parity("wave", first_ref[j], second_ref[j])
+        q_ref[j, own] = south
+        q_ref[halo + z.rows + j, own] = north
+    south, north = by_parity("wave", first_ref[z.rows], second_ref[z.rows])
+    f_ref[0, own] = south
+    f_ref[z.rows + 1, own] = north
     for j in range(z.rows):
-        q_ref[halo + j, own] = tracer_ref[:, j, :]
-        f_ref[1 + j, own] = flags_ref[:, j, :].astype(jnp.float32)
-    for got_ref, near, far in ((below_ref, halo - 1, 0), (above_ref, halo + z.levels, z.deep - 1)):
+        q_ref[halo + j, own] = own_ref[j]
+        f_ref[1 + j, own] = own_ref[z.rows + j]
+    below, above = by_parity("lev", lev_first_ref[...], lev_second_ref[...])
+    for got, near, far in ((below, halo - 1, 0), (above, halo + z.levels, z.deep - 1)):
         for j in range(z.rows + 2):
-            q_ref[halo - 1 + j, near : near + 1] = got_ref[j : j + 1]
+            q_ref[halo - 1 + j, near : near + 1] = got[j : j + 1]
         for j in range(z.rows):
             at = z.rows + 2 + j
-            q_ref[halo + j, far : far + 1] = got_ref[at : at + 1]
+            q_ref[halo + j, far : far + 1] = got[at : at + 1]
             at = 2 * z.rows + 2 + j
-            f_ref[1 + j, near : near + 1] = got_ref[at : at + 1]
+            f_ref[1 + j, near : near + 1] = got[at : at + 1]
 
     height = z.bands * z.slot_pad
 
@@ -313,11 +392,7 @@
     projected = contract(both, table_ref[...], ((1,), (1,)))
     count = z.rows * z.deep
     projected = projected[:count] + projected[count:]
-    scaled = []
-    for j in range(z.rows):
-        scale = weight_ref[j] * (1.0 / math.sqrt(z.lon))
-        scaled.append(projected[j * z.deep : (j + 1) * z.deep] * scale)
-    scaled = jnp.concatenate(scaled, axis=0)
+    scaled = projected * scale_ref[:, :1]
     top = scaled.astype(jnp.bfloat16)
     low = (scaled - top.astype(jnp.float32)).astype(jnp.bfloat16)
     both = jnp.concatenate([top, low], axis=0)
@@ -333,7 +408,7 @@
             reply_ref[b, j : j + 1] = jnp.sum(mine, axis=0, keepdims=True)
 
 
-def analysis_kernel(z, wave_ref, arrived_ref, legendre_ref, out_ref, turned_ref):
+def analysis_kernel(z, arrived_ref, live_ref, out_ref, turned_ref):
     arrived = arrived_ref[...].reshape(z.lats, z.reply)
     top = arrived.astype(jnp.bfloat16).astype(jnp.float32)
     turned = jnp.concatenate([top, arrived - top], axis=0)
@@ -341,58 +416,74 @@
     for c in range(turned_ref.shape[0]):
         turned_ref[c] = turned[c * width : (c + 1) * width].T
     height = 2 * z.levels
-    degree = lax.broadcasted_iota(jnp.int32, (height, z.degrees), 1)
     for s in range(z.slots):
         left = [
             turned_ref[c, pl.ds(s, height, stride=z.slot_pad), :].astype(jnp.bfloat16)
             for c in range(turned_ref.shape[0])
         ]
         left = jnp.concatenate(left, axis=1)
-        right = jnp.concatenate([legendre_ref[s], legendre_ref[s]], axis=0)
-        summed = contract(left, right, ((1,), (0,)))
-        summed = jnp.where(degree >= wave_ref[s], summed, 0.0)
-        out_ref[s] = summed.reshape(2, z.levels, z.degrees)
+        right = jnp.concatenate([live_ref[s], live_ref[s]], axis=0)
+        out_ref[s] = contract(left, right, ((1,), (0,))).reshape(2, z.levels, z.degrees)
+
+
+def in_hbm(array):
+    return pltpu.with_memory_space_constraint(array, pltpu.HBM)
 
 
 def nbytes(array, dtype=None):
     return array.size * jnp.dtype(dtype or array.dtype).itemsize
 
 
-def neighbours(axis):
+def swaps(axis):
     count = lax.axis_size(axis)
-    forward = [(i, i + 1) for i in range(count - 1)]
-    return forward, [(target, source) for source, target in forward]
+    pairs = [[(i, i + 1) for i in range(start, count - 1, 2)] for start in (0, 1)]
+    return [p + [(b, a) for a, b in p] for p in pairs]
 
 
 def on_device(spectra, legendre, derivative, tracer, limiter_flags, lat_weight, slot_wave):
     z = Sizes(spectra, legendre, tracer, lax.axis_size("wave"), lax.axis_size("lev"))
-    band_index = lax.axis_index("wave")
-    place = jnp.stack([band_index, lax.axis_index("lev")]).astype(jnp.int32)
-    local_wave = lax.dynamic_slice_in_dim(slot_wave, band_index * z.slots, z.slots)
-    f32 = jnp.float32
+    f32, bf16 = jnp.float32, jnp.bfloat16
     fan = 4 * z.bands * z.sets * z.slot_pad * z.piece
     table_bytes = 4 * z.bands * z.slot_pad * z.lon
+    any_spec = pl.BlockSpec(memory_space=pltpu.HBM)
     edge_shape = jax.ShapeDtypeStruct((z.rows + 1, z.levels, z.lon), f32)
-    pieces, to_north, to_south = pl.pallas_call(
-        functools.partial(legendre_kernel, z),
-        name="legendre",
-        in_specs=smem(1) + vmem(8),
+    own, to_first, to_second = pl.pallas_call(
+        functools.partial(pack_kernel, z),
+        name="pack",
+        in_specs=[any_spec] * 2,
         out_specs=tuple(vmem(3)),
         out_shape=(
-            jax.ShapeDtypeStruct((z.bands * z.sets, z.slot_pad, z.piece), jnp.bfloat16),
+            jax.ShapeDtypeStruct((2 * z.rows, z.levels, z.lon), f32),
             edge_shape,
             edge_shape,
         ),
-        compiler_params=params(2 * nbytes(spectra), 2 * nbytes(legendre), 4 * nbytes(tracer), fan),
-    )(
-        local_wave,
-        spectra,
-        legendre,
-        derivative,
-        *pack_constants(z),
-        tracer,
-        limiter_flags,
-    )
+        scratch_shapes=[
+            pltpu.VMEM(tracer.shape, tracer.dtype),
+            pltpu.VMEM(tracer.shape, limiter_flags.dtype),
+            pltpu.SemaphoreType.DMA((2,)),
+        ],
+        compiler_params=params(8 * nbytes(tracer)),
+    )(in_hbm(tracer), in_hbm(limiter_flags))
+    first_pairs, second_pairs = swaps("wave")
+    wave_first = lax.ppermute(to_first, "wave", first_pairs)
+    wave_second = lax.ppermute(to_second, "wave", second_pairs)
+    constants = pack_constants(z)
+    group_count = -(-z.slots // group_slots)
+    pieces, live, scale = pl.pallas_call(
+        functools.partial(legendre_kernel, z),
+        name="legendre",
+        in_specs=[any_spec] * 8,
+        out_specs=tuple(vmem(3)),
+        out_shape=(
+            jax.ShapeDtypeStruct((z.bands * z.sets, z.slot_pad, z.piece), bf16),
+            jax.ShapeDtypeStruct(legendre.shape, bf16),
+            jax.ShapeDtypeStruct((z.rows * z.deep, lanes), f32),
+        ),
+        scratch_shapes=[pltpu.SMEM(x.shape, x.dtype) for x in (slot_wave, lat_weight)]
+        + [pltpu.VMEM(x.shape, x.dtype) for x in (spectra, legendre, derivative, *constants)]
+        + [pltpu.SemaphoreType.DMA((8, group_count))],
+        compiler_params=params(2 * nbytes(spectra), 4 * nbytes(legendre), fan),
+    )(*map(in_hbm, (slot_wave, lat_weight, spectra, legendre, derivative, *constants)))
     arrived = lax.all_to_all(pieces, ("wave", "lev"), split_axis=0, concat_axis=0, tiled=True)
     padded_wave = jnp.pad(
         slot_wave.reshape(z.bands, z.slots), ((0, 0), (0, z.slot_pad - z.slots))
@@ -402,28 +493,25 @@
         name="table",
         in_specs=vmem(1),
         out_specs=vmem(1)[0],
-        out_shape=jax.ShapeDtypeStruct((2 * z.bands * z.slot_pad, z.lon), jnp.bfloat16),
+        out_shape=jax.ShapeDtypeStruct((2 * z.bands * z.slot_pad, z.lon), bf16),
         compiler_params=params(table_bytes),
     )(padded_wave)
-    forward, backward = neighbours("wave")
-    from_south = lax.ppermute(to_north, "wave", forward)
-    from_north = lax.ppermute(to_south, "wave", backward)
     up_shape = jax.ShapeDtypeStruct((3 * z.rows + 2, z.lon), f32)
     up, down = pl.pallas_call(
         functools.partial(edge_kernel, z),
         name="edges",
-        in_specs=vmem(4),
+        in_specs=vmem(3),
         out_specs=tuple(vmem(2)),
         out_shape=(up_shape, up_shape),
         compiler_params=params(8 * nbytes(tracer)),
-    )(tracer, limiter_flags, from_south, from_north)
-    forward, backward = neighbours("lev")
-    from_below = lax.ppermute(up, "lev", forward)
-    from_above = lax.ppermute(down, "lev", backward)
+    )(own, wave_first, wave_second)
+    first_pairs, second_pairs = swaps("lev")
+    lev_first = lax.ppermute(up, "lev", first_pairs)
+    lev_second = lax.ppermute(down, "lev", second_pairs)
     reply = pl.pallas_call(
         functools.partial(grid_kernel, z),
         name="grid",
-        in_specs=smem(2) + vmem(11),
+        in_specs=vmem(11),
         out_specs=vmem(1)[0],
         out_shape=jax.ShapeDtypeStruct((z.bands, z.rows, z.reply), f32),
         scratch_shapes=[
@@ -432,30 +520,28 @@
         ],
         compiler_params=params(3 * table_bytes, 24 * nbytes(tracer), fan),
     )(
-        place,
-        lat_weight,
         arrived.reshape(z.bands, z.sets, z.slot_pad, z.piece),
         unpack_constant(z),
         table,
-        tracer,
-        limiter_flags,
-        from_south,
-        from_north,
-        from_below,
-        from_above,
+        own,
+        wave_first,
+        wave_second,
+        lev_first,
+        lev_second,
         *reply_constants(z),
+        scale,
     )
     returned = lax.all_to_all(reply, "wave", split_axis=0, concat_axis=0, tiled=True)
     width = math.gcd(2 * z.lats, lanes)
     return pl.pallas_call(
         functools.partial(analysis_kernel, z),
         name="analysis",
-        in_specs=smem(1) + vmem(2),
+        in_specs=vmem(2),
         out_specs=vmem(1)[0],
         out_shape=jax.ShapeDtypeStruct((z.slots, 2, z.levels, z.degrees), f32),
         scratch_shapes=[pltpu.VMEM((2 * z.lats // width, z.reply, width), f32)],
         compiler_params=params(nbytes(spectra, f32), nbytes(legendre)),
-    )(local_wave, returned, legendre)
+    )(returned, live)
 
 
 def solution(mesh):

time: 53.2 us -> 41.4 us (0.78)
  the two profiles are of different devices: /device:TPU:1 before, /device:TPU:2 now
where the time goes in v3:
time: 41.4 us; the launch traced here: 41.1 us
  blocking collectives  13.6 us (33%)
  starting transfers between devices  12.4 us (30%)
  Pallas kernels  9.93 us (24%)
  waiting for transfers between devices  4.76 us (11%)
    all_to_all x1, blocking collectives, on_device(): lax.all_to_all(reply, 'wave', split_axis=0, concat_axis=0, tiled=True)  13.6 us
    all_to_all x1, starting transfers between devices, on_device(): lax.all_to_all(pieces, ('wave', 'lev'), split_axis=0, concat_axis=0, tile...  6.13 us
    pallas_call x1, Pallas kernels, on_device(): pl.pallas_call(functools.partial(legendre_kernel, z), name='legendre', in...  4.56 us
    ppermute x1, waiting for transfers between devices, on_device(): wave_first = lax.ppermute(to_first, 'wave', first_pairs)  4.11 us
    ppermute x1, starting transfers between devices, on_device(): lev_second = lax.ppermute(down, 'lev', second_pairs)  4.06 us
    pallas_call x1, Pallas kernels, on_device(): pl.pallas_call(functools.partial(grid_kernel, z), name='grid', in_specs=v...  1.83 us
    ppermute x1, starting transfers between devices, on_device(): wave_first = lax.ppermute(to_first, 'wave', first_pairs)  1.53 us
    pallas_call x1, Pallas kernels, on_device(): pl.pallas_call(functools.partial(table_kernel, z), name='table', in_specs...  1.26 us
  transfers between devices with their start and end apart: 5, of which 2 were waited for; matrix products, arithmetic and copies ran while one was open for 0% of the time, Pallas kernels for 6%

profile of v3, /device:TPU:2, one launch (start us, length us, event | category | flops | bytes accessed | tf_op | source)
XLA Modules:
  0.0 41.1 jit_solution(17672204289503678829)
XLA Ops:
  0.0 0.0 copy-start.3
  0.0 4.6 %legendre.1 = (bf16[32,16,128]{2,1,0:T(8,128)(2,1)}, bf16[13,16,1280]{2,1,0:T(8,128)(2,1)S(1)}, f32[16,128]{1,0:T(8,128)S(1)}) custom-call(s32[104]{0:T(128)} %wave_hbm.1, f32[2]{0:T(128)} %weight_hbm.1, bf16[13,4,4,1280]{3,2,1,0:T(4,128)(2,1)} %spectra_hbm.1, bf16[13,16,1280]{2,1,0:T(8,128)(2,1)} %legendre_hbm.1, bf16[13,16,1280]{2,1,0:T(8,128)(2,1)} %derivative_hbm.1, ...), custom_call_target="tpu_custom_call" | custom-call | tf_op jit(solution)/shard_map/legendre/pallas_call | solution.py:472
  4.6 0.0 copy-start
  4.6 0.0 copy-start.1
  4.6 0.0 copy-start.2
  4.6 6.1 %all-to-all-start = ((bf16[32,16,128]{2,1,0:T(8,128)(2,1)}), bf16[32,16,128]{2,1,0:T(8,128)(2,1)S(1)}, u32[]{:S(2)}, u32[]{:S(2)}) async-start(bf16[32,16,128]{2,1,0:T(8,128)(2,1)} %get-tuple-element.13), calls=%async_computation | async-start | bytes 262144 | tf_op jit(solution)/shard_map/all_to_all | solution.py:487
  10.8 1.0 %pack.1 = (f32[4,4,2560]{2,1,0:T(4,128)S(1)}, f32[3,4,2560]{2,1,0:T(4,128)S(1)}, f32[3,4,2560]{2,1,0:T(4,128)S(1)}) custom-call(f32[4,2,2560]{2,1,0:T(2,128)} %tracer_hbm.1, s32[4,2,2560]{2,1,0:T(2,128)} %flags_hbm.1), custom_call_target="tpu_custom_call" | custom-call | tf_op jit(solution)/shard_map/pack/pallas_call | solution.py:450
  11.7 1.5 %collective-permute-start = (f32[3,4,2560]{2,1,0:T(4,128)S(1)}, f32[3,4,2560]{2,1,0:T(4,128)S(1)}, u32[]{:S(2)}, u32[]{:S(2)}) collective-permute-start(f32[3,4,2560]{2,1,0:T(4,128)S(1)} %get-tuple-element.15), channel_id=1, source_target_pairs={{0,4},{8,12},{16,20},{24,28},{4,0},{12,8},{20,16},{28,24},{1,5},{9... | collective-permute-start | bytes 368648 | tf_op jit(solution)/shard_map/ppermute | solution.py:468
  13.3 0.7 %collective-permute-start.1 = (f32[3,4,2560]{2,1,0:T(4,128)S(1)}, f32[3,4,2560]{2,1,0:T(4,128)S(1)}, u32[]{:S(2)}, u32[]{:S(2)}) collective-permute-start(f32[3,4,2560]{2,1,0:T(4,128)S(1)} %get-tuple-element.16), channel_id=1, source_target_pairs={{4,8},{12,16},{20,24},{8,4},{16,12},{24,20},{5,9},{13,17},{21,25},... | collective-permute-start | bytes 368648 | tf_op jit(solution)/shard_map/ppermute | solution.py:469
  13.9 4.1 %collective-permute-done.first_ref = f32[3,4,2560]{2,1,0:T(4,128)S(1)} collective-permute-done((f32[3,4,2560]{2,1,0:T(4,128)S(1)}, f32[3,4,2560]{2,1,0:T(4,128)S(1)}, u32[]{:S(2)}, u32[]{:S(2)}) %collective-permute-start) | collective-permute-done | bytes 122912 | tf_op jit(solution)/shard_map/ppermute | solution.py:468
  18.0 0.0 collective-permute-done.1.second_ref
  18.0 0.1 edges.1
  18.2 0.1 collective-permute-start.2
  18.2 4.1 %collective-permute-start.3 = (f32[8,2560]{1,0:T(8,128)S(1)}, f32[8,2560]{1,0:T(8,128)S(1)}, u32[]{:S(2)}, u32[]{:S(2)}) collective-permute-start(f32[8,2560]{1,0:T(8,128)S(1)} %get-tuple-element.18), channel_id=1, source_target_pairs={{1,2},{2,1},{5,6},{6,5},{9,10},{10,9},{13,14},{14,13},{17,18},{18,... | collective-permute-start | bytes 245768 | tf_op jit(solution)/shard_map/ppermute | solution.py:510
  22.3 0.0 copy-done.3
  22.3 0.1 reshape.10
  22.4 0.1 reshape.12.wave_ref
  22.5 1.3 %table.1.table_ref = bf16[256,2560]{1,0:T(8,128)(2,1)S(1)} custom-call(s32[128,1]{1,0:T(8,128)S(1)} %reshape.12.wave_ref), custom_call_target="tpu_custom_call" | custom-call | tf_op jit(solution)/shard_map/table/pallas_call | solution.py:491
  23.8 0.0 collective-permute-done.2.lev_first_ref
  23.8 0.6 %collective-permute-done.3.lev_second_ref = f32[8,2560]{1,0:T(8,128)S(1)} collective-permute-done((f32[8,2560]{1,0:T(8,128)S(1)}, f32[8,2560]{1,0:T(8,128)S(1)}, u32[]{:S(2)}, u32[]{:S(2)}) %collective-permute-start.3) | collective-permute-done | bytes 81952 | tf_op jit(solution)/shard_map/ppermute | solution.py:510
  24.4 0.0 all-to-all-done
  24.4 0.0 copy-done
  24.4 0.0 copy-done.1
  24.4 0.0 copy-done.2
  24.4 1.8 %grid.1 = f32[8,2,128]{2,1,0:T(2,128)S(1)} custom-call(bf16[8,4,16,128]{3,2,1,0:T(8,128)(2,1)S(1)} %bitcast.1, bf16[256,384]{1,0:T(8,128)(2,1)S(1)} %copy-done, bf16[256,2560]{1,0:T(8,128)(2,1)S(1)} %table.1.table_ref, f32[4,4,2560]{2,1,0:T(4,128)S(1)} %get-tuple-element.14.own_ref, f32[3,4,2560]{2,1,0:T(4,128)S(1)} %collective-permute-done.first_ref, ...), custom_call_target="tpu_custom_call" | custom-call | tf_op jit(solution)/shard_map/grid/pallas_call | solution.py:511
  26.3 13.6 %all_to_all.10.arrived_ref = f32[8,2,128]{2,1,0:T(2,128)S(1)} all-to-all(f32[8,2,128]{2,1,0:T(2,128)S(1)} %grid.1), channel_id=1, replica_groups=mesh['wave'=8,'lev'=4] {'wave'}, dimensions={0} | all-to-all | bytes 16384 | tf_op jit(solution)/shard_map/all_to_all | solution.py:534
  39.9 1.2 %analysis.1 = f32[13,2,4,1280]{3,2,1,0:T(4,128)} custom-call(f32[8,2,128]{2,1,0:T(2,128)S(1)} %all_to_all.10.arrived_ref, bf16[13,16,1280]{2,1,0:T(8,128)(2,1)S(1)} %get-tuple-element.20.live_ref), custom_call_target="tpu_custom_call" | custom-call | tf_op jit(solution)/shard_map/analysis/pallas_call | solution.py:536
  (1 shorter events, 0.0 us)
Async XLA Ops:
  0.0 22.3 %copy-start.3 = (s32[104]{0:T(128)S(1)}, s32[104]{0:T(128)}, u32[]{:S(2)}) copy-start(s32[104]{0:T(128)} %wave_hbm.1) | copy-start | bytes 1252
  4.6 19.8 %copy-start = (bf16[256,384]{1,0:T(8,128)(2,1)S(1)}, bf16[256,384]{1,0:T(8,128)(2,1)}, u32[]{:S(2)}) copy-start(bf16[256,384]{1,0:T(8,128)(2,1)} %constant.17.clone.unpack_ref) | copy-start | bytes 589828
  4.6 19.8 %copy-start.1 = (bf16[32,128]{1,0:T(8,128)(2,1)S(1)}, bf16[32,128]{1,0:T(8,128)(2,1)}, u32[]{:S(2)}) copy-start(bf16[32,128]{1,0:T(8,128)(2,1)} %constant.18.clone.spread_ref) | copy-start | bytes 24580
  4.6 19.8 %copy-start.2 = (f32[8,128]{1,0:T(8,128)S(1)}, f32[8,128]{1,0:T(8,128)}, u32[]{:S(2)}) copy-start(f32[8,128]{1,0:T(8,128)} %constant.19.clone.pick_ref) | copy-start | bytes 12292
  4.6 19.8 %all-to-all-start = ((bf16[32,16,128]{2,1,0:T(8,128)(2,1)}), bf16[32,16,128]{2,1,0:T(8,128)(2,1)S(1)}, u32[]{:S(2)}, u32[]{:S(2)}) async-start(bf16[32,16,128]{2,1,0:T(8,128)(2,1)} %get-tuple-element.13), calls=%async_computation | async-start | bytes 262144 | tf_op jit(solution)/shard_map/all_to_all | solution.py:487
  11.7 6.3 %collective-permute-start = (f32[3,4,2560]{2,1,0:T(4,128)S(1)}, f32[3,4,2560]{2,1,0:T(4,128)S(1)}, u32[]{:S(2)}, u32[]{:S(2)}) collective-permute-start(f32[3,4,2560]{2,1,0:T(4,128)S(1)} %get-tuple-element.15), channel_id=1, source_target_pairs={{0,4},{8,12},{16,20},{24,28},{4,0},{12,8},{20,16},{28,24},{1,5},{9... | collective-permute-start | bytes 368648 | tf_op jit(solution)/shard_map/ppermute | solution.py:468
  13.3 4.8 %collective-permute-start.1 = (f32[3,4,2560]{2,1,0:T(4,128)S(1)}, f32[3,4,2560]{2,1,0:T(4,128)S(1)}, u32[]{:S(2)}, u32[]{:S(2)}) collective-permute-start(f32[3,4,2560]{2,1,0:T(4,128)S(1)} %get-tuple-element.16), channel_id=1, source_target_pairs={{4,8},{12,16},{20,24},{8,4},{16,12},{24,20},{5,9},{13,17},{21,25},... | collective-permute-start | bytes 368648 | tf_op jit(solution)/shard_map/ppermute | solution.py:469
  18.2 5.6 %collective-permute-start.2 = (f32[8,2560]{1,0:T(8,128)S(1)}, f32[8,2560]{1,0:T(8,128)S(1)}, u32[]{:S(2)}, u32[]{:S(2)}) collective-permute-start(f32[8,2560]{1,0:T(8,128)S(1)} %get-tuple-element.17), channel_id=1, source_target_pairs={{0,1},{2,3},{1,0},{3,2},{4,5},{6,7},{5,4},{7,6},{8,9},{10,11},{9,8... | collective-permute-start | bytes 245768 | tf_op jit(solution)/shard_map/ppermute | solution.py:509
  18.2 6.2 %collective-permute-start.3 = (f32[8,2560]{1,0:T(8,128)S(1)}, f32[8,2560]{1,0:T(8,128)S(1)}, u32[]{:S(2)}, u32[]{:S(2)}) collective-permute-start(f32[8,2560]{1,0:T(8,128)S(1)} %get-tuple-element.18), channel_id=1, source_target_pairs={{1,2},{2,1},{5,6},{6,5},{9,10},{10,9},{13,14},{14,13},{17,18},{18,... | collective-permute-start | bytes 245768 | tf_op jit(solution)/shard_map/ppermute | solution.py:510

commit v4 on v3

--- a/solution.py
+++ b/solution.py
@@ -14,7 +14,6 @@
 halo = 2
 lanes = 128
 packed_rows = 16
-group_slots = 8
 
 
 def round_up(value, step):
@@ -42,33 +41,18 @@
         self.slot_pad = round_up(self.slots, packed_rows)
         self.window = self.rows + 2 * halo
         self.deep = self.levels + 2 * halo
-        self.half = round_up(2 * self.levels * self.window, lanes // 2)
-        self.piece = round_up(2 * self.half, lanes)
+        self.unit = 4 * self.levels
+        self.piece = round_up(self.window * self.unit, lanes)
         self.stack = round_up(self.window * self.deep, 8)
         self.reply = round_up(2 * self.levels * self.slot_pad, lanes)
         assert self.rows == halo and self.deep == 8 and self.lon % lanes == 0
+        assert lanes % self.unit == 0 and self.lats % 8 == 0
 
 
 def piece_lanes(z):
     at = np.arange(z.piece)
-    part, rest = at // z.half, at % z.half
-    wind, rest = rest // (z.levels * z.window), rest % (z.levels * z.window)
-    valid = (part < 2) & (wind < 2)
-    return part, wind, rest // z.levels, rest % z.levels, valid
-
-
-def pack_constants(z):
-    part, wind, row, level, valid = piece_lanes(z)
-    source = np.arange(z.slots * 4 * z.levels)
-    channel = source // z.levels % 4
-    pick = (channel[:, None] == wind * 2 + part) & (source[:, None] % z.levels == level) & valid
-    gather = np.arange(z.slot_pad)[:, None] == source // (4 * z.levels)
-    offset = np.where(valid, row - halo, -(10**6)) - np.arange(z.lats)[:, None]
-    return (
-        pick.astype(np.float32),
-        jnp.asarray(gather, jnp.bfloat16),
-        offset.astype(np.int32),
-    )
+    row, channel, level = at // z.unit, at // z.levels % 4, at % z.levels
+    return channel % 2, channel // 2, row, level, row < z.window
 
 
 def unpack_constant(z):
@@ -97,28 +81,6 @@
     return jnp.asarray(spread, jnp.bfloat16), pick.astype(np.float32)
 
 
-def pack_kernel(z, tracer_hbm, flags_hbm, own_ref, first_ref, second_ref, tracer_ref, flags_ref, sems):
-    copies = [
-        pltpu.make_async_copy(tracer_hbm, tracer_ref, sems.at[0]),
-        pltpu.make_async_copy(flags_hbm, flags_ref, sems.at[1]),
-    ]
-    for copy in copies:
-        copy.start()
-    even = lax.axis_index("wave") % 2 == 0
-    copies[0].wait()
-    for j in range(z.rows):
-        row = tracer_ref[:, j, :]
-        own_ref[j] = row
-        first_ref[j] = row
-        second_ref[j] = row
-    copies[1].wait()
-    switched = [flags_ref[:, j, :].astype(jnp.float32) for j in range(z.rows)]
-    for j in range(z.rows):
-        own_ref[z.rows + j] = switched[j]
-    first_ref[z.rows] = jnp.where(even, switched[-1], switched[0])
-    second_ref[z.rows] = jnp.where(even, switched[0], switched[-1])
-
-
 def legendre_kernel(
     z,
     wave_hbm,
@@ -126,107 +88,132 @@
     spectra_hbm,
     legendre_hbm,
     derivative_hbm,
-    pick_hbm,
-    gather_hbm,
-    offset_hbm,
+    tracer_hbm,
+    flags_hbm,
     pieces_ref,
     live_ref,
     scale_ref,
+    own_ref,
+    first_ref,
+    second_ref,
     wave_ref,
     weight_ref,
     spectra_ref,
     legendre_ref,
     derivative_ref,
-    pick_ref,
-    gather_ref,
-    offset_ref,
+    tracer_ref,
+    flags_ref,
+    by_slot_ref,
     sems,
 ):
+    group_slots = lanes // z.unit
     groups = [
         (first, min(first + group_slots, z.slots)) for first in range(0, z.slots, group_slots)
+    ]
+    whole = [
+        pltpu.make_async_copy(hbm, ref, sems.at[a, 0])
+        for a, (hbm, ref) in enumerate(
+            (
+                (wave_hbm, wave_ref),
+                (weight_hbm, weight_ref),
+                (tracer_hbm, tracer_ref),
+                (flags_hbm, flags_ref),
+            )
+        )
     ]
     fetches = []
     for g, (first, last) in enumerate(groups):
         part = pl.ds(first, last - first)
         fetches.append(
             [
-                pltpu.make_async_copy(hbm.at[part], ref.at[part], sems.at[a, g])
+                pltpu.make_async_copy(hbm.at[part], ref.at[part], sems.at[4 + a, g])
                 for a, (hbm, ref) in enumerate(
                     (
-                        (spectra_hbm, spectra_ref),
                         (legendre_hbm, legendre_ref),
                         (derivative_hbm, derivative_ref),
+                        (spectra_hbm, spectra_ref),
                     )
                 )
             ]
         )
-    constants = [
-        pltpu.make_async_copy(hbm, ref, sems.at[3 + a, 0])
-        for a, (hbm, ref) in enumerate(
-            ((pick_hbm, pick_ref), (gather_hbm, gather_ref), (offset_hbm, offset_ref))
-        )
-    ]
-    scalars = [
-        pltpu.make_async_copy(hbm, ref, sems.at[6 + a, 0])
-        for a, (hbm, ref) in enumerate(((wave_hbm, wave_ref), (weight_hbm, weight_ref)))
-    ]
-    for copies in [scalars] + fetches:
+    for copies in [whole[:2], *fetches, whole[2:]]:
         for copy in copies:
             copy.start()
-    for copy in constants:
-        copy.start()
     base = lax.axis_index("wave") * z.slots
-    for copy in scalars:
-        copy.wait()
+    by_slot_ref[...] = jnp.zeros_like(by_slot_ref)
+    whole[0].wait()
+    whole[1].wait()
     for j in range(z.rows):
         scale = weight_ref[j] * (1.0 / math.sqrt(z.lon))
         scale_ref[j * z.deep : (j + 1) * z.deep] = jnp.full((z.deep, lanes), scale, jnp.float32)
-    height = 4 * z.levels
     degree = lax.broadcasted_iota(jnp.int32, (z.lats, z.degrees), 1)
-    channel = lax.broadcasted_iota(jnp.int32, (height, z.lats), 0) // z.levels
+    lane = lax.broadcasted_iota(jnp.int32, (z.lats, lanes), 1)
+    lane_slot, channel = lane // z.unit, lane // z.levels % 4
     sign_sum = jnp.where(channel % 2 == 0, -1.0, 1.0)
     sign_slope = jnp.where(channel < 2, -1.0, 1.0)
-    winds = []
     for (first, last), copies in zip(groups, fetches):
         waves = [wave_ref[base + s] for s in range(first, last)]
         for copy in copies:
             copy.wait()
-        right = []
+        sums, slopes = [], []
         for s, wave in zip(range(first, last), waves):
             live = jnp.where(degree >= wave, 1.0, 0.0).astype(jnp.bfloat16)
             masked = legendre_ref[s] * live
             live_ref[s] = masked
-            right += [masked, derivative_ref[s] * live]
-        left = [spectra_ref[s].reshape(height, z.degrees) for s in range(first, last)]
-        sums = contract(jnp.concatenate(left, axis=0), jnp.concatenate(right, axis=0), ((1,), (1,)))
+            sums.append(masked)
+            slopes.append(derivative_ref[s] * live)
+        right = [spectra_ref[s].reshape(z.unit, z.degrees) for s in range(first, last)]
+        right += [jnp.zeros_like(right[0])] * (group_slots - len(right))
+        right = jnp.concatenate(right, axis=0)
+        sums = contract(jnp.concatenate(sums, axis=0), right, ((1,), (1,)))
+        slopes = contract(jnp.concatenate(slopes, axis=0), right, ((1,), (1,)))
+        sum_of = jnp.zeros((z.lats, lanes), jnp.float32)
+        slope_of = sum_of
+        factor = sum_of
+        doubled = sum_of
         for at, wave in enumerate(waves):
-            mine = sums[at * height : (at + 1) * height]
-            sums_at = mine[:, 2 * at * z.lats : (2 * at + 1) * z.lats]
-            slopes = mine[:, (2 * at + 1) * z.lats : (2 * at + 2) * z.lats]
-            turned = jnp.concatenate(
-                [sums_at[c * z.levels : (c + 1) * z.levels] for c in (3, 2, 1, 0)], axis=0
-            )
-            scaled = wave.astype(jnp.float32) / z.degrees
-            doubled = jnp.where(wave == 0, 1.0, 2.0)
-            winds.append((scaled * sign_sum * turned + sign_slope * slopes) * doubled)
-    winds = jnp.concatenate(winds, axis=0).astype(jnp.bfloat16)
-    for copy in constants:
-        copy.wait()
-
-    def one_band(b, carry):
-        choose = jnp.where(offset_ref[...] + b * z.rows == 0, 1.0, 0.0).astype(jnp.bfloat16)
-        spread = contract(winds, choose, ((1,), (0,))) * pick_ref[...]
-        piece = contract(gather_ref[...], spread.astype(jnp.bfloat16), ((1,), (0,)))
-        piece = piece.astype(jnp.bfloat16)
+            mine = lane_slot == at
+            block = slice(at * z.lats, (at + 1) * z.lats)
+            sum_of = jnp.where(mine, sums[block], sum_of)
+            slope_of = jnp.where(mine, slopes[block], slope_of)
+            factor = jnp.where(mine, wave.astype(jnp.float32) / z.degrees, factor)
+            doubled = jnp.where(mine, jnp.where(wave == 0, 1.0, 2.0), doubled)
+        turned = sum_of
+        for c in range(4):
+            moved = pltpu.roll(sum_of, (2 * c - 3) * z.levels % lanes, 1)
+            turned = jnp.where(channel == c, moved, turned)
+        winds = (factor * sign_sum * turned + sign_slope * slope_of) * doubled
+        for at, s in enumerate(range(first, last)):
+            moved = winds if at == 0 else pltpu.roll(winds, lanes - at * z.unit, 1)
+            by_slot_ref[s * z.lats : (s + 1) * z.lats] = moved
+    tiles = round_up((z.lats + 2 * halo) * z.unit, lanes) // lanes + z.piece // lanes
+    rows = [jnp.zeros((z.slot_pad, lanes), jnp.float32) for _ in range(tiles)]
+    slot_lane = lax.broadcasted_iota(jnp.int32, (z.slot_pad, lanes), 1) // z.unit
+    for lat in range(z.lats):
+        tile, at = divmod((lat + halo) * z.unit, lanes)
+        block = by_slot_ref[pl.ds(lat, z.slot_pad, stride=z.lats), :]
+        block = block if at == 0 else pltpu.roll(block, at, 1)
+        rows[tile] = jnp.where(slot_lane == at // z.unit, block, rows[tile])
+    rows = jnp.concatenate(rows, axis=1)
+    for b in range(z.bands):
+        at = b * z.rows * z.unit
+        piece = rows[:, at : at + z.piece].astype(jnp.bfloat16)
         for l in range(z.sets):
             pieces_ref[b * z.sets + l] = piece
-        return carry
-
-    if z.bands <= 16:
-        for b in range(z.bands):
-            one_band(b, 0)
-    else:
-        lax.fori_loop(0, z.bands, one_band, 0)
+
+    even = lax.axis_index("wave") % 2 == 0
+    whole[2].wait()
+    for j in range(z.rows):
+        row = tracer_ref[:, j, :]
+        own_ref[j] = row
+        first_ref[j] = row
+        second_ref[j] = row
+    whole[3].wait()
+    switched = [flags_ref[:, j, :].astype(jnp.float32) for j in range(z.rows)]
+    for j in range(z.rows):
+        own_ref[z.rows + j] = switched[j]
+    first_ref[z.rows] = jnp.where(even, switched[-1], switched[0])
+    second_ref[z.rows] = jnp.where(even, switched[0], switched[-1])
 
 
 def table_kernel(z, wave_ref, table_ref):
@@ -447,43 +434,34 @@
     table_bytes = 4 * z.bands * z.slot_pad * z.lon
     any_spec = pl.BlockSpec(memory_space=pltpu.HBM)
     edge_shape = jax.ShapeDtypeStruct((z.rows + 1, z.levels, z.lon), f32)
-    own, to_first, to_second = pl.pallas_call(
-        functools.partial(pack_kernel, z),
-        name="pack",
-        in_specs=[any_spec] * 2,
-        out_specs=tuple(vmem(3)),
+    group_count = -(-z.slots * z.unit // lanes)
+    fetched = (slot_wave, lat_weight, spectra, legendre, derivative, tracer, limiter_flags)
+    pieces, live, scale, own, to_first, to_second = pl.pallas_call(
+        functools.partial(legendre_kernel, z),
+        name="legendre",
+        in_specs=[any_spec] * len(fetched),
+        out_specs=tuple(vmem(6)),
         out_shape=(
+            jax.ShapeDtypeStruct((z.bands * z.sets, z.slot_pad, z.piece), bf16),
+            jax.ShapeDtypeStruct(legendre.shape, bf16),
+            jax.ShapeDtypeStruct((z.rows * z.deep, lanes), f32),
             jax.ShapeDtypeStruct((2 * z.rows, z.levels, z.lon), f32),
             edge_shape,
             edge_shape,
         ),
-        scratch_shapes=[
-            pltpu.VMEM(tracer.shape, tracer.dtype),
-            pltpu.VMEM(tracer.shape, limiter_flags.dtype),
-            pltpu.SemaphoreType.DMA((2,)),
+        scratch_shapes=[pltpu.SMEM(x.shape, x.dtype) for x in fetched[:2]]
+        + [pltpu.VMEM(x.shape, x.dtype) for x in fetched[2:]]
+        + [
+            pltpu.VMEM((z.slot_pad * z.lats, lanes), f32),
+            pltpu.SemaphoreType.DMA((7, group_count)),
         ],
-        compiler_params=params(8 * nbytes(tracer)),
-    )(in_hbm(tracer), in_hbm(limiter_flags))
+        compiler_params=params(
+            2 * nbytes(spectra), 6 * nbytes(legendre), 8 * nbytes(tracer), fan
+        ),
+    )(*map(in_hbm, fetched))
     first_pairs, second_pairs = swaps("wave")
     wave_first = lax.ppermute(to_first, "wave", first_pairs)
     wave_second = lax.ppermute(to_second, "wave", second_pairs)
-    constants = pack_constants(z)
-    group_count = -(-z.slots // group_slots)
-    pieces, live, scale = pl.pallas_call(
-        functools.partial(legendre_kernel, z),
-        name="legendre",
-        in_specs=[any_spec] * 8,
-        out_specs=tuple(vmem(3)),
-        out_shape=(
-            jax.ShapeDtypeStruct((z.bands * z.sets, z.slot_pad, z.piece), bf16),
-            jax.ShapeDtypeStruct(legendre.shape, bf16),
-            jax.ShapeDtypeStruct((z.rows * z.deep, lanes), f32),
-        ),
-        scratch_shapes=[pltpu.SMEM(x.shape, x.dtype) for x in (slot_wave, lat_weight)]
-        + [pltpu.VMEM(x.shape, x.dtype) for x in (spectra, legendre, derivative, *constants)]
-        + [pltpu.SemaphoreType.DMA((8, group_count))],
-        compiler_params=params(2 * nbytes(spectra), 4 * nbytes(legendre), fan),
-    )(*map(in_hbm, (slot_wave, lat_weight, spectra, legendre, derivative, *constants)))
     arrived = lax.all_to_all(pieces, ("wave", "lev"), split_axis=0, concat_axis=0, tiled=True)
     padded_wave = jnp.pad(
         slot_wave.reshape(z.bands, z.slots), ((0, 0), (0, z.slot_pad - z.slots))

time: 41.4 us -> 38.9 us (0.940)
  waiting for transfers between devices: 4.76 us -> 7.29 us
  Pallas kernels: 9.93 us -> 7.49 us
  starting transfers between devices: 12.4 us -> 11.1 us
  blocking collectives: 13.6 us -> 12.4 us
    ppermute x1, waiting for transfers between devices: 4.11 us -> 5.74 us  [on_device(): wave_first = lax.ppermute(to_first, 'wave', first_pairs)]
    pallas_call x1, Pallas kernels: 4.56 us -> 3.09 us  [on_device(): pl.pallas_call(functools.partial(legendre_kernel, z), name='legendre', in...]
    ppermute x1, starting transfers between devices: 4.06 us -> 2.75 us  [on_device(): lev_second = lax.ppermute(down, 'lev', second_pairs)]
    all_to_all x1, blocking collectives: 13.6 us -> 12.4 us  [on_device(): lax.all_to_all(reply, 'wave', split_axis=0, concat_axis=0, tiled=True)]
    pallas_call x1 -> x0, Pallas kernels: 0.97 us -> none  [on_device(): pl.pallas_call(functools.partial(pack_kernel, z), name='pack', in_specs=[...]
    ppermute x1, waiting for transfers between devices: 0.64 us -> 1.54 us  [on_device(): lev_second = lax.ppermute(down, 'lev', second_pairs)]
  transfers between devices with their start and end apart: 5 -> 5, of which waited for: 2 -> 2; matrix products, arithmetic and copies ran while one was open for 0% -> 0% of each run, Pallas kernels for 6% -> 4%
where the time goes in v4:
time: 38.9 us; the launch traced here: 38.6 us
  blocking collectives  12.4 us (32%)
  starting transfers between devices  11.1 us (29%)
  Pallas kernels  7.49 us (19%)
  waiting for transfers between devices  7.29 us (19%)
    all_to_all x1, blocking collectives, on_device(): lax.all_to_all(reply, 'wave', split_axis=0, concat_axis=0, tiled=True)  12.4 us
    all_to_all x1, starting transfers between devices, on_device(): lax.all_to_all(pieces, ('wave', 'lev'), split_axis=0, concat_axis=0, tile...  6.13 us
    ppermute x1, waiting for transfers between devices, on_device(): wave_first = lax.ppermute(to_first, 'wave', first_pairs)  5.74 us
    pallas_call x1, Pallas kernels, on_device(): pl.pallas_call(functools.partial(legendre_kernel, z), name='legendre', in...  3.09 us
    ppermute x1, starting transfers between devices, on_device(): lev_second = lax.ppermute(down, 'lev', second_pairs)  2.75 us
    pallas_call x1, Pallas kernels, on_device(): pl.pallas_call(functools.partial(grid_kernel, z), name='grid', in_specs=v...  1.83 us
    ppermute x1, waiting for transfers between devices, on_device(): lev_second = lax.ppermute(down, 'lev', second_pairs)  1.54 us
    ppermute x1, starting transfers between devices, on_device(): wave_first = lax.ppermute(to_first, 'wave', first_pairs)  1.53 us
  transfers between devices with their start and end apart: 5, of which 2 were waited for; matrix products, arithmetic and copies ran while one was open for 0% of the time, Pallas kernels for 4%

profile of v4, /device:TPU:2, one launch (start us, length us, event | category | flops | bytes accessed | tf_op | source)
XLA Modules:
  0.0 38.6 jit_solution(6969184848689048584)
XLA Ops:
  0.0 0.0 copy-start.3
  0.0 3.1 %legendre.1 = (bf16[32,16,128]{2,1,0:T(8,128)(2,1)}, bf16[13,16,1280]{2,1,0:T(8,128)(2,1)S(1)}, f32[16,128]{1,0:T(8,128)S(1)}, f32[4,4,2560]{2,1,0:T(4,128)S(1)}...) custom-call(s32[104]{0:T(128)} %wave_hbm.1, f32[2]{0:T(128)} %weight_hbm.1, bf16[13,4,4,1280]{3,2,1,0:T(4,128)(2,1)} %spectra_hbm.1, ...), custom_call_target="tpu_custom_call" | custom-call | tf_op jit(solution)/shard_map/legendre/pallas_call | solution.py:439
  3.1 0.0 copy-start
  3.1 0.0 copy-start.1
  3.1 0.0 copy-start.2
  3.1 6.1 %all-to-all-start = ((bf16[32,16,128]{2,1,0:T(8,128)(2,1)}), bf16[32,16,128]{2,1,0:T(8,128)(2,1)S(1)}, u32[]{:S(2)}, u32[]{:S(2)}) async-start(bf16[32,16,128]{2,1,0:T(8,128)(2,1)} %get-tuple-element.13), calls=%async_computation | async-start | bytes 262144 | tf_op jit(solution)/shard_map/all_to_all | solution.py:465
  9.3 1.5 %collective-permute-start = (f32[3,4,2560]{2,1,0:T(4,128)S(1)}, f32[3,4,2560]{2,1,0:T(4,128)S(1)}, u32[]{:S(2)}, u32[]{:S(2)}) collective-permute-start(f32[3,4,2560]{2,1,0:T(4,128)S(1)} %get-tuple-element.15), channel_id=1, source_target_pairs={{0,4},{8,12},{16,20},{24,28},{4,0},{12,8},{20,16},{28,24},{1,5},{9... | collective-permute-start | bytes 368648 | tf_op jit(solution)/shard_map/ppermute | solution.py:463
  10.8 0.7 %collective-permute-start.1 = (f32[3,4,2560]{2,1,0:T(4,128)S(1)}, f32[3,4,2560]{2,1,0:T(4,128)S(1)}, u32[]{:S(2)}, u32[]{:S(2)}) collective-permute-start(f32[3,4,2560]{2,1,0:T(4,128)S(1)} %get-tuple-element.16), channel_id=1, source_target_pairs={{4,8},{12,16},{20,24},{8,4},{16,12},{24,20},{5,9},{13,17},{21,25},... | collective-permute-start | bytes 368648 | tf_op jit(solution)/shard_map/ppermute | solution.py:464
  11.5 5.7 %collective-permute-done.first_ref = f32[3,4,2560]{2,1,0:T(4,128)S(1)} collective-permute-done((f32[3,4,2560]{2,1,0:T(4,128)S(1)}, f32[3,4,2560]{2,1,0:T(4,128)S(1)}, u32[]{:S(2)}, u32[]{:S(2)}) %collective-permute-start) | collective-permute-done | bytes 122912 | tf_op jit(solution)/shard_map/ppermute | solution.py:463
  17.2 0.0 collective-permute-done.1.second_ref
  17.2 0.1 edges.1
  17.3 0.1 collective-permute-start.2
  17.4 2.7 %collective-permute-start.3 = (f32[8,2560]{1,0:T(8,128)S(1)}, f32[8,2560]{1,0:T(8,128)S(1)}, u32[]{:S(2)}, u32[]{:S(2)}) collective-permute-start(f32[8,2560]{1,0:T(8,128)S(1)} %get-tuple-element.18), channel_id=1, source_target_pairs={{1,2},{2,1},{5,6},{6,5},{9,10},{10,9},{13,14},{14,13},{17,18},{18,... | collective-permute-start | bytes 245768 | tf_op jit(solution)/shard_map/ppermute | solution.py:488
  20.2 0.0 copy-done.3
  20.2 0.1 reshape.10
  20.3 0.1 reshape.12.wave_ref
  20.4 1.3 %table.1.table_ref = bf16[256,2560]{1,0:T(8,128)(2,1)S(1)} custom-call(s32[128,1]{1,0:T(8,128)S(1)} %reshape.12.wave_ref), custom_call_target="tpu_custom_call" | custom-call | tf_op jit(solution)/shard_map/table/pallas_call | solution.py:469
  21.6 0.0 collective-permute-done.2.lev_first_ref
  21.6 1.5 %collective-permute-done.3.lev_second_ref = f32[8,2560]{1,0:T(8,128)S(1)} collective-permute-done((f32[8,2560]{1,0:T(8,128)S(1)}, f32[8,2560]{1,0:T(8,128)S(1)}, u32[]{:S(2)}, u32[]{:S(2)}) %collective-permute-start.3) | collective-permute-done | bytes 81952 | tf_op jit(solution)/shard_map/ppermute | solution.py:488
  23.2 0.0 all-to-all-done
  23.2 0.0 copy-done
  23.2 0.0 copy-done.1
  23.2 0.0 copy-done.2
  23.2 1.8 %grid.1 = f32[8,2,128]{2,1,0:T(2,128)S(1)} custom-call(bf16[8,4,16,128]{3,2,1,0:T(8,128)(2,1)S(1)} %bitcast.1, bf16[256,384]{1,0:T(8,128)(2,1)S(1)} %copy-done, bf16[256,2560]{1,0:T(8,128)(2,1)S(1)} %table.1.table_ref, f32[4,4,2560]{2,1,0:T(4,128)S(1)} %get-tuple-element.14.own_ref, f32[3,4,2560]{2,1,0:T(4,128)S(1)} %collective-permute-done.first_ref, ...), custom_call_target="tpu_custom_call" | custom-call | tf_op jit(solution)/shard_map/grid/pallas_call | solution.py:489
  25.0 12.4 %all_to_all.10.arrived_ref = f32[8,2,128]{2,1,0:T(2,128)S(1)} all-to-all(f32[8,2,128]{2,1,0:T(2,128)S(1)} %grid.1), channel_id=1, replica_groups=mesh['wave'=8,'lev'=4] {'wave'}, dimensions={0} | all-to-all | bytes 16384 | tf_op jit(solution)/shard_map/all_to_all | solution.py:512
  37.4 1.2 %analysis.1 = f32[13,2,4,1280]{3,2,1,0:T(4,128)} custom-call(f32[8,2,128]{2,1,0:T(2,128)S(1)} %all_to_all.10.arrived_ref, bf16[13,16,1280]{2,1,0:T(8,128)(2,1)S(1)} %get-tuple-element.20.live_ref), custom_call_target="tpu_custom_call" | custom-call | tf_op jit(solution)/shard_map/analysis/pallas_call | solution.py:514
  (1 shorter events, 0.0 us)
Async XLA Ops:
  0.0 20.2 %copy-start.3 = (s32[104]{0:T(128)S(1)}, s32[104]{0:T(128)}, u32[]{:S(2)}) copy-start(s32[104]{0:T(128)} %wave_hbm.1) | copy-start | bytes 1252
  3.1 20.1 %copy-start = (bf16[256,384]{1,0:T(8,128)(2,1)S(1)}, bf16[256,384]{1,0:T(8,128)(2,1)}, u32[]{:S(2)}) copy-start(bf16[256,384]{1,0:T(8,128)(2,1)} %constant.8.clone.unpack_ref) | copy-start | bytes 589828
  3.1 20.1 %copy-start.1 = (bf16[32,128]{1,0:T(8,128)(2,1)S(1)}, bf16[32,128]{1,0:T(8,128)(2,1)}, u32[]{:S(2)}) copy-start(bf16[32,128]{1,0:T(8,128)(2,1)} %constant.9.clone.spread_ref) | copy-start | bytes 24580
  3.1 20.1 %copy-start.2 = (f32[8,128]{1,0:T(8,128)S(1)}, f32[8,128]{1,0:T(8,128)}, u32[]{:S(2)}) copy-start(f32[8,128]{1,0:T(8,128)} %constant.10.clone.pick_ref) | copy-start | bytes 12292
  3.1 20.0 %all-to-all-start = ((bf16[32,16,128]{2,1,0:T(8,128)(2,1)}), bf16[32,16,128]{2,1,0:T(8,128)(2,1)S(1)}, u32[]{:S(2)}, u32[]{:S(2)}) async-start(bf16[32,16,128]{2,1,0:T(8,128)(2,1)} %get-tuple-element.13), calls=%async_computation | async-start | bytes 262144 | tf_op jit(solution)/shard_map/all_to_all | solution.py:465
  9.3 7.9 %collective-permute-start = (f32[3,4,2560]{2,1,0:T(4,128)S(1)}, f32[3,4,2560]{2,1,0:T(4,128)S(1)}, u32[]{:S(2)}, u32[]{:S(2)}) collective-permute-start(f32[3,4,2560]{2,1,0:T(4,128)S(1)} %get-tuple-element.15), channel_id=1, source_target_pairs={{0,4},{8,12},{16,20},{24,28},{4,0},{12,8},{20,16},{28,24},{1,5},{9... | collective-permute-start | bytes 368648 | tf_op jit(solution)/shard_map/ppermute | solution.py:463
  10.8 6.4 %collective-permute-start.1 = (f32[3,4,2560]{2,1,0:T(4,128)S(1)}, f32[3,4,2560]{2,1,0:T(4,128)S(1)}, u32[]{:S(2)}, u32[]{:S(2)}) collective-permute-start(f32[3,4,2560]{2,1,0:T(4,128)S(1)} %get-tuple-element.16), channel_id=1, source_target_pairs={{4,8},{12,16},{20,24},{8,4},{16,12},{24,20},{5,9},{13,17},{21,25},... | collective-permute-start | bytes 368648 | tf_op jit(solution)/shard_map/ppermute | solution.py:464
  17.3 4.3 %collective-permute-start.2 = (f32[8,2560]{1,0:T(8,128)S(1)}, f32[8,2560]{1,0:T(8,128)S(1)}, u32[]{:S(2)}, u32[]{:S(2)}) collective-permute-start(f32[8,2560]{1,0:T(8,128)S(1)} %get-tuple-element.17), channel_id=1, source_target_pairs={{0,1},{2,3},{1,0},{3,2},{4,5},{6,7},{5,4},{7,6},{8,9},{10,11},{9,8... | collective-permute-start | bytes 245768 | tf_op jit(solution)/shard_map/ppermute | solution.py:487
  17.4 5.8 %collective-permute-start.3 = (f32[8,2560]{1,0:T(8,128)S(1)}, f32[8,2560]{1,0:T(8,128)S(1)}, u32[]{:S(2)}, u32[]{:S(2)}) collective-permute-start(f32[8,2560]{1,0:T(8,128)S(1)} %get-tuple-element.18), channel_id=1, source_target_pairs={{1,2},{2,1},{5,6},{6,5},{9,10},{10,9},{13,14},{14,13},{17,18},{18,... | collective-permute-start | bytes 245768 | tf_op jit(solution)/shard_map/ppermute | solution.py:488

commit v5 on v4

--- a/solution.py
+++ b/solution.py
@@ -40,12 +40,11 @@
         self.bands, self.sets = bands, sets
         self.slot_pad = round_up(self.slots, packed_rows)
         self.window = self.rows + 2 * halo
-        self.deep = self.levels + 2 * halo
+        self.block = self.rows * self.levels
         self.unit = 4 * self.levels
         self.piece = round_up(self.window * self.unit, lanes)
-        self.stack = round_up(self.window * self.deep, 8)
         self.reply = round_up(2 * self.levels * self.slot_pad, lanes)
-        assert self.rows == halo and self.deep == 8 and self.lon % lanes == 0
+        assert self.rows == halo and self.block == 8 and self.lon % lanes == 0
         assert lanes % self.unit == 0 and self.lats % 8 == 0
 
 
@@ -57,18 +56,15 @@
 
 def unpack_constant(z):
     part, wind, row, level, valid = piece_lanes(z)
-    height = round_up(2 * z.stack, lanes)
-    target = np.arange(2 * height)
-    t_part, rest = target // height, target % height
-    t_wind, rest = rest // z.stack, rest % z.stack
-    t_row, t_deep = rest // z.deep, rest % z.deep
-    t_valid = (t_wind < 2) & (t_row < z.window)
-    same = (t_part[:, None] == part) & (t_wind[:, None] == wind) & (t_row[:, None] == row)
-    same = same & valid & t_valid[:, None]
-    own = same & (t_deep[:, None] == level + halo)
-    below = same & (t_deep[:, None] == halo - 1) & (level == z.levels - 1)
-    above = same & (t_deep[:, None] == halo + z.levels) & (level == 0)
-    return jnp.asarray(np.concatenate([own, below, above], axis=1), jnp.bfloat16)
+    tiles = [(0, 0, 1), (0, 2, -1), (1, -2, -1), (1, 0, 1), (1, 2, 3)]
+    target = [
+        (of, pair[j], k) for of, *pair in tiles for j in range(z.rows) for k in range(z.levels)
+    ]
+    target += [(-1, 0, 0)] * (round_up(len(target), packed_rows) - len(target))
+    t_wind, t_row, t_level = (np.array(x)[:, None] for x in zip(*target))
+    same = (t_wind == wind) & (t_row + halo == row) & (t_level == level) & valid
+    both = np.concatenate([same & (part == 0), same & (part == 1)], axis=0)
+    return jnp.asarray(both, jnp.bfloat16)
 
 
 def reply_constants(z):
@@ -77,8 +73,14 @@
     level, slot = rest // z.slot_pad, rest % z.slot_pad
     source = np.arange(2 * z.slot_pad)
     spread = (source[:, None] // z.slot_pad == part) & (source[:, None] % z.slot_pad == slot)
-    pick = np.arange(z.deep)[:, None] == level + halo
-    return jnp.asarray(spread, jnp.bfloat16), pick.astype(np.float32)
+    k = np.arange(z.block)[:, None] % z.levels
+    edge = 0.5 * diffusivity
+    picks = [
+        1.0 * (k == level),
+        edge * ((k == z.levels - 1) & (level == 0)),
+        edge * ((k == 0) & (level == z.levels - 1)),
+    ]
+    return jnp.asarray(spread, jnp.bfloat16), np.stack(picks).astype(np.float32)
 
 
 def legendre_kernel(
@@ -145,7 +147,8 @@
     whole[1].wait()
     for j in range(z.rows):
         scale = weight_ref[j] * (1.0 / math.sqrt(z.lon))
-        scale_ref[j * z.deep : (j + 1) * z.deep] = jnp.full((z.deep, lanes), scale, jnp.float32)
+        block = slice(j * z.levels, (j + 1) * z.levels)
+        scale_ref[block] = jnp.full((z.levels, lanes), scale, jnp.float32)
     degree = lax.broadcasted_iota(jnp.int32, (z.lats, z.degrees), 1)
     lane = lax.broadcasted_iota(jnp.int32, (z.lats, lanes), 1)
     lane_slot, channel = lane // z.unit, lane // z.levels % 4
@@ -197,9 +200,7 @@
     rows = jnp.concatenate(rows, axis=1)
     for b in range(z.bands):
         at = b * z.rows * z.unit
-        piece = rows[:, at : at + z.piece].astype(jnp.bfloat16)
-        for l in range(z.sets):
-            pieces_ref[b * z.sets + l] = piece
+        pieces_ref[b] = rows[:, at : at + z.piece].astype(jnp.bfloat16)
 
     even = lax.axis_index("wave") % 2 == 0
     whole[2].wait()
@@ -247,11 +248,8 @@
     _, north = by_parity("wave", first_ref[0], second_ref[0])
     even = lax.axis_index("lev") % 2 == 0
     rows = [south] + [own_ref[j] for j in range(z.rows)] + [north]
-    plan = [(row, z.levels - 1, 0) for row in rows]
-    plan += [(row, z.levels - 2, 1) for row in rows[1:-1]]
-    plan += [(own_ref[z.rows + j], z.levels - 1, 0) for j in range(z.rows)]
-    for at, (row, top, bottom) in enumerate(plan):
-        top, bottom = row[top : top + 1], row[bottom : bottom + 1]
+    for at, row in enumerate(rows):
+        top, bottom = row[z.levels - 1 :], row[:1]
         up_ref[at : at + 1] = jnp.where(even, top, bottom)
         down_ref[at : at + 1] = jnp.where(even, bottom, top)
 
@@ -270,59 +268,32 @@
     pick_ref,
     scale_ref,
     reply_ref,
-    q_ref,
-    f_ref,
 ):
     band, level_set = lax.axis_index("wave"), lax.axis_index("lev")
     lat_total = z.bands * z.rows
     lev_total = z.sets * z.levels
-    own = slice(halo, halo + z.levels)
-    q_ref[...] = jnp.zeros_like(q_ref)
-    f_ref[...] = jnp.zeros_like(f_ref)
-    for j in range(halo):
-        south, north = by_parity("wave", first_ref[j], second_ref[j])
-        q_ref[j, own] = south
-        q_ref[halo + z.rows + j, own] = north
-    south, north = by_parity("wave", first_ref[z.rows], second_ref[z.rows])
-    f_ref[0, own] = south
-    f_ref[z.rows + 1, own] = north
-    for j in range(z.rows):
-        q_ref[halo + j, own] = own_ref[j]
-        f_ref[1 + j, own] = own_ref[z.rows + j]
-    below, above = by_parity("lev", lev_first_ref[...], lev_second_ref[...])
-    for got, near, far in ((below, halo - 1, 0), (above, halo + z.levels, z.deep - 1)):
-        for j in range(z.rows + 2):
-            q_ref[halo - 1 + j, near : near + 1] = got[j : j + 1]
-        for j in range(z.rows):
-            at = z.rows + 2 + j
-            q_ref[halo + j, far : far + 1] = got[at : at + 1]
-            at = 2 * z.rows + 2 + j
-            f_ref[1 + j, near : near + 1] = got[at : at + 1]
-
     height = z.bands * z.slot_pad
-
-    def from_set(index):
-        return arrived_ref[:, index].reshape(height, z.piece)
-
-    blocks = jnp.concatenate(
-        [
-            from_set(level_set),
-            from_set(jnp.maximum(level_set - 1, 0)),
-            from_set(jnp.minimum(level_set + 1, z.sets - 1)),
-        ],
-        axis=1,
-    )
-    turned = contract(unpack_ref[...], blocks, ((1,), (1,))).astype(jnp.bfloat16)
+    f32 = jnp.float32
+
+    turned = contract(unpack_ref[...], arrived_ref[...].reshape(height, z.piece), ((1,), (1,)))
+    turned = turned.astype(jnp.bfloat16)
     span = turned.shape[0] // 2
     turned = jnp.concatenate([turned[:span], turned[span:]], axis=1)
     winds = contract(turned, table_ref[...], ((1,), (0,)))
-
-    def wind(which, j):
-        first = which * z.stack + j * z.deep
-        return courant_limit * jnp.tanh(winds[first : first + z.deep])
-
-    zonal = [wind(0, j) for j in range(1, z.rows + 3)]
-    merid = [wind(1, j) for j in range(z.window)]
+    winds = [
+        courant_limit * jnp.tanh(winds[t * z.block : (t + 1) * z.block]) for t in range(5)
+    ]
+    zonal, merid = winds[:2], winds[2:]
+
+    sublane = lax.broadcasted_iota(jnp.int32, (z.block, z.lon), 0)
+    low = sublane < z.levels
+    level = sublane % z.levels
+
+    def pair(a, b):
+        return jnp.concatenate([a, b], axis=0)
+
+    def swap(x):
+        return pltpu.roll(x, z.levels, 0)
 
     def west(x):
         return pltpu.roll(x, 1, 1)
@@ -330,59 +301,92 @@
     def east(x):
         return pltpu.roll(x, z.lon - 1, 1)
 
-    face = []
-    for j in range(z.rows + 2):
-        speed = 0.5 * (west(zonal[j]) + zonal[j])
+    def around(south, centre, north):
+        turn_s, turn_c, turn_n = swap(south), swap(centre), swap(north)
+        inner = (jnp.where(low, turn_s, turn_c), centre, jnp.where(low, turn_c, turn_n))
+        outer = (
+            jnp.where(low, turn_c, turn_s),
+            jnp.where(low, north, south),
+            jnp.where(low, turn_n, turn_c),
+        )
+        return inner, outer
+
+    def zonal_face(courant, flags):
+        speed = 0.5 * (west(courant) + courant)
         magnitude = jnp.abs(speed)
-        diffuse = 0.5 * (magnitude - f_ref[j] * (magnitude - speed * speed))
-        face.append((speed, diffuse))
-    lat_face = []
-    for j in range(1, z.window):
-        index = band * z.rows - halo + j
-        is_open = jnp.where((index > 0) & (index < lat_total), 0.5, 0.0).astype(jnp.float32)
-        speed = 0.5 * (merid[j - 1] + merid[j])
-        lat_face.append((speed * is_open, jnp.abs(speed) * is_open))
-    deep = lax.broadcasted_iota(jnp.int32, (z.deep, z.lon), 0) + (level_set * z.levels - halo)
-    rise = jnp.where((deep > 0) & (deep < lev_total), diffusivity, 0.0).astype(jnp.float32)
-
-    def tendency(q, first):
-        north_flux = []
-        for j in range(len(q) - 1):
-            mean, spread = lat_face[first - 1 + j]
-            north_flux.append(mean * (q[j] + q[j + 1]) - spread * (q[j + 1] - q[j]))
-        result = []
-        for j in range(1, len(q) - 1):
-            speed, diffuse = face[first - 2 + j]
-            centre = q[j]
-            western = west(centre)
-            flux = speed * 0.5 * (western + centre) - diffuse * (centre - western)
-            lift = rise * (centre - pltpu.roll(centre, 1, 0))
-            result.append(
-                -(east(flux) - flux)
-                - (north_flux[j] - north_flux[j - 1])
-                + (pltpu.roll(lift, z.deep - 1, 0) - lift)
-            )
-        return result
-
-    tracer = [q_ref[j] for j in range(z.window)]
-    first_tendency = tendency(tracer, 1)
-    section_one = [q + t for q, t in zip(tracer[1:-1], first_tendency)]
-    section_two = tendency(section_one, 2)
+        return 0.5 * speed, 0.5 * (magnitude - flags * (magnitude - speed * speed))
+
+    def lat_faces(courants, first_row, second_row):
+        faces = []
+        for a, b, step in ((courants[0], courants[1], 0), (courants[1], courants[2], 1)):
+            rows = [band * z.rows + row + step for row in (first_row, second_row)]
+            is_open = [jnp.where((row > 0) & (row < lat_total), 0.5, 0.0) for row in rows]
+            is_open = jnp.where(low, is_open[0], is_open[1])
+            speed = 0.5 * (a + b)
+            faces.append((speed * is_open, jnp.abs(speed) * is_open))
+        return faces
+
+    def horizontal(rows, zonal_face, lat_faces):
+        south, centre, north = rows
+        speed, diffuse = zonal_face
+        western = west(centre)
+        flux = speed * (western + centre) - diffuse * (centre - western)
+        (speed_s, spread_s), (speed_n, spread_n) = lat_faces
+        flux_s = speed_s * (south + centre) - spread_s * (centre - south)
+        flux_n = speed_n * (centre + north) - spread_n * (north - centre)
+        return -(east(flux) - flux) - (flux_n - flux_s)
+
+    place = level_set * z.levels + level
+    rise_low = jnp.where(place > 0, diffusivity, 0.0).astype(f32)
+    rise_high = jnp.where(place + 1 < lev_total, diffusivity, 0.0).astype(f32)
+
+    def vertical(x, below, above):
+        down = jnp.where(level == 0, below, pltpu.roll(x, 1, 0))
+        up = jnp.where(level == z.levels - 1, above, pltpu.roll(x, z.block - 1, 0))
+        return rise_high * (up - x) - rise_low * (x - down)
+
+    got = [by_parity("wave", first_ref[j], second_ref[j]) for j in range(z.rows + 1)]
+    flags_inner = pair(own_ref[z.rows], own_ref[z.rows + 1])
+    flags_outer = pair(got[z.rows][1], got[z.rows][0])
+    centre = pair(own_ref[0], own_ref[1])
+    inner, outer = around(pair(got[0][0], got[1][0]), centre, pair(got[0][1], got[1][1]))
+    merid_inner, merid_outer = around(*merid)
+    face_inner = zonal_face(zonal[0], flags_inner)
+    face_outer = zonal_face(zonal[1], flags_outer)
+    lat_inner = lat_faces(merid_inner, 0, 1)
+    lat_outer = lat_faces(merid_outer, z.rows, -1)
+    below, above = by_parity("lev", lev_first_ref[...], lev_second_ref[...])
+
+    def halo_tile(rows, first, second):
+        return jnp.where(low, rows[first : first + 1], rows[second : second + 1])
+
+    s_inner = horizontal(inner, face_inner, lat_inner) + vertical(
+        centre, halo_tile(below, 1, 2), halo_tile(above, 1, 2)
+    )
+    s_outer = horizontal(outer, face_outer, lat_outer) + vertical(
+        outer[1], halo_tile(below, 3, 0), halo_tile(above, 3, 0)
+    )
+    turn_inner, turn_outer = swap(s_inner), swap(s_outer)
+    rows = (
+        jnp.where(low, turn_outer, turn_inner),
+        s_inner,
+        jnp.where(low, turn_inner, turn_outer),
+    )
+    change = s_inner + 0.5 * (
+        horizontal(rows, face_inner, lat_inner) + vertical(s_inner, 0.0, 0.0)
+    )
     tops, lows = [], []
-    for j in range(z.rows):
-        q = tracer[halo + j]
-        change = 0.5 * q + 0.5 * (section_one[1 + j] + section_two[j]) - q
-        top = change.astype(jnp.bfloat16)
-        tops.append(top.astype(jnp.float32))
-        lows.append(change - tops[-1])
+    for x in (change, s_inner):
+        top = x.astype(jnp.bfloat16).astype(f32)
+        tops.append(top)
+        lows.append(x - top)
     both = jnp.concatenate(tops + lows, axis=0).astype(jnp.bfloat16)
     projected = contract(both, table_ref[...], ((1,), (1,)))
-    count = z.rows * z.deep
-    projected = projected[:count] + projected[count:]
-    scaled = projected * scale_ref[:, :1]
-    top = scaled.astype(jnp.bfloat16)
-    low = (scaled - top.astype(jnp.float32)).astype(jnp.bfloat16)
-    both = jnp.concatenate([top, low], axis=0)
+    count = 2 * z.block
+    scale = jnp.concatenate([scale_ref[:, :1]] * 2, axis=0)
+    projected = (projected[:count] + projected[count:]) * scale
+    top = projected.astype(jnp.bfloat16)
+    both = jnp.concatenate([top, (projected - top.astype(f32)).astype(jnp.bfloat16)], axis=0)
     for b in range(z.bands):
         first = b * z.slot_pad
         block = jnp.concatenate(
@@ -390,13 +394,30 @@
         )
         block = contract(block, spread_ref[...], ((1,), (0,)))
         block = block[:count] + block[count:]
-        for j in range(z.rows):
-            mine = block[j * z.deep : (j + 1) * z.deep] * pick_ref[...]
-            reply_ref[b, j : j + 1] = jnp.sum(mine, axis=0, keepdims=True)
+        mine, edge = block[: z.block], block[z.block :]
+
+        def by_row(x):
+            return jnp.concatenate(
+                [
+                    jnp.sum(x[j * z.levels : (j + 1) * z.levels], axis=0, keepdims=True)
+                    for j in range(z.rows)
+                ],
+                axis=0,
+            )
+
+        mine = by_row(mine * pick_ref[0])
+        to_above, to_below = by_row(edge * pick_ref[1]), by_row(edge * pick_ref[2])
+        for l in range(z.sets):
+            reply = jnp.where(level_set == l, mine, 0.0)
+            reply = jnp.where(level_set == l - 1, to_above, reply)
+            reply_ref[b * z.sets + l] = jnp.where(level_set == l + 1, to_below, reply)
 
 
 def analysis_kernel(z, arrived_ref, live_ref, out_ref, turned_ref):
-    arrived = arrived_ref[...].reshape(z.lats, z.reply)
+    arrived = arrived_ref[:, 0]
+    for l in range(1, z.sets):
+        arrived = arrived + arrived_ref[:, l]
+    arrived = arrived.reshape(z.lats, z.reply)
     top = arrived.astype(jnp.bfloat16).astype(jnp.float32)
     turned = jnp.concatenate([top, arrived - top], axis=0)
     width = turned_ref.shape[2]
@@ -442,9 +463,9 @@
         in_specs=[any_spec] * len(fetched),
         out_specs=tuple(vmem(6)),
         out_shape=(
-            jax.ShapeDtypeStruct((z.bands * z.sets, z.slot_pad, z.piece), bf16),
+            jax.ShapeDtypeStruct((z.bands, z.slot_pad, z.piece), bf16),
             jax.ShapeDtypeStruct(legendre.shape, bf16),
-            jax.ShapeDtypeStruct((z.rows * z.deep, lanes), f32),
+            jax.ShapeDtypeStruct((z.block, lanes), f32),
             jax.ShapeDtypeStruct((2 * z.rows, z.levels, z.lon), f32),
             edge_shape,
             edge_shape,
@@ -462,7 +483,7 @@
     first_pairs, second_pairs = swaps("wave")
     wave_first = lax.ppermute(to_first, "wave", first_pairs)
     wave_second = lax.ppermute(to_second, "wave", second_pairs)
-    arrived = lax.all_to_all(pieces, ("wave", "lev"), split_axis=0, concat_axis=0, tiled=True)
+    arrived = lax.all_to_all(pieces, "wave", split_axis=0, concat_axis=0, tiled=True)
     padded_wave = jnp.pad(
         slot_wave.reshape(z.bands, z.slots), ((0, 0), (0, z.slot_pad - z.slots))
     ).reshape(-1, 1)
@@ -474,7 +495,7 @@
         out_shape=jax.ShapeDtypeStruct((2 * z.bands * z.slot_pad, z.lon), bf16),
         compiler_params=params(table_bytes),
     )(padded_wave)
-    up_shape = jax.ShapeDtypeStruct((3 * z.rows + 2, z.lon), f32)
+    up_shape = jax.ShapeDtypeStruct((z.rows + 2, z.lon), f32)
     up, down = pl.pallas_call(
         functools.partial(edge_kernel, z),
         name="edges",
@@ -491,14 +512,10 @@
         name="grid",
         in_specs=vmem(11),
         out_specs=vmem(1)[0],
-        out_shape=jax.ShapeDtypeStruct((z.bands, z.rows, z.reply), f32),
-        scratch_shapes=[
-            pltpu.VMEM((z.window, z.deep, z.lon), f32),
-            pltpu.VMEM((z.rows + 2, z.deep, z.lon), f32),
-        ],
+        out_shape=jax.ShapeDtypeStruct((z.bands * z.sets, z.rows, z.reply), f32),
         compiler_params=params(3 * table_bytes, 24 * nbytes(tracer), fan),
     )(
-        arrived.reshape(z.bands, z.sets, z.slot_pad, z.piece),
+        arrived,
         unpack_constant(z),
         table,
         own,
@@ -509,7 +526,7 @@
         *reply_constants(z),
         scale,
     )
-    returned = lax.all_to_all(reply, "wave", split_axis=0, concat_axis=0, tiled=True)
+    returned = lax.all_to_all(reply, ("wave", "lev"), split_axis=0, concat_axis=0, tiled=True)
     width = math.gcd(2 * z.lats, lanes)
     return pl.pallas_call(
         functools.partial(analysis_kernel, z),
@@ -519,7 +536,7 @@
         out_shape=jax.ShapeDtypeStruct((z.slots, 2, z.levels, z.degrees), f32),
         scratch_shapes=[pltpu.VMEM((2 * z.lats // width, z.reply, width), f32)],
         compiler_params=params(nbytes(spectra, f32), nbytes(legendre)),
-    )(returned, live)
+    )(returned.reshape(z.bands, z.sets, z.rows, z.reply), live)
 
 
 def solution(mesh):

time: 38.9 us -> 36.1 us (0.928)
  the two profiles are of different devices: /device:TPU:2 before, /device:TPU:0 now
where the time goes in v5:
time: 36.1 us; the launch traced here: 35.8 us
  starting transfers between devices  12 us (33%)
  blocking collectives  11.9 us (33%)
  Pallas kernels  7.21 us (20%)
  waiting for transfers between devices  4.4 us (12%)
    all_to_all x1, blocking collectives, on_device(): lax.all_to_all(reply, ('wave', 'lev'), split_axis=0, concat_axis=0, tiled...  11.9 us
    all_to_all x1, starting transfers between devices, on_device(): lax.all_to_all(pieces, 'wave', split_axis=0, concat_axis=0, tiled=True)  7.59 us
    all_to_all x1, waiting for transfers between devices, on_device(): lax.all_to_all(pieces, 'wave', split_axis=0, concat_axis=0, tiled=True)  4.39 us
    ppermute x1, starting transfers between devices, on_device(): wave_first = lax.ppermute(to_first, 'wave', first_pairs)  3.06 us
    pallas_call x1, Pallas kernels, on_device(): pl.pallas_call(functools.partial(legendre_kernel, z), name='legendre', in...  3.05 us
    pallas_call x1, Pallas kernels, on_device(): pl.pallas_call(functools.partial(grid_kernel, z), name='grid', in_specs=v...  1.64 us
    pallas_call x1, Pallas kernels, on_device(): pl.pallas_call(functools.partial(table_kernel, z), name='table', in_specs...  1.26 us
    pallas_call x1, Pallas kernels, on_device(): pl.pallas_call(functools.partial(analysis_kernel, z), name='analysis', in...  1.2 us
  transfers between devices with their start and end apart: 5, of which 1 were waited for; matrix products, arithmetic and copies ran while one was open for 0% of the time, Pallas kernels for 4%

profile of v5, /device:TPU:0, one launch (start us, length us, event | category | flops | bytes accessed | tf_op | source)
XLA Modules:
  0.0 35.8 jit_solution(732450482003136614)
XLA Ops:
  0.0 0.0 copy-start.3
  0.0 3.0 %legendre.1 = (bf16[8,16,128]{2,1,0:T(8,128)(2,1)}, bf16[13,16,1280]{2,1,0:T(8,128)(2,1)S(1)}, f32[8,128]{1,0:T(8,128)S(1)}, f32[4,4,2560]{2,1,0:T(4,128)S(1)}, ...) custom-call(s32[104]{0:T(128)} %wave_hbm.1, f32[2]{0:T(128)} %weight_hbm.1, bf16[13,4,4,1280]{3,2,1,0:T(4,128)(2,1)} %spectra_hbm.1, ...), custom_call_target="tpu_custom_call" | custom-call | tf_op jit(solution)/shard_map/legendre/pallas_call | solution.py:460
  3.1 0.0 copy-start
  3.1 0.0 copy-start.1
  3.1 0.0 copy-start.2
  3.1 3.1 %collective-permute-start = (f32[3,4,2560]{2,1,0:T(4,128)S(1)}, f32[3,4,2560]{2,1,0:T(4,128)S(1)}, u32[]{:S(2)}, u32[]{:S(2)}) collective-permute-start(f32[3,4,2560]{2,1,0:T(4,128)S(1)} %get-tuple-element.15), channel_id=1, source_target_pairs={{0,4},{8,12},{16,20},{24,28},{4,0},{12,8},{20,16},{28,24},{1,5},{9... | collective-permute-start | bytes 368648 | tf_op jit(solution)/shard_map/ppermute | solution.py:484
  6.2 0.7 %collective-permute-start.1 = (f32[3,4,2560]{2,1,0:T(4,128)S(1)}, f32[3,4,2560]{2,1,0:T(4,128)S(1)}, u32[]{:S(2)}, u32[]{:S(2)}) collective-permute-start(f32[3,4,2560]{2,1,0:T(4,128)S(1)} %get-tuple-element.16), channel_id=1, source_target_pairs={{4,8},{12,16},{20,24},{8,4},{16,12},{24,20},{5,9},{13,17},{21,25},... | collective-permute-start | bytes 368648 | tf_op jit(solution)/shard_map/ppermute | solution.py:485
  6.8 7.6 %all-to-all-start = ((bf16[8,16,128]{2,1,0:T(8,128)(2,1)}), bf16[8,16,128]{2,1,0:T(8,128)(2,1)S(1)}, u32[]{:S(2)}, u32[]{:S(2)}) async-start(bf16[8,16,128]{2,1,0:T(8,128)(2,1)} %get-tuple-element.13), calls=%async_computation | async-start | bytes 65536 | tf_op jit(solution)/shard_map/all_to_all | solution.py:486
  14.4 0.0 collective-permute-done.first_ref
  14.4 0.0 collective-permute-done.1.second_ref
  14.4 0.1 edges.1
  14.5 0.1 collective-permute-start.2
  14.6 0.7 %collective-permute-start.3 = (f32[4,2560]{1,0:T(4,128)S(1)}, f32[4,2560]{1,0:T(4,128)S(1)}, u32[]{:S(2)}, u32[]{:S(2)}) collective-permute-start(f32[4,2560]{1,0:T(4,128)S(1)} %get-tuple-element.18), channel_id=1, source_target_pairs={{1,2},{2,1},{5,6},{6,5},{9,10},{10,9},{13,14},{14,13},{17,18},{18,... | collective-permute-start | bytes 122888 | tf_op jit(solution)/shard_map/ppermute | solution.py:509
  15.3 0.0 copy-done.3
  15.3 0.1 reshape.9
  15.4 0.1 reshape.12.wave_ref
  15.4 1.3 %table.1.table_ref = bf16[256,2560]{1,0:T(8,128)(2,1)S(1)} custom-call(s32[128,1]{1,0:T(8,128)S(1)} %reshape.12.wave_ref), custom_call_target="tpu_custom_call" | custom-call | tf_op jit(solution)/shard_map/table/pallas_call | solution.py:490
  16.7 4.4 %all-to-all-done.arrived_ref = bf16[8,16,128]{2,1,0:T(8,128)(2,1)S(1)} async-done(((bf16[8,16,128]{2,1,0:T(8,128)(2,1)}), bf16[8,16,128]{2,1,0:T(8,128)(2,1)S(1)}, u32[]{:S(2)}, u32[]{:S(2)}) %all-to-all-start) | async-done | bytes 32800 | tf_op jit(solution)/shard_map/all_to_all | solution.py:486
  21.1 0.0 collective-permute-done.2.lev_first_ref
  21.1 0.0 collective-permute-done.3.lev_second_ref
  21.1 0.0 copy-done
  21.1 0.0 copy-done.1
  21.1 0.0 copy-done.2
  21.1 1.6 %grid.1 = f32[32,2,128]{2,1,0:T(2,128)S(1)} custom-call(bf16[8,16,128]{2,1,0:T(8,128)(2,1)S(1)} %all-to-all-done.arrived_ref, bf16[96,128]{1,0:T(8,128)(2,1)S(1)} %copy-done, bf16[256,2560]{1,0:T(8,128)(2,1)S(1)} %table.1.table_ref, f32[4,4,2560]{2,1,0:T(4,128)S(1)} %get-tuple-element.14.own_ref, f32[3,4,2560]{2,1,0:T(4,128)S(1)} %collective-permute-done.first_ref, ...), custom_call_target="tpu_custom_call" | custom-call | tf_op jit(solution)/shard_map/grid/pallas_call | solution.py:510
  22.8 11.9 %all_to_all.10 = f32[32,2,128]{2,1,0:T(2,128)S(1)} all-to-all(f32[32,2,128]{2,1,0:T(2,128)S(1)} %grid.1), channel_id=1, replica_groups=mesh['wave'=8,'lev'=4] {'wave','lev'}, dimensions={0} | all-to-all | bytes 65536 | tf_op jit(solution)/shard_map/all_to_all | solution.py:529
  34.6 1.2 %analysis.1 = f32[13,2,4,1280]{3,2,1,0:T(4,128)} custom-call(f32[8,4,2,128]{3,2,1,0:T(2,128)S(1)} %bitcast.1, bf16[13,16,1280]{2,1,0:T(8,128)(2,1)S(1)} %get-tuple-element.20.live_ref), custom_call_target="tpu_custom_call" | custom-call | tf_op jit(solution)/shard_map/analysis/pallas_call | solution.py:531
  (1 shorter events, 0.0 us)
Async XLA Ops:
  0.0 15.3 %copy-start.3 = (s32[104]{0:T(128)S(1)}, s32[104]{0:T(128)}, u32[]{:S(2)}) copy-start(s32[104]{0:T(128)} %wave_hbm.1) | copy-start | bytes 1252
  3.1 18.1 %copy-start = (bf16[96,128]{1,0:T(8,128)(2,1)S(1)}, bf16[96,128]{1,0:T(8,128)(2,1)}, u32[]{:S(2)}) copy-start(bf16[96,128]{1,0:T(8,128)(2,1)} %constant.8.clone.unpack_ref) | copy-start | bytes 73732
  3.1 18.0 %copy-start.1 = (f32[3,8,128]{2,1,0:T(8,128)S(1)}, f32[3,8,128]{2,1,0:T(8,128)}, u32[]{:S(2)}) copy-start(f32[3,8,128]{2,1,0:T(8,128)} %constant.10.clone.pick_ref) | copy-start | bytes 36868
  3.1 18.0 %copy-start.2 = (bf16[32,128]{1,0:T(8,128)(2,1)S(1)}, bf16[32,128]{1,0:T(8,128)(2,1)}, u32[]{:S(2)}) copy-start(bf16[32,128]{1,0:T(8,128)(2,1)} %constant.9.clone.spread_ref) | copy-start | bytes 24580
  3.1 11.3 %collective-permute-start = (f32[3,4,2560]{2,1,0:T(4,128)S(1)}, f32[3,4,2560]{2,1,0:T(4,128)S(1)}, u32[]{:S(2)}, u32[]{:S(2)}) collective-permute-start(f32[3,4,2560]{2,1,0:T(4,128)S(1)} %get-tuple-element.15), channel_id=1, source_target_pairs={{0,4},{8,12},{16,20},{24,28},{4,0},{12,8},{20,16},{28,24},{1,5},{9... | collective-permute-start | bytes 368648 | tf_op jit(solution)/shard_map/ppermute | solution.py:484
  6.2 8.3 %collective-permute-start.1 = (f32[3,4,2560]{2,1,0:T(4,128)S(1)}, f32[3,4,2560]{2,1,0:T(4,128)S(1)}, u32[]{:S(2)}, u32[]{:S(2)}) collective-permute-start(f32[3,4,2560]{2,1,0:T(4,128)S(1)} %get-tuple-element.16), channel_id=1, source_target_pairs={{4,8},{12,16},{20,24},{8,4},{16,12},{24,20},{5,9},{13,17},{21,25},... | collective-permute-start | bytes 368648 | tf_op jit(solution)/shard_map/ppermute | solution.py:485
  6.8 14.3 %all-to-all-start = ((bf16[8,16,128]{2,1,0:T(8,128)(2,1)}), bf16[8,16,128]{2,1,0:T(8,128)(2,1)S(1)}, u32[]{:S(2)}, u32[]{:S(2)}) async-start(bf16[8,16,128]{2,1,0:T(8,128)(2,1)} %get-tuple-element.13), calls=%async_computation | async-start | bytes 65536 | tf_op jit(solution)/shard_map/all_to_all | solution.py:486
  14.5 6.6 %collective-permute-start.2 = (f32[4,2560]{1,0:T(4,128)S(1)}, f32[4,2560]{1,0:T(4,128)S(1)}, u32[]{:S(2)}, u32[]{:S(2)}) collective-permute-start(f32[4,2560]{1,0:T(4,128)S(1)} %get-tuple-element.17), channel_id=1, source_target_pairs={{0,1},{2,3},{1,0},{3,2},{4,5},{6,7},{5,4},{7,6},{8,9},{10,11},{9,8... | collective-permute-start | bytes 122888 | tf_op jit(solution)/shard_map/ppermute | solution.py:508
  14.6 6.5 %collective-permute-start.3 = (f32[4,2560]{1,0:T(4,128)S(1)}, f32[4,2560]{1,0:T(4,128)S(1)}, u32[]{:S(2)}, u32[]{:S(2)}) collective-permute-start(f32[4,2560]{1,0:T(4,128)S(1)} %get-tuple-element.18), channel_id=1, source_target_pairs={{1,2},{2,1},{5,6},{6,5},{9,10},{10,9},{13,14},{14,13},{17,18},{18,... | collective-permute-start | bytes 122888 | tf_op jit(solution)/shard_map/ppermute | solution.py:509

commit v6 on v4

--- a/solution.py
+++ b/solution.py
@@ -14,6 +14,7 @@
 halo = 2
 lanes = 128
 packed_rows = 16
+store_slots = 4
 
 
 def round_up(value, step):
@@ -38,6 +39,7 @@
         self.lats = legendre.shape[1]
         self.rows, self.lon = tracer.shape[1:]
         self.bands, self.sets = bands, sets
+        self.order = [(bands // 2 + 1 - b) % bands for b in range(bands)]
         self.slot_pad = round_up(self.slots, packed_rows)
         self.window = self.rows + 2 * halo
         self.deep = self.levels + 2 * halo
@@ -383,26 +385,32 @@
     top = scaled.astype(jnp.bfloat16)
     low = (scaled - top.astype(jnp.float32)).astype(jnp.bfloat16)
     both = jnp.concatenate([top, low], axis=0)
+
+    def of_band(b):
+        first = b * z.slot_pad
+        halves = [both[:, p * height + first : p * height + first + z.slot_pad] for p in range(2)]
+        return jnp.concatenate(halves, axis=1)
+
+    spread = jnp.concatenate([of_band(b) for b in range(z.bands)], axis=0)
+    spread = contract(spread, spread_ref[...], ((1,), (0,)))
     for b in range(z.bands):
-        first = b * z.slot_pad
-        block = jnp.concatenate(
-            [both[:, p * height + first : p * height + first + z.slot_pad] for p in range(2)], axis=1
-        )
-        block = contract(block, spread_ref[...], ((1,), (0,)))
+        block = spread[2 * b * count : 2 * (b + 1) * count]
         block = block[:count] + block[count:]
         for j in range(z.rows):
             mine = block[j * z.deep : (j + 1) * z.deep] * pick_ref[...]
-            reply_ref[b, j : j + 1] = jnp.sum(mine, axis=0, keepdims=True)
-
-
-def analysis_kernel(z, arrived_ref, live_ref, out_ref, turned_ref):
-    arrived = arrived_ref[...].reshape(z.lats, z.reply)
+            reply_ref[z.order.index(b), j : j + 1] = jnp.sum(mine, axis=0, keepdims=True)
+
+
+def analysis_kernel(z, arrived_ref, live_ref, out_hbm, turned_ref, out_ref, sems):
+    arrived = [arrived_ref[z.order.index(b)] for b in range(z.bands)]
+    arrived = jnp.concatenate(arrived, axis=0)
     top = arrived.astype(jnp.bfloat16).astype(jnp.float32)
     turned = jnp.concatenate([top, arrived - top], axis=0)
     width = turned_ref.shape[2]
     for c in range(turned_ref.shape[0]):
         turned_ref[c] = turned[c * width : (c + 1) * width].T
     height = 2 * z.levels
+    stores = []
     for s in range(z.slots):
         left = [
             turned_ref[c, pl.ds(s, height, stride=z.slot_pad), :].astype(jnp.bfloat16)
@@ -411,6 +419,15 @@
         left = jnp.concatenate(left, axis=1)
         right = jnp.concatenate([live_ref[s], live_ref[s]], axis=0)
         out_ref[s] = contract(left, right, ((1,), (0,))).reshape(2, z.levels, z.degrees)
+        if s % store_slots == store_slots - 1 or s == z.slots - 1:
+            first = s // store_slots * store_slots
+            part = pl.ds(first, s + 1 - first)
+            stores.append(
+                pltpu.make_async_copy(out_ref.at[part], out_hbm.at[part], sems.at[len(stores)])
+            )
+            stores[-1].start()
+    for store in stores:
+        store.wait()
 
 
 def in_hbm(array):
@@ -509,15 +526,21 @@
         *reply_constants(z),
         scale,
     )
-    returned = lax.all_to_all(reply, "wave", split_axis=0, concat_axis=0, tiled=True)
+    returned = lax.all_to_all(
+        reply, "wave", split_axis=0, concat_axis=0, axis_index_groups=[z.order], tiled=True
+    )
     width = math.gcd(2 * z.lats, lanes)
     return pl.pallas_call(
         functools.partial(analysis_kernel, z),
         name="analysis",
         in_specs=vmem(2),
-        out_specs=vmem(1)[0],
+        out_specs=any_spec,
         out_shape=jax.ShapeDtypeStruct((z.slots, 2, z.levels, z.degrees), f32),
-        scratch_shapes=[pltpu.VMEM((2 * z.lats // width, z.reply, width), f32)],
+        scratch_shapes=[
+            pltpu.VMEM((2 * z.lats // width, z.reply, width), f32),
+            pltpu.VMEM((z.slots, 2, z.levels, z.degrees), f32),
+            pltpu.SemaphoreType.DMA((-(-z.slots // store_slots),)),
+        ],
         compiler_params=params(nbytes(spectra, f32), nbytes(legendre)),
     )(returned, live)
 

time: 38.9 us -> 37 us (0.951)
  blocking collectives: 12.4 us -> 10.6 us
    all_to_all x1, blocking collectives: 12.4 us -> 10.6 us  [on_device(): lax.all_to_all(reply, 'wave', split_axis=0, concat_axis=0, axis_index_gro...]
where the time goes in v6:
time: 37 us; the launch traced here: 36.7 us
  starting transfers between devices  11.1 us (30%)
  blocking collectives  10.6 us (29%)
  Pallas kernels  7.4 us (20%)
  waiting for transfers between devices  7.29 us (20%)
    all_to_all x1, blocking collectives, on_device(): lax.all_to_all(reply, 'wave', split_axis=0, concat_axis=0, axis_index_gro...  10.6 us
    all_to_all x1, starting transfers between devices, on_device(): lax.all_to_all(pieces, ('wave', 'lev'), split_axis=0, concat_axis=0, tile...  6.13 us
    ppermute x1, waiting for transfers between devices, on_device(): wave_first = lax.ppermute(to_first, 'wave', first_pairs)  5.74 us
    pallas_call x1, Pallas kernels, on_device(): pl.pallas_call(functools.partial(legendre_kernel, z), name='legendre', in...  3.09 us
    ppermute x1, starting transfers between devices, on_device(): lev_second = lax.ppermute(down, 'lev', second_pairs)  2.75 us
    pallas_call x1, Pallas kernels, on_device(): pl.pallas_call(functools.partial(grid_kernel, z), name='grid', in_specs=v...  1.83 us
    ppermute x1, waiting for transfers between devices, on_device(): lev_second = lax.ppermute(down, 'lev', second_pairs)  1.54 us
    ppermute x1, starting transfers between devices, on_device(): wave_first = lax.ppermute(to_first, 'wave', first_pairs)  1.53 us
  transfers between devices with their start and end apart: 5, of which 2 were waited for; matrix products, arithmetic and copies ran while one was open for 0% of the time, Pallas kernels for 4%

profile of v6, /device:TPU:2, one launch (start us, length us, event | category | flops | bytes accessed | tf_op | source)
XLA Modules:
  0.0 36.7 jit_solution(9293507915114566839)
XLA Ops:
  0.0 0.0 copy-start.3
  0.0 3.1 %legendre.1 = (bf16[32,16,128]{2,1,0:T(8,128)(2,1)}, bf16[13,16,1280]{2,1,0:T(8,128)(2,1)S(1)}, f32[16,128]{1,0:T(8,128)S(1)}, f32[4,4,2560]{2,1,0:T(4,128)S(1)}...) custom-call(s32[104]{0:T(128)} %wave_hbm.1, f32[2]{0:T(128)} %weight_hbm.1, bf16[13,4,4,1280]{3,2,1,0:T(4,128)(2,1)} %spectra_hbm.1, ...), custom_call_target="tpu_custom_call" | custom-call | tf_op jit(solution)/shard_map/legendre/pallas_call | solution.py:456
  3.1 0.0 copy-start
  3.1 0.0 copy-start.1
  3.1 0.0 copy-start.2
  3.1 6.1 %all-to-all-start = ((bf16[32,16,128]{2,1,0:T(8,128)(2,1)}), bf16[32,16,128]{2,1,0:T(8,128)(2,1)S(1)}, u32[]{:S(2)}, u32[]{:S(2)}) async-start(bf16[32,16,128]{2,1,0:T(8,128)(2,1)} %get-tuple-element.13), calls=%async_computation | async-start | bytes 262144 | tf_op jit(solution)/shard_map/all_to_all | solution.py:482
  9.3 1.5 %collective-permute-start = (f32[3,4,2560]{2,1,0:T(4,128)S(1)}, f32[3,4,2560]{2,1,0:T(4,128)S(1)}, u32[]{:S(2)}, u32[]{:S(2)}) collective-permute-start(f32[3,4,2560]{2,1,0:T(4,128)S(1)} %get-tuple-element.15), channel_id=1, source_target_pairs={{0,4},{8,12},{16,20},{24,28},{4,0},{12,8},{20,16},{28,24},{1,5},{9... | collective-permute-start | bytes 368648 | tf_op jit(solution)/shard_map/ppermute | solution.py:480
  10.8 0.7 %collective-permute-start.1 = (f32[3,4,2560]{2,1,0:T(4,128)S(1)}, f32[3,4,2560]{2,1,0:T(4,128)S(1)}, u32[]{:S(2)}, u32[]{:S(2)}) collective-permute-start(f32[3,4,2560]{2,1,0:T(4,128)S(1)} %get-tuple-element.16), channel_id=1, source_target_pairs={{4,8},{12,16},{20,24},{8,4},{16,12},{24,20},{5,9},{13,17},{21,25},... | collective-permute-start | bytes 368648 | tf_op jit(solution)/shard_map/ppermute | solution.py:481
  11.5 5.7 %collective-permute-done.first_ref = f32[3,4,2560]{2,1,0:T(4,128)S(1)} collective-permute-done((f32[3,4,2560]{2,1,0:T(4,128)S(1)}, f32[3,4,2560]{2,1,0:T(4,128)S(1)}, u32[]{:S(2)}, u32[]{:S(2)}) %collective-permute-start) | collective-permute-done | bytes 122912 | tf_op jit(solution)/shard_map/ppermute | solution.py:480
  17.2 0.0 collective-permute-done.1.second_ref
  17.2 0.1 edges.1
  17.3 0.1 collective-permute-start.2
  17.4 2.7 %collective-permute-start.3 = (f32[8,2560]{1,0:T(8,128)S(1)}, f32[8,2560]{1,0:T(8,128)S(1)}, u32[]{:S(2)}, u32[]{:S(2)}) collective-permute-start(f32[8,2560]{1,0:T(8,128)S(1)} %get-tuple-element.18), channel_id=1, source_target_pairs={{1,2},{2,1},{5,6},{6,5},{9,10},{10,9},{13,14},{14,13},{17,18},{18,... | collective-permute-start | bytes 245768 | tf_op jit(solution)/shard_map/ppermute | solution.py:505
  20.2 0.0 copy-done.3
  20.2 0.1 reshape.10
  20.3 0.1 reshape.12.wave_ref
  20.4 1.3 %table.1.table_ref = bf16[256,2560]{1,0:T(8,128)(2,1)S(1)} custom-call(s32[128,1]{1,0:T(8,128)S(1)} %reshape.12.wave_ref), custom_call_target="tpu_custom_call" | custom-call | tf_op jit(solution)/shard_map/table/pallas_call | solution.py:486
  21.6 0.0 collective-permute-done.2.lev_first_ref
  21.6 1.5 %collective-permute-done.3.lev_second_ref = f32[8,2560]{1,0:T(8,128)S(1)} collective-permute-done((f32[8,2560]{1,0:T(8,128)S(1)}, f32[8,2560]{1,0:T(8,128)S(1)}, u32[]{:S(2)}, u32[]{:S(2)}) %collective-permute-start.3) | collective-permute-done | bytes 81952 | tf_op jit(solution)/shard_map/ppermute | solution.py:505
  23.2 0.0 all-to-all-done
  23.2 0.0 copy-done
  23.2 0.0 copy-done.1
  23.2 0.0 copy-done.2
  23.2 1.8 %grid.1 = f32[8,2,128]{2,1,0:T(2,128)S(1)} custom-call(bf16[8,4,16,128]{3,2,1,0:T(8,128)(2,1)S(1)} %bitcast.1, bf16[256,384]{1,0:T(8,128)(2,1)S(1)} %copy-done, bf16[256,2560]{1,0:T(8,128)(2,1)S(1)} %table.1.table_ref, f32[4,4,2560]{2,1,0:T(4,128)S(1)} %get-tuple-element.14.own_ref, f32[3,4,2560]{2,1,0:T(4,128)S(1)} %collective-permute-done.first_ref, ...), custom_call_target="tpu_custom_call" | custom-call | tf_op jit(solution)/shard_map/grid/pallas_call | solution.py:506
  25.0 10.6 %all_to_all.10.arrived_ref = f32[8,2,128]{2,1,0:T(2,128)S(1)} all-to-all(f32[8,2,128]{2,1,0:T(2,128)S(1)} %grid.1), channel_id=1, replica_groups={{20,16,12,8,4,0,28,24},{21,17,13,9,5,1,29,25},{22,18,14,10,6,2,30,26},{..., dimensions={0} | all-to-all | bytes 16384 | tf_op jit(solution)/shard_map/all_to_all | solution.py:529
  35.6 1.1 %analysis.1 = f32[13,2,4,1280]{3,2,1,0:T(4,128)} custom-call(f32[8,2,128]{2,1,0:T(2,128)S(1)} %all_to_all.10.arrived_ref, bf16[13,16,1280]{2,1,0:T(8,128)(2,1)S(1)} %get-tuple-element.20.live_ref), custom_call_target="tpu_custom_call" | custom-call | tf_op jit(solution)/shard_map/analysis/pallas_call | solution.py:533
  (1 shorter events, 0.0 us)
Async XLA Ops:
  0.0 20.2 %copy-start.3 = (s32[104]{0:T(128)S(1)}, s32[104]{0:T(128)}, u32[]{:S(2)}) copy-start(s32[104]{0:T(128)} %wave_hbm.1) | copy-start | bytes 1252
  3.1 20.1 %copy-start = (bf16[256,384]{1,0:T(8,128)(2,1)S(1)}, bf16[256,384]{1,0:T(8,128)(2,1)}, u32[]{:S(2)}) copy-start(bf16[256,384]{1,0:T(8,128)(2,1)} %constant.8.clone.unpack_ref) | copy-start | bytes 589828
  3.1 20.1 %copy-start.1 = (bf16[32,128]{1,0:T(8,128)(2,1)S(1)}, bf16[32,128]{1,0:T(8,128)(2,1)}, u32[]{:S(2)}) copy-start(bf16[32,128]{1,0:T(8,128)(2,1)} %constant.9.clone.spread_ref) | copy-start | bytes 24580
  3.1 20.1 %copy-start.2 = (f32[8,128]{1,0:T(8,128)S(1)}, f32[8,128]{1,0:T(8,128)}, u32[]{:S(2)}) copy-start(f32[8,128]{1,0:T(8,128)} %constant.10.clone.pick_ref) | copy-start | bytes 12292
  3.1 20.0 %all-to-all-start = ((bf16[32,16,128]{2,1,0:T(8,128)(2,1)}), bf16[32,16,128]{2,1,0:T(8,128)(2,1)S(1)}, u32[]{:S(2)}, u32[]{:S(2)}) async-start(bf16[32,16,128]{2,1,0:T(8,128)(2,1)} %get-tuple-element.13), calls=%async_computation | async-start | bytes 262144 | tf_op jit(solution)/shard_map/all_to_all | solution.py:482
  9.3 7.9 %collective-permute-start = (f32[3,4,2560]{2,1,0:T(4,128)S(1)}, f32[3,4,2560]{2,1,0:T(4,128)S(1)}, u32[]{:S(2)}, u32[]{:S(2)}) collective-permute-start(f32[3,4,2560]{2,1,0:T(4,128)S(1)} %get-tuple-element.15), channel_id=1, source_target_pairs={{0,4},{8,12},{16,20},{24,28},{4,0},{12,8},{20,16},{28,24},{1,5},{9... | collective-permute-start | bytes 368648 | tf_op jit(solution)/shard_map/ppermute | solution.py:480
  10.8 6.4 %collective-permute-start.1 = (f32[3,4,2560]{2,1,0:T(4,128)S(1)}, f32[3,4,2560]{2,1,0:T(4,128)S(1)}, u32[]{:S(2)}, u32[]{:S(2)}) collective-permute-start(f32[3,4,2560]{2,1,0:T(4,128)S(1)} %get-tuple-element.16), channel_id=1, source_target_pairs={{4,8},{12,16},{20,24},{8,4},{16,12},{24,20},{5,9},{13,17},{21,25},... | collective-permute-start | bytes 368648 | tf_op jit(solution)/shard_map/ppermute | solution.py:481
  17.3 4.3 %collective-permute-start.2 = (f32[8,2560]{1,0:T(8,128)S(1)}, f32[8,2560]{1,0:T(8,128)S(1)}, u32[]{:S(2)}, u32[]{:S(2)}) collective-permute-start(f32[8,2560]{1,0:T(8,128)S(1)} %get-tuple-element.17), channel_id=1, source_target_pairs={{0,1},{2,3},{1,0},{3,2},{4,5},{6,7},{5,4},{7,6},{8,9},{10,11},{9,8... | collective-permute-start | bytes 245768 | tf_op jit(solution)/shard_map/ppermute | solution.py:504
  17.4 5.8 %collective-permute-start.3 = (f32[8,2560]{1,0:T(8,128)S(1)}, f32[8,2560]{1,0:T(8,128)S(1)}, u32[]{:S(2)}, u32[]{:S(2)}) collective-permute-start(f32[8,2560]{1,0:T(8,128)S(1)} %get-tuple-element.18), channel_id=1, source_target_pairs={{1,2},{2,1},{5,6},{6,5},{9,10},{10,9},{13,14},{14,13},{17,18},{18,... | collective-permute-start | bytes 245768 | tf_op jit(solution)/shard_map/ppermute | solution.py:505

commit v7 on v6

--- a/solution.py
+++ b/solution.py
@@ -123,22 +123,19 @@
             )
         )
     ]
-    fetches = []
-    for g, (first, last) in enumerate(groups):
-        part = pl.ds(first, last - first)
-        fetches.append(
-            [
-                pltpu.make_async_copy(hbm.at[part], ref.at[part], sems.at[4 + a, g])
-                for a, (hbm, ref) in enumerate(
-                    (
-                        (legendre_hbm, legendre_ref),
-                        (derivative_hbm, derivative_ref),
-                        (spectra_hbm, spectra_ref),
-                    )
+    fetches = [
+        [
+            pltpu.make_async_copy(hbm, ref, sems.at[4 + a, 0])
+            for a, (hbm, ref) in enumerate(
+                (
+                    (spectra_hbm, spectra_ref),
+                    (legendre_hbm, legendre_ref),
+                    (derivative_hbm, derivative_ref),
                 )
-            ]
-        )
-    for copies in [whole[:2], *fetches, whole[2:]]:
+            )
+        ]
+    ] + [[] for _ in groups[1:]]
+    for copies in [*fetches, whole]:
         for copy in copies:
             copy.start()
     base = lax.axis_index("wave") * z.slots
@@ -201,7 +198,7 @@
         at = b * z.rows * z.unit
         piece = rows[:, at : at + z.piece].astype(jnp.bfloat16)
         for l in range(z.sets):
-            pieces_ref[b * z.sets + l] = piece
+            pieces_ref[z.bands * z.sets - 1 - (b * z.sets + l)] = piece
 
     even = lax.axis_index("wave") % 2 == 0
     whole[2].wait()
@@ -304,7 +301,8 @@
     height = z.bands * z.slot_pad
 
     def from_set(index):
-        return arrived_ref[:, index].reshape(height, z.piece)
+        blocks = [arrived_ref[z.bands - 1 - b, z.sets - 1 - index] for b in range(z.bands)]
+        return jnp.concatenate(blocks, axis=0)
 
     blocks = jnp.concatenate(
         [
@@ -479,7 +477,14 @@
     first_pairs, second_pairs = swaps("wave")
     wave_first = lax.ppermute(to_first, "wave", first_pairs)
     wave_second = lax.ppermute(to_second, "wave", second_pairs)
-    arrived = lax.all_to_all(pieces, ("wave", "lev"), split_axis=0, concat_axis=0, tiled=True)
+    arrived = lax.all_to_all(
+        pieces,
+        ("wave", "lev"),
+        split_axis=0,
+        concat_axis=0,
+        axis_index_groups=[list(range(z.bands * z.sets))[::-1]],
+        tiled=True,
+    )
     padded_wave = jnp.pad(
         slot_wave.reshape(z.bands, z.slots), ((0, 0), (0, z.slot_pad - z.slots))
     ).reshape(-1, 1)

time: 37 us -> 36.9 us (level)
  no operation moved by 1% of the time
where the time goes in v7:
time: 36.9 us; the launch traced here: 36.6 us
  starting transfers between devices  11.1 us (30%)
  blocking collectives  10.5 us (28%)
  waiting for transfers between devices  7.46 us (20%)
  Pallas kernels  7.29 us (20%)
    all_to_all x1, blocking collectives, on_device(): lax.all_to_all(reply, 'wave', split_axis=0, concat_axis=0, axis_index_gro...  10.5 us
    all_to_all x1, starting transfers between devices, on_device(): lax.all_to_all(pieces, ('wave', 'lev'), split_axis=0, concat_axis=0, axis...  6.13 us
    ppermute x1, waiting for transfers between devices, on_device(): wave_first = lax.ppermute(to_first, 'wave', first_pairs)  5.83 us
    pallas_call x1, Pallas kernels, on_device(): pl.pallas_call(functools.partial(legendre_kernel, z), name='legendre', in...  2.98 us
    ppermute x1, starting transfers between devices, on_device(): lev_second = lax.ppermute(down, 'lev', second_pairs)  2.66 us
    pallas_call x1, Pallas kernels, on_device(): pl.pallas_call(functools.partial(grid_kernel, z), name='grid', in_specs=v...  1.82 us
    ppermute x1, waiting for transfers between devices, on_device(): lev_second = lax.ppermute(down, 'lev', second_pairs)  1.62 us
    ppermute x1, starting transfers between devices, on_device(): wave_first = lax.ppermute(to_first, 'wave', first_pairs)  1.53 us
  transfers between devices with their start and end apart: 5, of which 2 were waited for; matrix products, arithmetic and copies ran while one was open for 0% of the time, Pallas kernels for 4%

profile of v7, /device:TPU:2, one launch (start us, length us, event | category | flops | bytes accessed | tf_op | source)
XLA Modules:
  0.0 36.6 jit_solution(12223028659365492185)
XLA Ops:
  0.0 0.0 copy-start.3
  0.0 3.0 %legendre.1 = (bf16[32,16,128]{2,1,0:T(8,128)(2,1)}, bf16[13,16,1280]{2,1,0:T(8,128)(2,1)S(1)}, f32[16,128]{1,0:T(8,128)S(1)}, f32[4,4,2560]{2,1,0:T(4,128)S(1)}...) custom-call(s32[104]{0:T(128)} %wave_hbm.1, f32[2]{0:T(128)} %weight_hbm.1, bf16[13,4,4,1280]{3,2,1,0:T(4,128)(2,1)} %spectra_hbm.1, ...), custom_call_target="tpu_custom_call" | custom-call | tf_op jit(solution)/shard_map/legendre/pallas_call | solution.py:454
  3.0 0.0 copy-start
  3.0 0.0 copy-start.1
  3.0 0.0 copy-start.2
  3.0 6.1 %all-to-all-start = ((bf16[32,16,128]{2,1,0:T(8,128)(2,1)}), bf16[32,16,128]{2,1,0:T(8,128)(2,1)S(1)}, u32[]{:S(2)}, u32[]{:S(2)}) async-start(bf16[32,16,128]{2,1,0:T(8,128)(2,1)} %get-tuple-element.13), calls=%async_computation | async-start | bytes 262144 | tf_op jit(solution)/shard_map/all_to_all | solution.py:480
  9.2 1.5 %collective-permute-start = (f32[3,4,2560]{2,1,0:T(4,128)S(1)}, f32[3,4,2560]{2,1,0:T(4,128)S(1)}, u32[]{:S(2)}, u32[]{:S(2)}) collective-permute-start(f32[3,4,2560]{2,1,0:T(4,128)S(1)} %get-tuple-element.15), channel_id=1, source_target_pairs={{0,4},{8,12},{16,20},{24,28},{4,0},{12,8},{20,16},{28,24},{1,5},{9... | collective-permute-start | bytes 368648 | tf_op jit(solution)/shard_map/ppermute | solution.py:478
  10.7 0.7 %collective-permute-start.1 = (f32[3,4,2560]{2,1,0:T(4,128)S(1)}, f32[3,4,2560]{2,1,0:T(4,128)S(1)}, u32[]{:S(2)}, u32[]{:S(2)}) collective-permute-start(f32[3,4,2560]{2,1,0:T(4,128)S(1)} %get-tuple-element.16), channel_id=1, source_target_pairs={{4,8},{12,16},{20,24},{8,4},{16,12},{24,20},{5,9},{13,17},{21,25},... | collective-permute-start | bytes 368648 | tf_op jit(solution)/shard_map/ppermute | solution.py:479
  11.4 5.8 %collective-permute-done.first_ref = f32[3,4,2560]{2,1,0:T(4,128)S(1)} collective-permute-done((f32[3,4,2560]{2,1,0:T(4,128)S(1)}, f32[3,4,2560]{2,1,0:T(4,128)S(1)}, u32[]{:S(2)}, u32[]{:S(2)}) %collective-permute-start) | collective-permute-done | bytes 122912 | tf_op jit(solution)/shard_map/ppermute | solution.py:478
  17.2 0.0 collective-permute-done.1.second_ref
  17.2 0.1 edges.1
  17.3 0.1 collective-permute-start.2
  17.4 2.7 %collective-permute-start.3 = (f32[8,2560]{1,0:T(8,128)S(1)}, f32[8,2560]{1,0:T(8,128)S(1)}, u32[]{:S(2)}, u32[]{:S(2)}) collective-permute-start(f32[8,2560]{1,0:T(8,128)S(1)} %get-tuple-element.18), channel_id=1, source_target_pairs={{1,2},{2,1},{5,6},{6,5},{9,10},{10,9},{13,14},{14,13},{17,18},{18,... | collective-permute-start | bytes 245768 | tf_op jit(solution)/shard_map/ppermute | solution.py:510
  20.1 0.0 copy-done.3
  20.1 0.1 reshape.10
  20.2 0.1 reshape.12.wave_ref
  20.3 1.3 %table.1.table_ref = bf16[256,2560]{1,0:T(8,128)(2,1)S(1)} custom-call(s32[128,1]{1,0:T(8,128)S(1)} %reshape.12.wave_ref), custom_call_target="tpu_custom_call" | custom-call | tf_op jit(solution)/shard_map/table/pallas_call | solution.py:491
  21.5 0.0 collective-permute-done.2.lev_first_ref
  21.5 1.6 %collective-permute-done.3.lev_second_ref = f32[8,2560]{1,0:T(8,128)S(1)} collective-permute-done((f32[8,2560]{1,0:T(8,128)S(1)}, f32[8,2560]{1,0:T(8,128)S(1)}, u32[]{:S(2)}, u32[]{:S(2)}) %collective-permute-start.3) | collective-permute-done | bytes 81952 | tf_op jit(solution)/shard_map/ppermute | solution.py:510
  23.2 0.0 all-to-all-done
  23.2 0.0 copy-done
  23.2 0.0 copy-done.1
  23.2 0.0 copy-done.2
  23.2 1.8 %grid.1 = f32[8,2,128]{2,1,0:T(2,128)S(1)} custom-call(bf16[8,4,16,128]{3,2,1,0:T(8,128)(2,1)S(1)} %bitcast.1, bf16[256,384]{1,0:T(8,128)(2,1)S(1)} %copy-done, bf16[256,2560]{1,0:T(8,128)(2,1)S(1)} %table.1.table_ref, f32[4,4,2560]{2,1,0:T(4,128)S(1)} %get-tuple-element.14.own_ref, f32[3,4,2560]{2,1,0:T(4,128)S(1)} %collective-permute-done.first_ref, ...), custom_call_target="tpu_custom_call" | custom-call | tf_op jit(solution)/shard_map/grid/pallas_call | solution.py:511
  25.0 10.5 %all_to_all.10.arrived_ref = f32[8,2,128]{2,1,0:T(2,128)S(1)} all-to-all(f32[8,2,128]{2,1,0:T(2,128)S(1)} %grid.1), channel_id=1, replica_groups={{20,16,12,8,4,0,28,24},{21,17,13,9,5,1,29,25},{22,18,14,10,6,2,30,26},{..., dimensions={0} | all-to-all | bytes 16384 | tf_op jit(solution)/shard_map/all_to_all | solution.py:534
  35.5 1.1 %analysis.1 = f32[13,2,4,1280]{3,2,1,0:T(4,128)} custom-call(f32[8,2,128]{2,1,0:T(2,128)S(1)} %all_to_all.10.arrived_ref, bf16[13,16,1280]{2,1,0:T(8,128)(2,1)S(1)} %get-tuple-element.20.live_ref), custom_call_target="tpu_custom_call" | custom-call | tf_op jit(solution)/shard_map/analysis/pallas_call | solution.py:538
  (1 shorter events, 0.0 us)
Async XLA Ops:
  0.0 20.1 %copy-start.3 = (s32[104]{0:T(128)S(1)}, s32[104]{0:T(128)}, u32[]{:S(2)}) copy-start(s32[104]{0:T(128)} %wave_hbm.1) | copy-start | bytes 1252
  3.0 20.2 %copy-start = (bf16[256,384]{1,0:T(8,128)(2,1)S(1)}, bf16[256,384]{1,0:T(8,128)(2,1)}, u32[]{:S(2)}) copy-start(bf16[256,384]{1,0:T(8,128)(2,1)} %constant.8.clone.unpack_ref) | copy-start | bytes 589828
  3.0 20.2 %copy-start.1 = (bf16[32,128]{1,0:T(8,128)(2,1)S(1)}, bf16[32,128]{1,0:T(8,128)(2,1)}, u32[]{:S(2)}) copy-start(bf16[32,128]{1,0:T(8,128)(2,1)} %constant.9.clone.spread_ref) | copy-start | bytes 24580
  3.0 20.2 %copy-start.2 = (f32[8,128]{1,0:T(8,128)S(1)}, f32[8,128]{1,0:T(8,128)}, u32[]{:S(2)}) copy-start(f32[8,128]{1,0:T(8,128)} %constant.10.clone.pick_ref) | copy-start | bytes 12292
  3.0 20.1 %all-to-all-start = ((bf16[32,16,128]{2,1,0:T(8,128)(2,1)}), bf16[32,16,128]{2,1,0:T(8,128)(2,1)S(1)}, u32[]{:S(2)}, u32[]{:S(2)}) async-start(bf16[32,16,128]{2,1,0:T(8,128)(2,1)} %get-tuple-element.13), calls=%async_computation | async-start | bytes 262144 | tf_op jit(solution)/shard_map/all_to_all | solution.py:480
  9.2 8.0 %collective-permute-start = (f32[3,4,2560]{2,1,0:T(4,128)S(1)}, f32[3,4,2560]{2,1,0:T(4,128)S(1)}, u32[]{:S(2)}, u32[]{:S(2)}) collective-permute-start(f32[3,4,2560]{2,1,0:T(4,128)S(1)} %get-tuple-element.15), channel_id=1, source_target_pairs={{0,4},{8,12},{16,20},{24,28},{4,0},{12,8},{20,16},{28,24},{1,5},{9... | collective-permute-start | bytes 368648 | tf_op jit(solution)/shard_map/ppermute | solution.py:478
  10.7 6.5 %collective-permute-start.1 = (f32[3,4,2560]{2,1,0:T(4,128)S(1)}, f32[3,4,2560]{2,1,0:T(4,128)S(1)}, u32[]{:S(2)}, u32[]{:S(2)}) collective-permute-start(f32[3,4,2560]{2,1,0:T(4,128)S(1)} %get-tuple-element.16), channel_id=1, source_target_pairs={{4,8},{12,16},{20,24},{8,4},{16,12},{24,20},{5,9},{13,17},{21,25},... | collective-permute-start | bytes 368648 | tf_op jit(solution)/shard_map/ppermute | solution.py:479
  17.3 4.2 %collective-permute-start.2 = (f32[8,2560]{1,0:T(8,128)S(1)}, f32[8,2560]{1,0:T(8,128)S(1)}, u32[]{:S(2)}, u32[]{:S(2)}) collective-permute-start(f32[8,2560]{1,0:T(8,128)S(1)} %get-tuple-element.17), channel_id=1, source_target_pairs={{0,1},{2,3},{1,0},{3,2},{4,5},{6,7},{5,4},{7,6},{8,9},{10,11},{9,8... | collective-permute-start | bytes 245768 | tf_op jit(solution)/shard_map/ppermute | solution.py:509
  17.4 5.8 %collective-permute-start.3 = (f32[8,2560]{1,0:T(8,128)S(1)}, f32[8,2560]{1,0:T(8,128)S(1)}, u32[]{:S(2)}, u32[]{:S(2)}) collective-permute-start(f32[8,2560]{1,0:T(8,128)S(1)} %get-tuple-element.18), channel_id=1, source_target_pairs={{1,2},{2,1},{5,6},{6,5},{9,10},{10,9},{13,14},{14,13},{17,18},{18,... | collective-permute-start | bytes 245768 | tf_op jit(solution)/shard_map/ppermute | solution.py:510

commit v8 on v7

--- a/solution.py
+++ b/solution.py
@@ -198,7 +198,7 @@
         at = b * z.rows * z.unit
         piece = rows[:, at : at + z.piece].astype(jnp.bfloat16)
         for l in range(z.sets):
-            pieces_ref[z.bands * z.sets - 1 - (b * z.sets + l)] = piece
+            pieces_ref[b * z.sets + z.sets - 1 - l] = piece
 
     even = lax.axis_index("wave") % 2 == 0
     whole[2].wait()
@@ -301,7 +301,7 @@
     height = z.bands * z.slot_pad
 
     def from_set(index):
-        blocks = [arrived_ref[z.bands - 1 - b, z.sets - 1 - index] for b in range(z.bands)]
+        blocks = [arrived_ref[b, z.sets - 1 - index] for b in range(z.bands)]
         return jnp.concatenate(blocks, axis=0)
 
     blocks = jnp.concatenate(
@@ -482,7 +482,9 @@
         ("wave", "lev"),
         split_axis=0,
         concat_axis=0,
-        axis_index_groups=[list(range(z.bands * z.sets))[::-1]],
+        axis_index_groups=[
+            [b * z.sets + l for b in range(z.bands) for l in reversed(range(z.sets))]
+        ],
         tiled=True,
     )
     padded_wave = jnp.pad(

time: 36.9 us -> 36.9 us (level)
  no operation moved by 1% of the time
where the time goes in v8:
time: 36.9 us; the launch traced here: 36.6 us
  starting transfers between devices  11.1 us (30%)
  blocking collectives  10.5 us (28%)
  waiting for transfers between devices  7.4 us (20%)
  Pallas kernels  7.28 us (20%)
    all_to_all x1, blocking collectives, on_device(): lax.all_to_all(reply, 'wave', split_axis=0, concat_axis=0, axis_index_gro...  10.5 us
    all_to_all x1, starting transfers between devices, on_device(): lax.all_to_all(pieces, ('wave', 'lev'), split_axis=0, concat_axis=0, axis...  6.13 us
    ppermute x1, waiting for transfers between devices, on_device(): wave_first = lax.ppermute(to_first, 'wave', first_pairs)  5.8 us
    pallas_call x1, Pallas kernels, on_device(): pl.pallas_call(functools.partial(legendre_kernel, z), name='legendre', in...  2.98 us
    ppermute x1, starting transfers between devices, on_device(): lev_second = lax.ppermute(down, 'lev', second_pairs)  2.69 us
    pallas_call x1, Pallas kernels, on_device(): pl.pallas_call(functools.partial(grid_kernel, z), name='grid', in_specs=v...  1.82 us
    ppermute x1, waiting for transfers between devices, on_device(): lev_second = lax.ppermute(down, 'lev', second_pairs)  1.59 us
    ppermute x1, starting transfers between devices, on_device(): wave_first = lax.ppermute(to_first, 'wave', first_pairs)  1.53 us
  transfers between devices with their start and end apart: 5, of which 2 were waited for; matrix products, arithmetic and copies ran while one was open for 0% of the time, Pallas kernels for 4%

profile of v8, /device:TPU:2, one launch (start us, length us, event | category | flops | bytes accessed | tf_op | source)
XLA Modules:
  0.0 36.6 jit_solution(6168977248400151854)
XLA Ops:
  0.0 0.0 copy-start.3
  0.0 3.0 %legendre.1 = (bf16[32,16,128]{2,1,0:T(8,128)(2,1)}, bf16[13,16,1280]{2,1,0:T(8,128)(2,1)S(1)}, f32[16,128]{1,0:T(8,128)S(1)}, f32[4,4,2560]{2,1,0:T(4,128)S(1)}...) custom-call(s32[104]{0:T(128)} %wave_hbm.1, f32[2]{0:T(128)} %weight_hbm.1, bf16[13,4,4,1280]{3,2,1,0:T(4,128)(2,1)} %spectra_hbm.1, ...), custom_call_target="tpu_custom_call" | custom-call | tf_op jit(solution)/shard_map/legendre/pallas_call | solution.py:454
  3.0 0.0 copy-start
  3.0 0.0 copy-start.1
  3.0 0.0 copy-start.2
  3.0 6.1 %all-to-all-start = ((bf16[32,16,128]{2,1,0:T(8,128)(2,1)}), bf16[32,16,128]{2,1,0:T(8,128)(2,1)S(1)}, u32[]{:S(2)}, u32[]{:S(2)}) async-start(bf16[32,16,128]{2,1,0:T(8,128)(2,1)} %get-tuple-element.13), calls=%async_computation | async-start | bytes 262144 | tf_op jit(solution)/shard_map/all_to_all | solution.py:480
  9.2 1.5 %collective-permute-start = (f32[3,4,2560]{2,1,0:T(4,128)S(1)}, f32[3,4,2560]{2,1,0:T(4,128)S(1)}, u32[]{:S(2)}, u32[]{:S(2)}) collective-permute-start(f32[3,4,2560]{2,1,0:T(4,128)S(1)} %get-tuple-element.15), channel_id=1, source_target_pairs={{0,4},{8,12},{16,20},{24,28},{4,0},{12,8},{20,16},{28,24},{1,5},{9... | collective-permute-start | bytes 368648 | tf_op jit(solution)/shard_map/ppermute | solution.py:478
  10.7 0.7 %collective-permute-start.1 = (f32[3,4,2560]{2,1,0:T(4,128)S(1)}, f32[3,4,2560]{2,1,0:T(4,128)S(1)}, u32[]{:S(2)}, u32[]{:S(2)}) collective-permute-start(f32[3,4,2560]{2,1,0:T(4,128)S(1)} %get-tuple-element.16), channel_id=1, source_target_pairs={{4,8},{12,16},{20,24},{8,4},{16,12},{24,20},{5,9},{13,17},{21,25},... | collective-permute-start | bytes 368648 | tf_op jit(solution)/shard_map/ppermute | solution.py:479
  11.4 5.8 %collective-permute-done.first_ref = f32[3,4,2560]{2,1,0:T(4,128)S(1)} collective-permute-done((f32[3,4,2560]{2,1,0:T(4,128)S(1)}, f32[3,4,2560]{2,1,0:T(4,128)S(1)}, u32[]{:S(2)}, u32[]{:S(2)}) %collective-permute-start) | collective-permute-done | bytes 122912 | tf_op jit(solution)/shard_map/ppermute | solution.py:478
  17.2 0.0 collective-permute-done.1.second_ref
  17.2 0.1 edges.1
  17.3 0.1 collective-permute-start.2
  17.4 2.7 %collective-permute-start.3 = (f32[8,2560]{1,0:T(8,128)S(1)}, f32[8,2560]{1,0:T(8,128)S(1)}, u32[]{:S(2)}, u32[]{:S(2)}) collective-permute-start(f32[8,2560]{1,0:T(8,128)S(1)} %get-tuple-element.18), channel_id=1, source_target_pairs={{1,2},{2,1},{5,6},{6,5},{9,10},{10,9},{13,14},{14,13},{17,18},{18,... | collective-permute-start | bytes 245768 | tf_op jit(solution)/shard_map/ppermute | solution.py:512
  20.1 0.0 copy-done.3
  20.1 0.1 reshape.10
  20.2 0.1 reshape.12.wave_ref
  20.3 1.3 %table.1.table_ref = bf16[256,2560]{1,0:T(8,128)(2,1)S(1)} custom-call(s32[128,1]{1,0:T(8,128)S(1)} %reshape.12.wave_ref), custom_call_target="tpu_custom_call" | custom-call | tf_op jit(solution)/shard_map/table/pallas_call | solution.py:493
  21.5 0.0 collective-permute-done.2.lev_first_ref
  21.5 1.6 %collective-permute-done.3.lev_second_ref = f32[8,2560]{1,0:T(8,128)S(1)} collective-permute-done((f32[8,2560]{1,0:T(8,128)S(1)}, f32[8,2560]{1,0:T(8,128)S(1)}, u32[]{:S(2)}, u32[]{:S(2)}) %collective-permute-start.3) | collective-permute-done | bytes 81952 | tf_op jit(solution)/shard_map/ppermute | solution.py:512
  23.1 0.0 all-to-all-done
  23.1 0.0 copy-done
  23.1 0.0 copy-done.1
  23.1 0.0 copy-done.2
  23.1 1.8 %grid.1 = f32[8,2,128]{2,1,0:T(2,128)S(1)} custom-call(bf16[8,4,16,128]{3,2,1,0:T(8,128)(2,1)S(1)} %bitcast.1, bf16[256,384]{1,0:T(8,128)(2,1)S(1)} %copy-done, bf16[256,2560]{1,0:T(8,128)(2,1)S(1)} %table.1.table_ref, f32[4,4,2560]{2,1,0:T(4,128)S(1)} %get-tuple-element.14.own_ref, f32[3,4,2560]{2,1,0:T(4,128)S(1)} %collective-permute-done.first_ref, ...), custom_call_target="tpu_custom_call" | custom-call | tf_op jit(solution)/shard_map/grid/pallas_call | solution.py:513
  25.0 10.5 %all_to_all.10.arrived_ref = f32[8,2,128]{2,1,0:T(2,128)S(1)} all-to-all(f32[8,2,128]{2,1,0:T(2,128)S(1)} %grid.1), channel_id=1, replica_groups={{20,16,12,8,4,0,28,24},{21,17,13,9,5,1,29,25},{22,18,14,10,6,2,30,26},{..., dimensions={0} | all-to-all | bytes 16384 | tf_op jit(solution)/shard_map/all_to_all | solution.py:536
  35.5 1.1 %analysis.1 = f32[13,2,4,1280]{3,2,1,0:T(4,128)} custom-call(f32[8,2,128]{2,1,0:T(2,128)S(1)} %all_to_all.10.arrived_ref, bf16[13,16,1280]{2,1,0:T(8,128)(2,1)S(1)} %get-tuple-element.20.live_ref), custom_call_target="tpu_custom_call" | custom-call | tf_op jit(solution)/shard_map/analysis/pallas_call | solution.py:540
  (1 shorter events, 0.0 us)
Async XLA Ops:
  0.0 20.1 %copy-start.3 = (s32[104]{0:T(128)S(1)}, s32[104]{0:T(128)}, u32[]{:S(2)}) copy-start(s32[104]{0:T(128)} %wave_hbm.1) | copy-start | bytes 1252
  3.0 20.1 %copy-start = (bf16[256,384]{1,0:T(8,128)(2,1)S(1)}, bf16[256,384]{1,0:T(8,128)(2,1)}, u32[]{:S(2)}) copy-start(bf16[256,384]{1,0:T(8,128)(2,1)} %constant.8.clone.unpack_ref) | copy-start | bytes 589828
  3.0 20.1 %copy-start.1 = (bf16[32,128]{1,0:T(8,128)(2,1)S(1)}, bf16[32,128]{1,0:T(8,128)(2,1)}, u32[]{:S(2)}) copy-start(bf16[32,128]{1,0:T(8,128)(2,1)} %constant.9.clone.spread_ref) | copy-start | bytes 24580
  3.0 20.1 %copy-start.2 = (f32[8,128]{1,0:T(8,128)S(1)}, f32[8,128]{1,0:T(8,128)}, u32[]{:S(2)}) copy-start(f32[8,128]{1,0:T(8,128)} %constant.10.clone.pick_ref) | copy-start | bytes 12292
  3.0 20.1 %all-to-all-start = ((bf16[32,16,128]{2,1,0:T(8,128)(2,1)}), bf16[32,16,128]{2,1,0:T(8,128)(2,1)S(1)}, u32[]{:S(2)}, u32[]{:S(2)}) async-start(bf16[32,16,128]{2,1,0:T(8,128)(2,1)} %get-tuple-element.13), calls=%async_computation | async-start | bytes 262144 | tf_op jit(solution)/shard_map/all_to_all | solution.py:480
  9.2 8.0 %collective-permute-start = (f32[3,4,2560]{2,1,0:T(4,128)S(1)}, f32[3,4,2560]{2,1,0:T(4,128)S(1)}, u32[]{:S(2)}, u32[]{:S(2)}) collective-permute-start(f32[3,4,2560]{2,1,0:T(4,128)S(1)} %get-tuple-element.15), channel_id=1, source_target_pairs={{0,4},{8,12},{16,20},{24,28},{4,0},{12,8},{20,16},{28,24},{1,5},{9... | collective-permute-start | bytes 368648 | tf_op jit(solution)/shard_map/ppermute | solution.py:478
  10.7 6.5 %collective-permute-start.1 = (f32[3,4,2560]{2,1,0:T(4,128)S(1)}, f32[3,4,2560]{2,1,0:T(4,128)S(1)}, u32[]{:S(2)}, u32[]{:S(2)}) collective-permute-start(f32[3,4,2560]{2,1,0:T(4,128)S(1)} %get-tuple-element.16), channel_id=1, source_target_pairs={{4,8},{12,16},{20,24},{8,4},{16,12},{24,20},{5,9},{13,17},{21,25},... | collective-permute-start | bytes 368648 | tf_op jit(solution)/shard_map/ppermute | solution.py:479
  17.3 4.2 %collective-permute-start.2 = (f32[8,2560]{1,0:T(8,128)S(1)}, f32[8,2560]{1,0:T(8,128)S(1)}, u32[]{:S(2)}, u32[]{:S(2)}) collective-permute-start(f32[8,2560]{1,0:T(8,128)S(1)} %get-tuple-element.17), channel_id=1, source_target_pairs={{0,1},{2,3},{1,0},{3,2},{4,5},{6,7},{5,4},{7,6},{8,9},{10,11},{9,8... | collective-permute-start | bytes 245768 | tf_op jit(solution)/shard_map/ppermute | solution.py:511
  17.4 5.8 %collective-permute-start.3 = (f32[8,2560]{1,0:T(8,128)S(1)}, f32[8,2560]{1,0:T(8,128)S(1)}, u32[]{:S(2)}, u32[]{:S(2)}) collective-permute-start(f32[8,2560]{1,0:T(8,128)S(1)} %get-tuple-element.18), channel_id=1, source_target_pairs={{1,2},{2,1},{5,6},{6,5},{9,10},{10,9},{13,14},{14,13},{17,18},{18,... | collective-permute-start | bytes 245768 | tf_op jit(solution)/shard_map/ppermute | solution.py:512
